TPU v7x, 32 devices: a whole 2x2x4 slice. The times are simulated.
32 devices in a mesh: groups: 2 (over x), tile: 16 (over z, y, core).
Axes of the slice: x: 2, y: 2, z: 4, core: 2. Of those that a mesh axis runs over, the one named last changes fastest.
Arguments:
- tracer_state: float32 [2, 50, 4096], P(None, None, ('groups', 'tile')), parts along dimension 2, may hold values from -6 to 6
- krylov_direction: float32 [2, 50, 4096], P(None, None, ('groups', 'tile')), parts along dimension 2, may hold values from -6 to 6
- explicit_tiles: bfloat16 [800, 6, 128, 128], P('tile')
- implicit_tiles: bfloat16 [800, 3, 128, 128], P('tile')
- explicit_columns: int32 [800, 6], P('tile'), may hold values from 0 to 450, as said below
- ghost_levels: int32 [256, 25], P('tile'), may hold values from 0 to 50, as said below
- wet_levels: int32 [2048], P('tile'), may hold values from 0 to 50
- surface_light: float32 [4096], P(('groups', 'tile')), parts along dimension 0, may hold values from 0.25 to 4
- martin_exponent: float32 [4096], P(('groups', 'tile')), parts along dimension 0, may hold values from 0.5 to 2
- column_slots: int32 [256, 12], P('tile'), may hold values from 0 to 128, as said below
Outputs:
- state_out: float32 [2, 50, 4096], P(None, None, ('groups', 'tile')), parts along dimension 2
- tangent_out: float32 [2, 50, 4096], P(None, None, ('groups', 'tile')), parts along dimension 2
- export_flux: float32 [6144], P(('groups', 'tile')), parts along dimension 0
There are 2 independent parts, one for each index of `groups`. A program takes and returns all parts, laid end to end along the dimension named above; an argument that names none is the same for every part. Nothing has to cross between parts.
Inputs may be any that keep to these rules, and one draw needn't show every extreme that they name: `explicit_columns`: row d * 50 + l holds l, then l - 1 and l + 1 (50 beyond the ends), then one position for each of the devices d - 1, d + 1 and d + D / 2 of the D devices (wrapping), in that order: 51 + s * 25 + l when ghost_levels sends level l from that device s to d, else 50. `ghost_levels`: row s * D + d, slot k, holds k or 50. It holds k exactly for k below a depth of 1 to 25 when s is d - 1, d + 1 or d + D / 2 (wrapping), and 50 for all other pairs; some device gets depth 25 from all three. `column_slots`: row s * D + b lists local columns of device s handed to device b, 128 marking an empty slot. Each column of s with wet_levels above 0 stands exactly once in rows s * D to s * D + D - 1, no dry column does, and some row is full.
All inputs are finite; a program needn't handle non-finite values.
Results may differ from a plain program's by a relative error of at most 0.012.
Values may be sent and summed in bfloat16 or wider, within the bound.
No kernel may reach another device: no remote copies, remote signals or barrier semaphores. Data moves between devices by JAX's collectives and lax.ppermute only.
A program may use at most 64 MiB of HBM per device.

v0:
```python
import jax
import jax.numpy as jnp
from jax import lax
from jax.sharding import PartitionSpec as P

EUPHOTIC = 6
STEPS = 3


max_uptake = 1.0
half_saturation = 0.5
dop_fraction = 0.67
dop_decay = 0.2
time_step = 0.5


def shifted(value, axis, steps):
    count = lax.axis_size(axis)
    pairs = [(source, (source + steps) % count) for source in range(count)]
    return lax.ppermute(value, axis, pairs)


def sources(phosphate, organic, depth_count, surface_light, martin_exponent):
    levels = jnp.arange(phosphate.shape[0], dtype=jnp.float32)[:, None]
    wet_mask = (levels < depth_count[None, :]).astype(jnp.float32)
    sunlit = (levels < EUPHOTIC).astype(jnp.float32)
    depth_ratio = (levels + 1.0) ** 1.5 / (EUPHOTIC * 1.0) ** 1.5
    reaching = jnp.where(
        levels >= EUPHOTIC - 1, jnp.exp(-martin_exponent[None, :] * jnp.log(depth_ratio)), 1.0
    )
    passing = reaching * (levels < depth_count[None, :] - 1.0).astype(jnp.float32)
    passing_above = jnp.concatenate([jnp.ones_like(passing[:1]), passing[:-1]], 0)
    squared = phosphate * phosphate
    uptake = (
        max_uptake
        * surface_light[None, :]
        * jnp.exp(-2.0 * levels / EUPHOTIC)
        * sunlit
        * wet_mask
        * squared
        / (half_saturation**2 + squared)
    )
    export = (1.0 - dop_fraction) * jnp.sum(uptake, 0)
    remineral = export[None, :] * (passing_above - passing)
    decayed = dop_decay * organic * wet_mask
    return (-uptake + decayed + remineral, dop_fraction * uptake - decayed, export)


def column_sources(columns, params):

    def column_rates(phosphate, organic):
        return sources(phosphate, organic, params[0], params[1], params[2])

    primal, tangent = jax.jvp(
        column_rates, (columns[:, 0], columns[:, 1]), (columns[:, 2], columns[:, 3])
    )
    return (jnp.stack([primal[0], primal[1], tangent[0], tangent[1]], 1), primal[2])


def fetch_ghosts(outgoing):
    tile_count = lax.axis_size("tile")
    my_index = lax.axis_index("tile")
    arrived = jnp.zeros_like(outgoing)
    for offset in (1, -1, tile_count // 2):
        sending = lax.dynamic_slice_in_dim(outgoing, (my_index + offset) % tile_count, 1, 0)
        incoming = shifted(sending, "tile", offset)
        arrived = lax.dynamic_update_slice_in_dim(
            arrived, incoming, (my_index - offset) % tile_count, 0
        )
    return arrived


def on_device(
    tracer_state,
    krylov_direction,
    explicit_tiles,
    implicit_tiles,
    explicit_columns,
    ghost_levels,
    wet_levels,
    surface_light,
    martin_exponent,
    column_slots,
):
    levels = tracer_state.shape[1]
    column_count = tracer_state.shape[2]
    half_channels = tracer_state.shape[0]
    channels = 2 * half_channels
    depth_count = wet_levels.astype(jnp.float32)
    params = jnp.stack([depth_count, surface_light, martin_exponent])
    wet_mask = (jnp.arange(levels, dtype=jnp.float32)[:, None] < depth_count[None, :]).astype(
        jnp.float32
    )
    fields = jnp.concatenate([tracer_state, krylov_direction], 0).transpose(1, 0, 2)
    export_total = jnp.zeros((column_count,), jnp.float32)
    boundary = jnp.zeros((1, channels, column_count), jnp.bfloat16)
    for time_index in range(STEPS):
        source_rates, export = column_sources(fields, params)
        export_total = export_total + export
        rounded = jnp.concatenate([fields.astype(jnp.bfloat16), boundary], 0)
        ghosts = fetch_ghosts(rounded[ghost_levels])
        tile_pool = jnp.concatenate([rounded, ghosts.reshape(-1, channels, column_count)], 0)
        carried = jnp.einsum(
            "lkcj,lkji->lci",
            tile_pool[explicit_columns],
            explicit_tiles,
            preferred_element_type=jnp.float32,
        )
        intermediate = (carried + time_step * source_rates).astype(jnp.bfloat16)
        padded_field = jnp.concatenate([boundary, intermediate, boundary], 0)
        stacked = jnp.stack([padded_field[:-2], padded_field[1:-1], padded_field[2:]], 1)
        settled = jnp.einsum(
            "lkcj,lkji->lci", stacked, implicit_tiles, preferred_element_type=jnp.float32
        )
        fields = wet_mask[:, None, :] * settled
    slot_values = jnp.concatenate([export_total, jnp.zeros((1,), jnp.float32)])[column_slots]
    export_flux = lax.all_to_all(
        slot_values, "tile", split_axis=0, concat_axis=0, tiled=True
    ).reshape(-1)
    result = fields.transpose(1, 0, 2)
    return (result[:half_channels], result[half_channels:], export_flux)


def solution(mesh):
    return jax.shard_map(
        on_device,
        mesh=mesh,
        in_specs=(
            P(None, None, ("groups", "tile")),
            P(None, None, ("groups", "tile")),
            P("tile", None, None, None),
            P("tile", None, None, None),
            P("tile", None),
            P("tile", None),
            P("tile"),
            P(("groups", "tile")),
            P(("groups", "tile")),
            P("tile", None),
        ),
        out_specs=(
            P(None, None, ("groups", "tile")),
            P(None, None, ("groups", "tile")),
            P(("groups", "tile")),
        ),
        check_vma=False,
    )
```

profile of v0, /device:TPU:0, one launch (start us, length us, event | category | flops | bytes accessed | tf_op | source)
XLA Modules:
  0.0 86.5 jit_solution(18425667601931482971)
XLA Ops:
  0.7 0.8 copy.92
  1.5 0.8 copy.93
  2.3 0.7 compare_select_fusion.1
  3.2 2.1 %gather_fusion = bf16[400,4,128]{2,1,0:T(4,128)(2,1)S(1)} fusion(bf16[51,4,128]{2,1,0:T(4,128)(2,1)S(1)} %concatenate.54.clone, s32[1024]{0:T(1024)S(1)} %pad_clamp_fusion.2), kind=kCustom, calls=%fused_computation | custom fusion | bytes 820800 | tf_op jit(solution)/shard_map/gather | solution.py:101
  5.4 0.5 collective-permute-start
  5.9 5.0 %collective-permute-start.1 = (bf16[1,25,4,128]{3,2,1,0:T(4,128)(2,1)S(1)}, bf16[1,25,4,128]{3,2,1,0:T(4,128)(2,1)S(1)}, u32[]{:S(2)}, u32[]{:S(2)}) collective-permute-start(bf16[1,25,4,128]{3,2,1,0:T(4,128)(2,1)S(1)} %get-tuple-element.33), channel_id=1, source_target_pairs={{0,15},{1,0},{2,1},{3,2},{4,3},{5,4},{6,5},{7,6},{8,7},{9,8},{10,9... | collective-permute-start | bytes 76808 | tf_op jit(solution)/shard_map/ppermute | solution.py:20
  10.9 1.2 %collective-permute-start.2 = (bf16[1,25,4,128]{3,2,1,0:T(4,128)(2,1)S(1)}, bf16[1,25,4,128]{3,2,1,0:T(4,128)(2,1)S(1)}, u32[]{:S(2)}, u32[]{:S(2)}) collective-permute-start(bf16[1,25,4,128]{3,2,1,0:T(4,128)(2,1)S(1)} %get-tuple-element.32), channel_id=1, source_target_pairs={{0,8},{1,9},{2,10},{3,11},{4,12},{5,13},{6,14},{7,15},{8,0},{9,1},... | collective-permute-start | bytes 76808 | tf_op jit(solution)/shard_map/ppermute | solution.py:20
  12.2 0.7 convert_element_type.46
  12.8 0.7 broadcast_add_fusion
  13.5 0.8 fusion.85
  14.3 0.8 select_subtract_fusion.3
  15.1 0.7 neg.43
  15.7 0.7 compare_select_fusion.2
  16.4 0.1 copy.96
  16.5 0.1 reshape.339
  16.7 0.7 compare_select_fusion
  17.6 0.8 fusion.63
  18.5 0.1 broadcast.361.clone
  18.7 2.6 %pad_maximum_fusion = bf16[451,4,128]{2,1,0:T(4,128)(2,1)S(1)} fusion(bf16[400,4,128]{2,1,0:T(4,128)(2,1)S(1)} %bitcast.225, bf16[50,4,128]{2,1,0:T(4,128)(2,1)S(1)} %copy.95, bf16[451]{0:T(512)(128)(2,1)S(1)} %pad.40.clone), kind=kLoop, calls=%fused_computation.21 | loop fusion | flops 461824 | bytes 923526 | tf_op jit(solution)/shard_map/concatenate | solution.py:102
  21.3 2.2 %gather_fusion.1 = bf16[300,4,128]{2,1,0:T(4,128)(2,1)S(1)} fusion(bf16[451,4,128]{2,1,0:T(4,128)(2,1)S(1)} %pad_maximum_fusion, s32[1024]{0:T(1024)S(1)} %pad_clamp_fusion.1), kind=kCustom, calls=%fused_computation.1 | custom fusion | bytes 615600 | tf_op jit(solution)/shard_map/gather | solution.py:105
  23.6 5.4 %fusion.12 = bf16[50,4,128]{2,1,0:T(4,128)(2,1)S(1)} fusion(bf16[50,6,4,128]{3,2,1,0:T(4,128)(2,1)S(1)} %bitcast.222, bf16[50,6,128,128]{3,2,1,0:T(8,128)(2,1)} %param.12, f32[50,4,128]{2,0,1:T(8,128)S(1)} %pad_maximum_fusion.4), kind=kOutput, calls=%fused_computation.19 | convolution fusion | flops 39398400 | bytes 10291200 | tf_op jit(solution)/shard_map/lkcj,lkji->lci/dot_general | solution.py:103
  29.1 1.0 %fusion.4 = f32[50,4,128]{2,1,0:T(4,128)S(1)} fusion(bf16[50,3,128,128]{3,2,1,0:T(8,128)(2,1)S(1)} %bitcast.216, bf16[50,1,4,128]{3,2,0,1:T(4,128)(2,1)S(1)} %get-tuple-element.58, bf16[50,1,4,128]{3,2,0,1:T(4,128)(2,1)S(1)} %bitcast.234, bf16[50,1,4,128]{3,2,0,1:T(4,128)(2,1)S(1)} %get-tuple-element.57), kind=kOutput, calls=%fused_computation.11 | convolution fusion | flops 20121600 | bytes 5171200 | tf_op jit(solution)/shard_map/lkcj,lkji->lci/dot_general | solution.py:112
  30.1 2.1 %gather_fusion.2 = bf16[400,4,128]{2,1,0:T(4,128)(2,1)S(1)} fusion(bf16[51,4,128]{2,1,0:T(4,128)(2,1)S(1)} %concatenate.59.clone, s32[1024]{0:T(1024)S(1)} %pad_clamp_fusion.2), kind=kCustom, calls=%fused_computation.2 | custom fusion | bytes 820800 | tf_op jit(solution)/shard_map/gather | solution.py:101
  32.7 4.7 %collective-permute-start.4 = (bf16[1,25,4,128]{3,2,1,0:T(4,128)(2,1)S(1)}, bf16[1,25,4,128]{3,2,1,0:T(4,128)(2,1)S(1)}, u32[]{:S(2)}, u32[]{:S(2)}) collective-permute-start(bf16[1,25,4,128]{3,2,1,0:T(4,128)(2,1)S(1)} %get-tuple-element.30), channel_id=1, source_target_pairs={{0,15},{1,0},{2,1},{3,2},{4,3},{5,4},{6,5},{7,6},{8,7},{9,8},{10,9... | collective-permute-start | bytes 76808 | tf_op jit(solution)/shard_map/ppermute | solution.py:20
  37.4 0.9 %collective-permute-done.3 = bf16[1,25,4,128]{3,2,1,0:T(4,128)(2,1)S(1)} collective-permute-done((bf16[1,25,4,128]{3,2,1,0:T(4,128)(2,1)S(1)}, bf16[1,25,4,128]{3,2,1,0:T(4,128)(2,1)S(1)}, u32[]{:S(2)}, u32[]{:S(2)}) %collective-permute-start.3) | collective-permute-done | bytes 25632 | tf_op jit(solution)/shard_map/ppermute | solution.py:20
  38.5 0.4 collective-permute-done.4
  38.9 3.2 %collective-permute-done.5 = bf16[1,25,4,128]{3,2,1,0:T(4,128)(2,1)S(1)} collective-permute-done((bf16[1,25,4,128]{3,2,1,0:T(4,128)(2,1)S(1)}, bf16[1,25,4,128]{3,2,1,0:T(4,128)(2,1)S(1)}, u32[]{:S(2)}, u32[]{:S(2)}) %collective-permute-start.5) | collective-permute-done | bytes 25632 | tf_op jit(solution)/shard_map/ppermute | solution.py:20
  42.1 2.6 %pad_maximum_fusion.1 = bf16[451,4,128]{2,1,0:T(4,128)(2,1)S(1)} fusion(bf16[400,4,128]{2,1,0:T(4,128)(2,1)S(1)} %bitcast.226, bf16[50,4,128]{2,1,0:T(4,128)(2,1)S(1)} %copy.106, bf16[451]{0:T(512)(128)(2,1)S(1)} %pad.40.clone), kind=kLoop, calls=%fused_computation.22 | loop fusion | flops 461824 | bytes 923526 | tf_op jit(solution)/shard_map/concatenate | solution.py:102
  44.8 2.2 %gather_fusion.3 = bf16[300,4,128]{2,1,0:T(4,128)(2,1)S(1)} fusion(bf16[451,4,128]{2,1,0:T(4,128)(2,1)S(1)} %pad_maximum_fusion.1, s32[1024]{0:T(1024)S(1)} %pad_clamp_fusion.1), kind=kCustom, calls=%fused_computation.3 | custom fusion | bytes 615600 | tf_op jit(solution)/shard_map/gather | solution.py:105
  47.0 5.5 %convolution_bitcast_fusion.2 = f32[50,4,128]{2,1,0:T(4,128)S(1)} fusion(bf16[50,6,4,128]{3,2,1,0:T(4,128)(2,1)S(1)} %bitcast.221, bf16[50,6,128,128]{3,2,1,0:T(8,128)(2,1)} %param.12), kind=kOutput, calls=%fused_computation.16 | convolution fusion | flops 39321600 | bytes 10240000 | tf_op jit(solution)/shard_map/lkcj,lkji->lci/dot_general | solution.py:103
  52.6 1.0 %convolution_bitcast_fusion.1 = f32[50,4,128]{2,1,0:T(4,128)S(1)} fusion(bf16[50,3,128,128]{3,2,1,0:T(8,128)(2,1)S(1)} %bitcast.218, bf16[50,3,4,128]{3,0,2,1:T(8,128)(2,1)S(1)} %pad_maximum_fusion.3), kind=kOutput, calls=%fused_computation.15 | convolution fusion | flops 19660800 | bytes 5171200 | tf_op jit(solution)/shard_map/lkcj,lkji->lci/dot_general | solution.py:112
  53.7 0.1 fusion.72
  54.1 2.1 %gather_fusion.4 = bf16[400,4,128]{2,1,0:T(4,128)(2,1)S(1)} fusion(bf16[51,4,128]{2,1,0:T(4,128)(2,1)S(1)} %concatenate.63.clone, s32[1024]{0:T(1024)S(1)} %pad_clamp_fusion.2), kind=kCustom, calls=%fused_computation.4 | custom fusion | bytes 820800 | tf_op jit(solution)/shard_map/gather | solution.py:101
  56.3 1.6 %gather_fusion.6 = f32[192]{0:T(256)S(1)} fusion(f32[129]{0:T(256)S(1)} %pad_maximum_fusion.5, s32[1024]{0:T(1024)S(1)} %pad_clamp_fusion), kind=kCustom, calls=%fused_computation.6 | custom fusion | bytes 2304 | tf_op jit(solution)/shard_map/gather | solution.py:116
  57.9 0.7 all_to_all.6
  58.6 5.8 %all-to-all-start = ((f32[16,1,12]{2,1,0:T(1,128)}), f32[16,1,12]{2,1,0:T(1,128)S(1)}, u32[]{:S(2)}, u32[]{:S(2)}) async-start(f32[16,1,12]{2,1,0:T(1,128)} %bitcast.46), calls=%async_computation | async-start | bytes 16384 | tf_op jit(solution)/shard_map/all_to_all | solution.py:117
  64.6 4.4 %collective-permute-start.7 = (bf16[1,25,4,128]{3,2,1,0:T(4,128)(2,1)S(1)}, bf16[1,25,4,128]{3,2,1,0:T(4,128)(2,1)S(1)}, u32[]{:S(2)}, u32[]{:S(2)}) collective-permute-start(bf16[1,25,4,128]{3,2,1,0:T(4,128)(2,1)S(1)} %get-tuple-element.27), channel_id=1, source_target_pairs={{0,15},{1,0},{2,1},{3,2},{4,3},{5,4},{6,5},{7,6},{8,7},{9,8},{10,9... | collective-permute-start | bytes 76808 | tf_op jit(solution)/shard_map/ppermute | solution.py:20
  69.0 1.8 %all-to-all-done = f32[16,1,12]{2,1,0:T(1,128)S(1)} async-done(((f32[16,1,12]{2,1,0:T(1,128)}), f32[16,1,12]{2,1,0:T(1,128)S(1)}, u32[]{:S(2)}, u32[]{:S(2)}) %all-to-all-start) | async-done | bytes 800 | tf_op jit(solution)/shard_map/all_to_all | solution.py:117
  70.8 0.5 broadcast.510
  71.3 0.7 reduce.3
  72.0 0.7 reshape.328
  72.8 0.9 %collective-permute-done.8 = bf16[1,25,4,128]{3,2,1,0:T(4,128)(2,1)S(1)} collective-permute-done((bf16[1,25,4,128]{3,2,1,0:T(4,128)(2,1)S(1)}, bf16[1,25,4,128]{3,2,1,0:T(4,128)(2,1)S(1)}, u32[]{:S(2)}, u32[]{:S(2)}) %collective-permute-start.8) | collective-permute-done | bytes 25632 | tf_op jit(solution)/shard_map/ppermute | solution.py:20
  73.8 2.6 %pad_maximum_fusion.2 = bf16[451,4,128]{2,1,0:T(4,128)(2,1)S(1)} fusion(bf16[400,4,128]{2,1,0:T(4,128)(2,1)S(1)} %bitcast.224, bf16[50,4,128]{2,1,0:T(4,128)(2,1)S(1)} %copy.116, bf16[451]{0:T(512)(128)(2,1)S(1)} %pad.40.clone), kind=kLoop, calls=%fused_computation.23 | loop fusion | flops 461824 | bytes 923526 | tf_op jit(solution)/shard_map/concatenate | solution.py:102
  76.4 2.2 %gather_fusion.5 = bf16[300,4,128]{2,1,0:T(4,128)(2,1)S(1)} fusion(bf16[451,4,128]{2,1,0:T(4,128)(2,1)S(1)} %pad_maximum_fusion.2, s32[1024]{0:T(1024)S(1)} %pad_clamp_fusion.1), kind=kCustom, calls=%fused_computation.5 | custom fusion | bytes 615600 | tf_op jit(solution)/shard_map/gather | solution.py:105
  78.7 5.5 %fusion.13 = bf16[50,4,128]{2,1,0:T(4,128)(2,1)S(1)} fusion(bf16[50,6,4,128]{3,2,1,0:T(4,128)(2,1)S(1)} %bitcast.223, bf16[50,6,128,128]{3,2,1,0:T(8,128)(2,1)} %param.12, f32[50,1,128]{2,1,0:T(1,128)S(1)} %get-tuple-element.16, f32[50,1,128]{2,1,0:T(1,128)S(1)} %copy.130, f32[50,1,128]{2,1,0:T(1,128)S(1)} %get-tuple-element.12, f32[50,1,128]{2,1,0:T(1,128)S(1)} %copy.129), kind=kOutput, calls=%fused_computation.20 | convolution fusion | flops 39475200 | bytes 10291200 | tf_op jit(solution)/shard_map/lkcj,lkji->lci/dot_general | solution.py:103
  84.2 1.0 %fusion.7 = f32[50,4,128]{2,1,0:T(4,128)S(1)} fusion(bf16[50,3,128,128]{3,2,1,0:T(8,128)(2,1)S(1)} %bitcast.220, bf16[50,1,4,128]{3,2,0,1:T(4,128)(2,1)S(1)} %get-tuple-element.56, bf16[50,1,4,128]{3,2,0,1:T(4,128)(2,1)S(1)} %bitcast.233, bf16[50,1,4,128]{3,2,0,1:T(4,128)(2,1)S(1)} %get-tuple-element.55), kind=kOutput, calls=%fused_computation.12 | convolution fusion | flops 20121600 | bytes 5171200 | tf_op jit(solution)/shard_map/lkcj,lkji->lci/dot_general | solution.py:112
  85.2 0.6 copy.134
  85.9 0.6 copy.135
  (87 shorter events, 2.3 us)
Async XLA Ops:
  5.4 13.1 %collective-permute-start = (bf16[1,25,4,128]{3,2,1,0:T(4,128)(2,1)S(1)}, bf16[1,25,4,128]{3,2,1,0:T(4,128)(2,1)S(1)}, u32[]{:S(2)}, u32[]{:S(2)}) collective-permute-start(bf16[1,25,4,128]{3,2,1,0:T(4,128)(2,1)S(1)} %get-tuple-element.34), channel_id=1, source_target_pairs={{0,1},{1,2},{2,3},{3,4},{4,5},{5,6},{6,7},{7,8},{8,9},{9,10},{10,1... | collective-permute-start | bytes 76808 | tf_op jit(solution)/shard_map/ppermute | solution.py:20
  5.9 12.7 %collective-permute-start.1 = (bf16[1,25,4,128]{3,2,1,0:T(4,128)(2,1)S(1)}, bf16[1,25,4,128]{3,2,1,0:T(4,128)(2,1)S(1)}, u32[]{:S(2)}, u32[]{:S(2)}) collective-permute-start(bf16[1,25,4,128]{3,2,1,0:T(4,128)(2,1)S(1)} %get-tuple-element.33), channel_id=1, source_target_pairs={{0,15},{1,0},{2,1},{3,2},{4,3},{5,4},{6,5},{7,6},{8,7},{9,8},{10,9... | collective-permute-start | bytes 76808 | tf_op jit(solution)/shard_map/ppermute | solution.py:20
  10.9 7.7 %collective-permute-start.2 = (bf16[1,25,4,128]{3,2,1,0:T(4,128)(2,1)S(1)}, bf16[1,25,4,128]{3,2,1,0:T(4,128)(2,1)S(1)}, u32[]{:S(2)}, u32[]{:S(2)}) collective-permute-start(bf16[1,25,4,128]{3,2,1,0:T(4,128)(2,1)S(1)} %get-tuple-element.32), channel_id=1, source_target_pairs={{0,8},{1,9},{2,10},{3,11},{4,12},{5,13},{6,14},{7,15},{8,0},{9,1},... | collective-permute-start | bytes 76808 | tf_op jit(solution)/shard_map/ppermute | solution.py:20
  21.3 7.7 %slice-start = ((s8[4915200]{0:T(1024)(128)(4,1)}), s8[720896]{0:T(1024)(128)(4,1)S(1)}, s32[]{:S(2)}) async-start(s8[4915200]{0:T(1024)(128)(4,1)} %bitcast.215), calls=%async_computation.1 | async-start | bytes 1441792
  23.5 5.5 %slice-start.1 = ((s8[4915200]{0:T(1024)(128)(4,1)}), s8[4194304]{0:T(1024)(128)(4,1)S(1)}, s32[]{:S(2)}) async-start(s8[4915200]{0:T(1024)(128)(4,1)} %bitcast.215), calls=%async_computation.2 | async-start | bytes 8388608
  29.0 3.4 %copy-start = (f32[128]{0:T(128)S(1)}, f32[128]{0:T(128)}, u32[]{:S(2)}) copy-start(f32[128]{0:T(128)} %param.17) | copy-start | bytes 1540
  32.3 6.0 %collective-permute-start.3 = (bf16[1,25,4,128]{3,2,1,0:T(4,128)(2,1)S(1)}, bf16[1,25,4,128]{3,2,1,0:T(4,128)(2,1)S(1)}, u32[]{:S(2)}, u32[]{:S(2)}) collective-permute-start(bf16[1,25,4,128]{3,2,1,0:T(4,128)(2,1)S(1)} %get-tuple-element.31), channel_id=1, source_target_pairs={{0,1},{1,2},{2,3},{3,4},{4,5},{5,6},{6,7},{7,8},{8,9},{9,10},{10,1... | collective-permute-start | bytes 76808 | tf_op jit(solution)/shard_map/ppermute | solution.py:20
  32.7 6.2 %collective-permute-start.4 = (bf16[1,25,4,128]{3,2,1,0:T(4,128)(2,1)S(1)}, bf16[1,25,4,128]{3,2,1,0:T(4,128)(2,1)S(1)}, u32[]{:S(2)}, u32[]{:S(2)}) collective-permute-start(bf16[1,25,4,128]{3,2,1,0:T(4,128)(2,1)S(1)} %get-tuple-element.30), channel_id=1, source_target_pairs={{0,15},{1,0},{2,1},{3,2},{4,3},{5,4},{6,5},{7,6},{8,7},{9,8},{10,9... | collective-permute-start | bytes 76808 | tf_op jit(solution)/shard_map/ppermute | solution.py:20
  37.4 4.7 %collective-permute-start.5 = (bf16[1,25,4,128]{3,2,1,0:T(4,128)(2,1)S(1)}, bf16[1,25,4,128]{3,2,1,0:T(4,128)(2,1)S(1)}, u32[]{:S(2)}, u32[]{:S(2)}) collective-permute-start(bf16[1,25,4,128]{3,2,1,0:T(4,128)(2,1)S(1)} %get-tuple-element.29), channel_id=1, source_target_pairs={{0,8},{1,9},{2,10},{3,11},{4,12},{5,13},{6,14},{7,15},{8,0},{9,1},... | collective-permute-start | bytes 76808 | tf_op jit(solution)/shard_map/ppermute | solution.py:20
  44.8 7.8 %slice-start.2 = ((s8[4915200]{0:T(1024)(128)(4,1)}), s8[720896]{0:T(1024)(128)(4,1)S(1)}, s32[]{:S(2)}) async-start(s8[4915200]{0:T(1024)(128)(4,1)} %bitcast.217), calls=%async_computation.3 | async-start | bytes 1441792
  47.0 5.6 %slice-start.3 = ((s8[4915200]{0:T(1024)(128)(4,1)}), s8[4194304]{0:T(1024)(128)(4,1)S(1)}, s32[]{:S(2)}) async-start(s8[4915200]{0:T(1024)(128)(4,1)} %bitcast.217), calls=%async_computation.4 | async-start | bytes 8388608
  56.2 16.4 %collective-permute-start.6 = (bf16[1,25,4,128]{3,2,1,0:T(4,128)(2,1)S(1)}, bf16[1,25,4,128]{3,2,1,0:T(4,128)(2,1)S(1)}, u32[]{:S(2)}, u32[]{:S(2)}) collective-permute-start(bf16[1,25,4,128]{3,2,1,0:T(4,128)(2,1)S(1)} %get-tuple-element.28), channel_id=1, source_target_pairs={{0,1},{1,2},{2,3},{3,4},{4,5},{5,6},{6,7},{7,8},{8,9},{9,10},{10,1... | collective-permute-start | bytes 76808 | tf_op jit(solution)/shard_map/ppermute | solution.py:20
  58.6 12.2 %all-to-all-start = ((f32[16,1,12]{2,1,0:T(1,128)}), f32[16,1,12]{2,1,0:T(1,128)S(1)}, u32[]{:S(2)}, u32[]{:S(2)}) async-start(f32[16,1,12]{2,1,0:T(1,128)} %bitcast.46), calls=%async_computation | async-start | bytes 16384 | tf_op jit(solution)/shard_map/all_to_all | solution.py:117
  64.6 8.2 %collective-permute-start.7 = (bf16[1,25,4,128]{3,2,1,0:T(4,128)(2,1)S(1)}, bf16[1,25,4,128]{3,2,1,0:T(4,128)(2,1)S(1)}, u32[]{:S(2)}, u32[]{:S(2)}) collective-permute-start(bf16[1,25,4,128]{3,2,1,0:T(4,128)(2,1)S(1)} %get-tuple-element.27), channel_id=1, source_target_pairs={{0,15},{1,0},{2,1},{3,2},{4,3},{5,4},{6,5},{7,6},{8,7},{9,8},{10,9... | collective-permute-start | bytes 76808 | tf_op jit(solution)/shard_map/ppermute | solution.py:20
  69.0 4.7 %collective-permute-start.8 = (bf16[1,25,4,128]{3,2,1,0:T(4,128)(2,1)S(1)}, bf16[1,25,4,128]{3,2,1,0:T(4,128)(2,1)S(1)}, u32[]{:S(2)}, u32[]{:S(2)}) collective-permute-start(bf16[1,25,4,128]{3,2,1,0:T(4,128)(2,1)S(1)} %get-tuple-element.26), channel_id=1, source_target_pairs={{0,8},{1,9},{2,10},{3,11},{4,12},{5,13},{6,14},{7,15},{8,0},{9,1},... | collective-permute-start | bytes 76808 | tf_op jit(solution)/shard_map/ppermute | solution.py:20
  73.8 10.4 %slice-start.4 = ((s8[4915200]{0:T(1024)(128)(4,1)}), s8[720896]{0:T(1024)(128)(4,1)S(1)}, s32[]{:S(2)}) async-start(s8[4915200]{0:T(1024)(128)(4,1)} %bitcast.219), calls=%async_computation.5 | async-start | bytes 1441792
  78.6 5.6 %slice-start.5 = ((s8[4915200]{0:T(1024)(128)(4,1)}), s8[4194304]{0:T(1024)(128)(4,1)S(1)}, s32[]{:S(2)}) async-start(s8[4915200]{0:T(1024)(128)(4,1)} %bitcast.219), calls=%async_computation.6 | async-start | bytes 8388608
where the time goes:
time: 87 us; the launch traced here: 86.5 us
  starting transfers between devices  21.7 us (25%)
  local copies, waits for them, and re-layouts  20.8 us (24%)
  matrix products  19.2 us (22%)
  other arithmetic  16.1 us (19%)
  waiting for transfers between devices  7.3 us (8%)
  between operations  1.35 us (2%)
    dot_general x3, matrix products, on_device(): jnp.einsum('lkcj,lkji->lci', tile_pool[explicit_columns], explicit_tiles,...  16.4 us
    ppermute x9, starting transfers between devices, shifted(): return lax.ppermute(value, axis, pairs)  15.9 us
    concatenate x3, other arithmetic, on_device(): jnp.concatenate([rounded, ghosts.reshape(-1, channels, column_count)], 0)  7.91 us
    gather x3, local copies, waits for them, and re-layouts, on_device(): tile_pool[explicit_columns]  6.62 us
    gather x3, local copies, waits for them, and re-layouts, on_device(): ghosts = fetch_ghosts(rounded[ghost_levels])  6.33 us
    all_to_all x1, starting transfers between devices, on_device(): lax.all_to_all(slot_values, 'tile', split_axis=0, concat_axis=0, tiled=True)  5.8 us
    ppermute x9, waiting for transfers between devices, shifted(): return lax.ppermute(value, axis, pairs)  5.52 us
    unnamed x18, local copies, waits for them, and re-layouts  2.97 us
  transfers between devices with their start and end apart: 10, of which 5 were waited for; matrix products, arithmetic and copies ran while one was open for 12% of the time, Pallas kernels for 0%

commit v1 on v0

v1 whole, which is shorter than its diff:
```python
import functools

import jax
import jax.numpy as jnp
from jax import lax
from jax.experimental import pallas as pl
from jax.experimental.pallas import tpu as pltpu
from jax.sharding import PartitionSpec as P

EUPHOTIC = 6
STEPS = 3

max_uptake = 1.0
half_saturation = 0.5
dop_fraction = 0.67
dop_decay = 0.2
time_step = 0.5

F32 = jnp.float32
BF16 = jnp.bfloat16
MIB = 1 << 20

CHANNELS = 4
PAIR = 2 * CHANNELS
QUAD = 4 * CHANNELS
EDGE = PAIR


class Sizes:
    def __init__(self, levels, columns, depth):
        self.levels = levels
        self.columns = columns
        self.depth = depth
        self.pairs = levels // 2
        self.quads = (levels + 3) // 4
        self.rows = QUAD * self.quads
        self.padded = self.rows + 2 * EDGE
        self.ghost_pairs = (depth + 1) // 2
        self.low_pairs = min((depth + 2) // 2, self.pairs)
        self.ghost_quads = (self.ghost_pairs + 1) // 2
        self.low_quads = (self.low_pairs + 1) // 2
        self.send_rows = QUAD * self.ghost_quads
        self.low_rows = PAIR * self.low_pairs
        self.high_rows = PAIR * (self.pairs - self.low_pairs)


def sublane(columns):
    return lax.broadcasted_iota(jnp.int32, (PAIR, columns), 0)


def tiles_of(ref, level, columns):
    return ref[level].reshape(3 * columns, columns)


def pair_product(lhs, ref, pair, columns):
    rhs = jnp.concatenate(
        [tiles_of(ref, 2 * pair, columns), tiles_of(ref, 2 * pair + 1, columns)], axis=1
    )
    product = jnp.dot(lhs, rhs, preferred_element_type=F32)
    top = PAIR * (pair % 2)
    upper = product[top : top + PAIR, :columns]
    lower = product[top : top + PAIR, columns:]
    return jnp.where(sublane(columns) < CHANNELS, upper, lower)


def window(ref, start, offsets):
    parts = [ref[start + offset : start + offset + QUAD, :] for offset in offsets]
    return jnp.concatenate(parts, axis=1).astype(BF16)


def wet_rows(pair, wet, columns):
    return (2 * pair + sublane(columns) // CHANNELS) < wet


def uptake_of(ref, base, wet, light, columns):
    level = lax.broadcasted_iota(jnp.int32, (PAIR, columns), 0)
    phosphate = ref[pl.ds(base, PAIR, stride=CHANNELS), :]
    direction = ref[pl.ds(base + 2, PAIR, stride=CHANNELS), :]
    scale = max_uptake * light * jnp.exp(-2.0 * level.astype(F32) / EUPHOTIC)
    scale = jnp.where((level < EUPHOTIC) & (level < wet), scale, 0.0)
    squared = phosphate * phosphate
    half = half_saturation**2
    inverse = 1.0 / (half + squared)
    uptake = scale * squared * inverse
    slope = scale * half * (2.0 * phosphate * direction) * inverse * inverse
    return uptake, slope


def passing_at(level, wet, exponent):
    ratio = (level + 1).astype(F32) / EUPHOTIC
    ratio = jnp.maximum(ratio, 1.0)
    reaching = jnp.where(level >= EUPHOTIC - 1, jnp.exp(-1.5 * exponent * jnp.log(ratio)), 1.0)
    return jnp.where(level < wet - 1, reaching, 0.0)


def prepare_kernel(size, state_ref, krylov_ref, low_ref, high_ref, send_ref, fields_ref):
    fields_ref[...] = jnp.zeros_like(fields_ref)
    for channel in range(CHANNELS):
        source = state_ref if channel < 2 else krylov_ref
        fields_ref[pl.ds(channel, size.levels, stride=CHANNELS), :] = source[:, channel % 2, :]
    low_ref[...] = fields_ref[: size.low_rows, :]
    high_ref[...] = fields_ref[size.low_rows : size.low_rows + size.high_rows, :]
    send_ref[...] = fields_ref[: size.send_rows, :].astype(BF16)


def chunks_of(size):
    cuts = [size.quads * k // 3 for k in range(4)]
    return [(4 * a, min(4 * b, size.levels)) for a, b in zip(cuts, cuts[1:])]


def weight_copies(size, explicit_hbm, implicit_hbm, own_ref, ghost_ref, implicit_ref, semaphore):
    copies = []
    low = 2 * size.low_pairs

    def add(source, target):
        copies.append(pltpu.make_async_copy(source, target, semaphore.at[len(copies)]))

    for start, stop in chunks_of(size):
        part = pl.ds(start, stop - start)
        add(explicit_hbm.at[part, pl.ds(0, 3)], own_ref.at[part])
    part = pl.ds(low, size.levels - low)
    add(implicit_hbm.at[part], implicit_ref.at[part])
    part = pl.ds(0, 2 * size.ghost_pairs)
    add(explicit_hbm.at[part, pl.ds(3, 3)], ghost_ref)
    part = pl.ds(0, low)
    add(implicit_hbm.at[part], implicit_ref.at[part])
    return copies


def local_kernel(size, stage, slots, *refs):
    low_ref, high_ref, wet_ref, light_ref = refs[:4]
    copies = None
    if stage == "first":
        exponent_ref, columns_ref, explicit_hbm, implicit_hbm = refs[4:8]
        partial_ref, next_high_ref, total_ref, remineral_ref, depth_ref = refs[8:13]
        own_ref, ghost_ref, implicit_ref = refs[13:16]
        fields_ref, middle_ref, rate_ref, semaphore = refs[16:]
        copies = weight_copies(
            size, explicit_hbm, implicit_hbm, own_ref, ghost_ref, implicit_ref, semaphore
        )
        for copy in copies:
            copy.start()
    else:
        remineral_ref, total_in_ref, own_ref, implicit_ref = refs[4:8]
        if stage == "last":
            slots_ref, partial_ref, next_high_ref, payload_ref = refs[8:12]
        else:
            partial_ref, next_high_ref, total_ref = refs[8:11]
        fields_ref, middle_ref, rate_ref = refs[-3:]
    columns = size.columns
    wet = wet_ref[...]
    light = light_ref[...]
    zero_edge = jnp.zeros((EDGE, columns), F32)
    live = PAIR * size.pairs
    for ref in (fields_ref, middle_ref):
        ref[:EDGE, :] = zero_edge
        for start in range(EDGE + live, size.padded, PAIR):
            ref[start : start + PAIR, :] = zero_edge
    fields_ref[EDGE : EDGE + size.low_rows, :] = low_ref[...]
    fields_ref[EDGE + size.low_rows : EDGE + live, :] = high_ref[...]
    if stage == "first":
        exponent = exponent_ref[...]
        level = lax.broadcasted_iota(jnp.int32, (size.rows // CHANNELS, columns), 0)
        above = jnp.where(level == 0, 1.0, passing_at(level - 1, wet, exponent))
        share = time_step * (above - passing_at(level, wet, exponent))
        blank = jnp.zeros_like(share)
        for channel in range(CHANNELS):
            remineral_ref[pl.ds(channel, size.rows // CHANNELS, stride=CHANNELS), :] = (
                blank if channel % 2 else share
            )
        here = (columns_ref[...] != size.levels).astype(F32)
        depth = jnp.sum(here, axis=1, keepdims=True).astype(jnp.int32)
        depth_ref[...] = jnp.broadcast_to(depth, depth_ref.shape)
    uptake, slope = uptake_of(fields_ref, EDGE, wet, light, columns)
    export = (1.0 - dop_fraction) * jnp.sum(uptake, axis=0, keepdims=True)
    export_slope = (1.0 - dop_fraction) * jnp.sum(slope, axis=0, keepdims=True)
    total = export if stage == "first" else total_in_ref[...] + export
    if stage == "last":
        targets, _, width = payload_ref.shape
        column = lax.broadcasted_iota(jnp.int32, (targets, columns), 1)
        lane = lax.broadcasted_iota(jnp.int32, (targets, width), 1) - slots * lax.axis_index("tile")
        payload = jnp.zeros((targets, width), F32)
        for slot in range(slots):
            chosen = column == slots_ref[:, slot : slot + 1]
            value = jnp.sum(jnp.where(chosen, total, 0.0), axis=1, keepdims=True)
            payload = jnp.where(lane == slot, value, payload)
        payload_ref[:, 0, :] = payload
    else:
        total_ref[...] = total
    for channel, rate in enumerate((uptake, uptake, slope, slope)):
        factor = time_step * (dop_fraction if channel % 2 else -1.0)
        rate_ref[pl.ds(channel, PAIR, stride=CHANNELS), :] = factor * rate
    row = sublane(columns)
    sinking = jnp.where(row % CHANNELS < 2, export, export_slope)
    organic_row = row % 2 == 1

    def sources(pair):
        top = PAIR * pair
        own = fields_ref[EDGE + top : EDGE + top + PAIR, :]
        following = fields_ref[EDGE + top + 1 : EDGE + top + PAIR + 1, :]
        decayed = (time_step * dop_decay) * jnp.where(organic_row, -own, following)
        rate = jnp.where(wet_rows(pair, wet, columns), decayed, 0.0)
        rate = rate + remineral_ref[top : top + PAIR, :] * sinking
        if top < CHANNELS * PAIR:
            rate = rate + rate_ref[top : top + PAIR, :]
        return rate

    arrivals = {start // 4: place for place, (start, _) in enumerate(chunks_of(size))}
    for quad in range(size.quads):
        if copies and quad in arrivals:
            copies[arrivals[quad]].wait()
        lhs = window(fields_ref, EDGE + QUAD * quad, (0, -CHANNELS, CHANNELS))
        for pair in range(2 * quad, min(2 * quad + 2, size.pairs)):
            top = PAIR * pair
            value = pair_product(lhs, own_ref, pair, columns) + sources(pair)
            partial_ref[top : top + PAIR, :] = value
            middle_ref[EDGE + top : EDGE + top + PAIR, :] = value
    for start in range(live, size.rows, PAIR):
        partial_ref[start : start + PAIR, :] = zero_edge
    if copies:
        copies[-3].wait()
    for quad in range(size.low_pairs // 2, size.quads):
        lhs = window(middle_ref, EDGE + QUAD * quad, (-CHANNELS, 0, CHANNELS))
        for pair in range(max(2 * quad, size.low_pairs), min(2 * quad + 2, size.pairs)):
            settled = pair_product(lhs, implicit_ref, pair, columns)
            top = PAIR * (pair - size.low_pairs)
            next_high_ref[top : top + PAIR, :] = jnp.where(
                wet_rows(pair, wet, columns), settled, 0.0
            )
    if copies:
        copies[-2].wait()
        copies[-1].wait()


def ghost_kernel(size, last, *refs):
    partial_ref, pair_ref, other_ref, across_ref, depth_ref, wet_ref = refs[:6]
    if last:
        explicit_hbm, implicit_hbm, high_ref = refs[6:9]
        state_ref, tangent_ref, middle_ref, fields_ref, ghost_ref, implicit_ref, semaphore = refs[9:]
        low = pl.ds(0, 2 * size.low_pairs)
        part = pl.ds(0, 2 * size.ghost_pairs)
        copies = [
            pltpu.make_async_copy(
                explicit_hbm.at[part, pl.ds(3, 3)], ghost_ref, semaphore.at[0]
            ),
            pltpu.make_async_copy(implicit_hbm.at[low], implicit_ref, semaphore.at[1]),
        ]
        for copy in copies:
            copy.start()
    else:
        ghost_ref, implicit_ref, low_ref, send_ref, middle_ref = refs[6:]
    columns = size.columns
    wet = wet_ref[...]
    even = lax.axis_index("tile") % 2 == 0
    middle_ref[:EDGE, :] = jnp.zeros((EDGE, columns), F32)
    for top in range(PAIR * size.ghost_pairs, QUAD * size.low_quads + EDGE, PAIR):
        middle_ref[EDGE + top : EDGE + top + PAIR, :] = partial_ref[top : top + PAIR, :]
    if last:
        copies[0].wait()
    for quad in range(size.ghost_quads):
        span = slice(QUAD * quad, QUAD * quad + QUAD)
        own_chip = pair_ref[span, :].astype(F32)
        next_chip = other_ref[span, :].astype(F32)
        across = across_ref[span, :].astype(F32)
        level = lax.broadcasted_iota(jnp.int32, (QUAD, columns), 0) // CHANNELS + CHANNELS * quad
        before = jnp.where(even, next_chip, own_chip)
        after = jnp.where(even, own_chip, next_chip)
        before = jnp.where(level < depth_ref[3:4, :], before, 0.0)
        after = jnp.where(level < depth_ref[4:5, :], after, 0.0)
        across = jnp.where(level < depth_ref[5:6, :], across, 0.0)
        lhs = jnp.concatenate([before, after, across], axis=1).astype(BF16)
        for pair in range(2 * quad, min(2 * quad + 2, size.ghost_pairs)):
            top = PAIR * pair
            value = pair_product(lhs, ghost_ref, pair, columns)
            middle_ref[EDGE + top : EDGE + top + PAIR, :] = value + partial_ref[top : top + PAIR, :]
    if last:
        copies[1].wait()
    values = []
    for quad in range(size.low_quads):
        lhs = window(middle_ref, EDGE + QUAD * quad, (-CHANNELS, 0, CHANNELS))
        for pair in range(2 * quad, min(2 * quad + 2, size.low_pairs)):
            settled = pair_product(lhs, implicit_ref, pair, columns)
            values.append(jnp.where(wet_rows(pair, wet, columns), settled, 0.0))
    if last:
        for pair, value in enumerate(values):
            fields_ref[PAIR * pair : PAIR * pair + PAIR, :] = value
        fields_ref[size.low_rows : size.low_rows + size.high_rows, :] = high_ref[...]
        for channel in range(CHANNELS):
            out_ref = state_ref if channel < 2 else tangent_ref
            out_ref[:, channel % 2, :] = fields_ref[pl.ds(channel, size.levels, stride=CHANNELS), :]
        return
    for pair, value in enumerate(values):
        low_ref[PAIR * pair : PAIR * pair + PAIR, :] = value
    blank = jnp.zeros((PAIR, columns), F32)
    for quad in range(size.ghost_quads):
        two = [
            values[pair] if pair < len(values) else blank for pair in (2 * quad, 2 * quad + 1)
        ]
        send_ref[QUAD * quad : QUAD * quad + QUAD, :] = jnp.concatenate(two, axis=0).astype(BF16)


def gather_kernel(arrived_ref, flux_ref):
    flux = jnp.sum(arrived_ref[:, 0, :], axis=0, keepdims=True)
    flux_ref[...] = flux[:, : flux_ref.shape[1]]


def call(body, name, outputs, scratch, operands, flops=1000000, in_hbm=()):
    space = lambda place: pltpu.HBM if place in in_hbm else pltpu.VMEM
    operands = [
        pltpu.with_memory_space_constraint(value, pltpu.HBM) if place in in_hbm else value
        for place, value in enumerate(operands)
    ]
    return pl.pallas_call(
        body,
        name=name,
        out_shape=outputs,
        in_specs=[pl.BlockSpec(memory_space=space(k)) for k in range(len(operands))],
        out_specs=[pl.BlockSpec(memory_space=pltpu.VMEM)] * len(outputs),
        scratch_shapes=scratch,
        compiler_params=pltpu.CompilerParams(vmem_limit_bytes=8 * MIB),
        cost_estimate=pl.CostEstimate(flops=flops, bytes_accessed=100000, transcendentals=0),
    )(*operands)


def on_device(
    tracer_state,
    krylov_direction,
    explicit_tiles,
    implicit_tiles,
    explicit_columns,
    ghost_levels,
    wet_levels,
    surface_light,
    martin_exponent,
    column_slots,
):
    size = Sizes(tracer_state.shape[1], tracer_state.shape[2], ghost_levels.shape[1])
    columns = size.columns
    tile_count = lax.axis_size("tile")
    slots = column_slots.shape[1]
    width = -(-tile_count * slots // 128) * 128
    row_of = lambda value: value.reshape(1, columns)
    wet, light, exponent = row_of(wet_levels), row_of(surface_light), row_of(martin_exponent)

    same_chip = [(d, d ^ 1) for d in range(tile_count)]
    next_chip = [(d, (d + (1 if d % 2 else -1)) % tile_count) for d in range(tile_count)]
    opposite = [(d, (d + tile_count // 2) % tile_count) for d in range(tile_count)]

    def exchange(value):
        across = lax.ppermute(value, "tile", opposite)
        other = lax.ppermute(value, "tile", next_chip)
        pair = lax.ppermute(value, "tile", same_chip)
        return pair, other, across

    def shape(rows, dtype=F32):
        return pltpu.VMEM((rows, columns), dtype)

    def tiles(levels):
        return pltpu.VMEM((levels, 3, columns, columns), BF16)

    padded = pltpu.VMEM((size.padded, columns), F32)
    low_scratch = pltpu.VMEM((QUAD * size.low_quads + 2 * EDGE, columns), F32)
    local_scratch = [padded, padded, pltpu.VMEM((CHANNELS * PAIR, columns), F32)]
    depth_shape = pltpu.VMEM((explicit_columns.shape[1], columns), jnp.int32)

    low, high, send = call(
        functools.partial(prepare_kernel, size),
        "prepare",
        [shape(size.low_rows), shape(size.high_rows), shape(size.send_rows, BF16)],
        [pltpu.VMEM((size.rows, columns), F32)],
        [tracer_state.transpose(1, 0, 2), krylov_direction.transpose(1, 0, 2)],
    )
    for time_index in range(STEPS):
        first, last = time_index == 0, time_index == STEPS - 1
        ghosts = exchange(send)
        operands = [low, high, wet, light]
        outputs = [shape(size.rows), shape(size.high_rows)]
        if first:
            partial, high, total, remineral, depth, own, ghost, implicit = call(
                functools.partial(local_kernel, size, "first", slots),
                "local_first",
                outputs
                + [
                    shape(1),
                    shape(size.rows),
                    depth_shape,
                    tiles(size.levels),
                    tiles(2 * size.ghost_pairs),
                    tiles(size.levels),
                ],
                local_scratch + [pltpu.SemaphoreType.DMA((6,))],
                operands + [exponent, explicit_columns.T, explicit_tiles, implicit_tiles],
                8000000,
                (6, 7),
            )
        elif last:
            partial, high, payload = call(
                functools.partial(local_kernel, size, "last", slots),
                "local_last",
                outputs + [jax.ShapeDtypeStruct((tile_count, 1, width), F32)],
                local_scratch,
                operands + [remineral, total, own, implicit, column_slots],
                4000000,
            )
            arrived = lax.all_to_all(payload, "tile", split_axis=0, concat_axis=0, tiled=True)
        else:
            partial, high, total = call(
                functools.partial(local_kernel, size, "middle", slots),
                "local",
                outputs + [shape(1)],
                local_scratch,
                operands + [remineral, total, own, implicit],
                4000000,
            )
        operands = [partial, *ghosts, depth, wet]
        if last:
            tall = jax.ShapeDtypeStruct((size.levels, CHANNELS // 2, columns), F32)
            state_out, tangent_out = call(
                functools.partial(ghost_kernel, size, True),
                "ghost_last",
                [tall, tall],
                [
                    low_scratch,
                    pltpu.VMEM((size.rows, columns), F32),
                    tiles(2 * size.ghost_pairs),
                    tiles(2 * size.low_pairs),
                    pltpu.SemaphoreType.DMA((2,)),
                ],
                operands + [explicit_tiles, implicit_tiles, high],
                2000000,
                (6, 7),
            )
        else:
            low, send = call(
                functools.partial(ghost_kernel, size, False),
                "ghost",
                [shape(size.low_rows), shape(size.send_rows, BF16)],
                [low_scratch],
                operands + [ghost, implicit],
            )
    (flux,) = call(
        gather_kernel,
        "gather",
        [jax.ShapeDtypeStruct((1, tile_count * slots), F32)],
        [],
        [arrived],
    )
    return state_out.transpose(1, 0, 2), tangent_out.transpose(1, 0, 2), flux.reshape(-1)


def solution(mesh):
    return jax.shard_map(
        on_device,
        mesh=mesh,
        in_specs=(
            P(None, None, ("groups", "tile")),
            P(None, None, ("groups", "tile")),
            P("tile", None, None, None),
            P("tile", None, None, None),
            P("tile", None),
            P("tile", None),
            P("tile"),
            P(("groups", "tile")),
            P(("groups", "tile")),
            P("tile", None),
        ),
        out_specs=(
            P(None, None, ("groups", "tile")),
            P(None, None, ("groups", "tile")),
            P(("groups", "tile")),
        ),
        check_vma=False,
    )
```

time: 87 us -> 43.8 us (0.50)
  matrix products: 19.2 us -> 0 us
  local copies, waits for them, and re-layouts: 20.8 us -> 4.3 us
  other arithmetic: 16.1 us -> 0 us
  Pallas kernels: 0 us -> 13 us
  starting transfers between devices: 21.7 us -> 18.4 us
    dot_general x6 -> x0, matrix products: 19.2 us -> none  [the longest x3 16.4 us: on_device(): jnp.einsum('lkcj,lkji->lci', tile_pool[explicit_columns], explicit_tiles,...]
    gather x7 -> x0, local copies, waits for them, and re-layouts: 14.6 us -> none  [the longest x3 6.62 us: on_device(): tile_pool[explicit_columns]]
    pallas_call x0 -> x8, Pallas kernels: none -> 13 us  [call(): pl.pallas_call(body, name=name, out_shape=outputs, in_specs=[pl.BlockSpec...]
    concatenate x4 -> x0, other arithmetic: 7.92 us -> none  [the longest x3 7.91 us: on_device(): jnp.concatenate([rounded, ghosts.reshape(-1, channels, column_count)], 0)]
    select_n x3 -> x0, other arithmetic: 2.09 us -> none  [the longest x1 0.7 us: on_device(): jnp.concatenate([export_total, jnp.zeros((1,), jnp.float32)])[column_slots]]
    ppermute x9, starting transfers between devices: 15.9 us -> 14.1 us  [the longest x3 11.3 us: exchange(): other = lax.ppermute(value, 'tile', next_chip)]
    all_to_all x1, waiting for transfers between devices: 1.78 us -> 0.01 us  [on_device(): lax.all_to_all(payload, 'tile', split_axis=0, concat_axis=0, tiled=True)]
    sub x5 -> x0, other arithmetic: 1.74 us -> none  [the longest x4 1.09 us: sources(): dop_fraction * uptake - decayed]
  transfers between devices with their start and end apart: 10 -> 10, of which waited for: 5 -> 4; matrix products, arithmetic and copies ran while one was open for 12% -> 0% of each run, Pallas kernels for 0% -> 22%
where the time goes in v1:
time: 43.8 us; the launch traced here: 43.5 us
  starting transfers between devices  18.4 us (42%)
  Pallas kernels  13 us (30%)
  waiting for transfers between devices  7.03 us (16%)
  local copies, waits for them, and re-layouts  4.3 us (10%)
  between operations  0.8 us (2%)
    pallas_call x8, Pallas kernels, call(): pl.pallas_call(body, name=name, out_shape=outputs, in_specs=[pl.BlockSpec...  13 us
    ppermute x3, starting transfers between devices, exchange(): other = lax.ppermute(value, 'tile', next_chip)  11.3 us
    unnamed x16, local copies, waits for them, and re-layouts  4.3 us
    all_to_all x1, starting transfers between devices, on_device(): lax.all_to_all(payload, 'tile', split_axis=0, concat_axis=0, tiled=True)  4.24 us
    ppermute x3, waiting for transfers between devices, exchange(): other = lax.ppermute(value, 'tile', next_chip)  3.72 us
    ppermute x3, waiting for transfers between devices, exchange(): across = lax.ppermute(value, 'tile', opposite)  3.29 us
    ppermute x3, starting transfers between devices, exchange(): across = lax.ppermute(value, 'tile', opposite)  1.75 us
    ppermute x3, starting transfers between devices, exchange(): pair = lax.ppermute(value, 'tile', same_chip)  1.06 us
  transfers between devices with their start and end apart: 10, of which 4 were waited for; matrix products, arithmetic and copies ran while one was open for 0% of the time, Pallas kernels for 22%

profile of v1, /device:TPU:0, one launch (start us, length us, event | category | flops | bytes accessed | tf_op | source)
XLA Modules:
  0.0 43.5 jit_solution(8561540333509638667)
XLA Ops:
  0.6 0.0 copy-start
  0.6 0.8 %copy-done = f32[2,50,128]{2,0,1:T(2,128)S(1)} copy-done((f32[2,50,128]{2,0,1:T(2,128)S(1)}, f32[2,50,128]{2,0,1:T(2,128)}, u32[]{:S(2)}) %copy-start) | copy-done | bytes 51224
  1.4 0.0 copy-start.1
  1.4 0.8 %copy-done.1 = f32[2,50,128]{2,0,1:T(2,128)S(1)} copy-done((f32[2,50,128]{2,0,1:T(2,128)S(1)}, f32[2,50,128]{2,0,1:T(2,128)}, u32[]{:S(2)}) %copy-start.1) | copy-done | bytes 51224
  2.2 0.1 prepare.1
  2.3 0.6 %collective-permute-start = (bf16[112,128]{1,0:T(8,128)(2,1)S(1)}, bf16[112,128]{1,0:T(8,128)(2,1)S(1)}, u32[]{:S(2)}, u32[]{:S(2)}) collective-permute-start(bf16[112,128]{1,0:T(8,128)(2,1)S(1)} %get-tuple-element.29), channel_id=1, source_target_pairs={{0,1},{1,0},{2,3},{3,2},{4,5},{5,4},{6,7},{7,6},{8,9},{9,8},{10,11... | collective-permute-start | bytes 86024 | tf_op jit(solution)/shard_map/ppermute | solution.py:352
  2.9 5.7 %collective-permute-start.1 = (bf16[112,128]{1,0:T(8,128)(2,1)S(1)}, bf16[112,128]{1,0:T(8,128)(2,1)S(1)}, u32[]{:S(2)}, u32[]{:S(2)}) collective-permute-start(bf16[112,128]{1,0:T(8,128)(2,1)S(1)} %get-tuple-element.29), channel_id=1, source_target_pairs={{0,15},{1,2},{2,1},{3,4},{4,3},{5,6},{6,5},{7,8},{8,7},{9,10},{10,... | collective-permute-start | bytes 86024 | tf_op jit(solution)/shard_map/ppermute | solution.py:351
  8.5 0.0 collective-permute-start.2
  8.5 0.0 copy-start.2
  8.5 0.7 %copy-done.2 = s32[128]{0:T(128)S(1)} copy-done((s32[128]{0:T(128)S(1)}, s32[128]{0:T(128)}, u32[]{:S(2)}) %copy-start.2) | copy-done | bytes 536
  9.2 0.0 copy-start.5
  9.2 0.7 %copy-done.5 = f32[128]{0:T(128)S(1)} copy-done((f32[128]{0:T(128)S(1)}, f32[128]{0:T(128)}, u32[]{:S(2)}) %copy-start.5) | copy-done | bytes 536
  9.8 0.0 copy-start.6
  9.8 0.7 %copy-done.6 = s32[50,6]{0,1:T(8,128)S(1)} copy-done((s32[50,6]{0,1:T(8,128)S(1)}, s32[50,6]{0,1:T(8,128)}, u32[]{:S(2)}) %copy-start.6) | copy-done | bytes 1224
  10.5 0.0 copy-start.7
  10.5 0.7 %copy-done.7 = f32[128]{0:T(128)S(1)} copy-done((f32[128]{0:T(128)S(1)}, f32[128]{0:T(128)}, u32[]{:S(2)}) %copy-start.7) | copy-done | bytes 536
  11.2 4.7 %local_first.1 = (f32[208,128]{1,0:T(8,128)S(1)}, f32[96,128]{1,0:T(8,128)S(1)}, f32[1,128]{1,0:T(1,128)S(1)}, f32[208,128]{1,0:T(8,128)S(1)}, s32[6,128]{1,0:T(...) custom-call(f32[104,128]{1,0:T(8,128)S(1)} %get-tuple-element.26.ref, ...), custom_call_target="tpu_custom_call" | custom-call | flops 8000000 | bytes 100000 | tf_op jit(solution)/shard_map/local_first/pallas_call | solution.py:313
  15.9 0.0 collective-permute-done.refs_1_
  15.9 0.0 collective-permute-done.1.refs_2_
  15.9 0.0 collective-permute-done.2.refs_3_
  15.9 0.7 %ghost.2 = (f32[104,128]{1,0:T(8,128)S(1)}, bf16[112,128]{1,0:T(8,128)(2,1)S(1)}) custom-call(f32[208,128]{1,0:T(8,128)S(1)} %get-tuple-element.28.refs_0_, bf16[112,128]{1,0:T(8,128)(2,1)S(1)} %collective-permute-done.refs_1_, bf16[112,128]{1,0:T(8,128)(2,1)S(1)} %collective-permute-done.1.refs_2_, bf16[112,128]{1,0:T(8,128)(2,1)S(1)} %collective-permute-done.2.refs_3_, ...), custom_call_target="tpu_custom_call" | custom-call | flops 1000000 | bytes 100000 | tf_op jit(solution)/shard_map/ghost/pallas_call | solution.py:313
  16.6 0.1 collective-permute-start.3
  16.7 1.3 %collective-permute-start.4 = (bf16[112,128]{1,0:T(8,128)(2,1)S(1)}, bf16[112,128]{1,0:T(8,128)(2,1)S(1)}, u32[]{:S(2)}, u32[]{:S(2)}) collective-permute-start(bf16[112,128]{1,0:T(8,128)(2,1)S(1)} %get-tuple-element.39), channel_id=1, source_target_pairs={{0,15},{1,2},{2,1},{3,4},{4,3},{5,6},{6,5},{7,8},{8,7},{9,10},{10,... | collective-permute-start | bytes 86024 | tf_op jit(solution)/shard_map/ppermute | solution.py:351
  18.0 1.7 %collective-permute-start.5 = (bf16[112,128]{1,0:T(8,128)(2,1)S(1)}, bf16[112,128]{1,0:T(8,128)(2,1)S(1)}, u32[]{:S(2)}, u32[]{:S(2)}) collective-permute-start(bf16[112,128]{1,0:T(8,128)(2,1)S(1)} %get-tuple-element.39), channel_id=1, source_target_pairs={{0,8},{1,9},{2,10},{3,11},{4,12},{5,13},{6,14},{7,15},{8,0},{9,1},... | collective-permute-start | bytes 86024 | tf_op jit(solution)/shard_map/ppermute | solution.py:350
  19.8 1.1 %local.1 = (f32[208,128]{1,0:T(8,128)S(1)}, f32[96,128]{1,0:T(8,128)S(1)}, f32[1,128]{1,0:T(1,128)S(1)}) custom-call(f32[104,128]{1,0:T(8,128)S(1)} %get-tuple-element.33.refs_0_, f32[96,128]{1,0:T(8,128)S(1)} %get-tuple-element.34.refs_1_, s32[1,128]{1,0:T(1,128)S(1)} %bitcast.13, f32[1,128]{1,0:T(1,128)S(1)} %bitcast.18, ...), custom_call_target="tpu_custom_call" | custom-call | flops 4000000 | bytes 100000 | tf_op jit(solution)/shard_map/local/pallas_call | solution.py:313
  20.8 0.0 copy-start.4
  20.8 0.0 collective-permute-done.3.refs_1_
  20.9 2.0 %collective-permute-done.4.refs_2_ = bf16[112,128]{1,0:T(8,128)(2,1)S(1)} collective-permute-done((bf16[112,128]{1,0:T(8,128)(2,1)S(1)}, bf16[112,128]{1,0:T(8,128)(2,1)S(1)}, u32[]{:S(2)}, u32[]{:S(2)}) %collective-permute-start.4) | collective-permute-done | bytes 28704 | tf_op jit(solution)/shard_map/ppermute | solution.py:351
  22.9 0.2 collective-permute-done.5.refs_3_
  23.1 0.7 %ghost.3 = (f32[104,128]{1,0:T(8,128)S(1)}, bf16[112,128]{1,0:T(8,128)(2,1)S(1)}) custom-call(f32[208,128]{1,0:T(8,128)S(1)} %get-tuple-element.38.refs_0_, bf16[112,128]{1,0:T(8,128)(2,1)S(1)} %collective-permute-done.3.refs_1_, bf16[112,128]{1,0:T(8,128)(2,1)S(1)} %collective-permute-done.4.refs_2_, bf16[112,128]{1,0:T(8,128)(2,1)S(1)} %collective-permute-done.5.refs_3_, ...), custom_call_target="tpu_custom_call" | custom-call | flops 1000000 | bytes 100000 | tf_op jit(solution)/shard_map/ghost/pallas_call | solution.py:313
  23.8 0.0 copy-done.4
  23.8 0.0 copy-start.3
  23.9 1.6 %local_last.1 = (f32[208,128]{1,0:T(8,128)S(1)}, f32[96,128]{1,0:T(8,128)S(1)}, f32[16,1,256]{2,1,0:T(1,128)}) custom-call(f32[104,128]{1,0:T(8,128)S(1)} %get-tuple-element.40.refs_0_, f32[96,128]{1,0:T(8,128)S(1)} %get-tuple-element.41.refs_1_, s32[1,128]{1,0:T(1,128)S(1)} %bitcast.15, f32[1,128]{1,0:T(1,128)S(1)} %bitcast.19, ...), custom_call_target="tpu_custom_call" | custom-call | flops 4000000 | bytes 100000 | tf_op jit(solution)/shard_map/local_last/pallas_call | solution.py:313
  25.5 4.2 %all-to-all-start = ((f32[16,1,256]{2,1,0:T(1,128)}), f32[16,1,256]{2,1,0:T(1,128)S(1)}, u32[]{:S(2)}, u32[]{:S(2)}) async-start(f32[16,1,256]{2,1,0:T(1,128)} %get-tuple-element.48), calls=%async_computation | async-start | bytes 32768 | tf_op jit(solution)/shard_map/all_to_all | solution.py:405
  29.7 0.4 collective-permute-start.6
  30.1 4.3 %collective-permute-start.7 = (bf16[112,128]{1,0:T(8,128)(2,1)S(1)}, bf16[112,128]{1,0:T(8,128)(2,1)S(1)}, u32[]{:S(2)}, u32[]{:S(2)}) collective-permute-start(bf16[112,128]{1,0:T(8,128)(2,1)S(1)} %get-tuple-element.44), channel_id=1, source_target_pairs={{0,15},{1,2},{2,1},{3,4},{4,3},{5,6},{6,5},{7,8},{8,7},{9,10},{10,... | collective-permute-start | bytes 86024 | tf_op jit(solution)/shard_map/ppermute | solution.py:351
  34.5 0.0 collective-permute-start.8
  34.5 0.0 collective-permute-done.6.refs_1_
  34.5 1.7 %collective-permute-done.7.refs_2_ = bf16[112,128]{1,0:T(8,128)(2,1)S(1)} collective-permute-done((bf16[112,128]{1,0:T(8,128)(2,1)S(1)}, bf16[112,128]{1,0:T(8,128)(2,1)S(1)}, u32[]{:S(2)}, u32[]{:S(2)}) %collective-permute-start.7) | collective-permute-done | bytes 28704 | tf_op jit(solution)/shard_map/ppermute | solution.py:351
  36.2 3.0 %collective-permute-done.8.refs_3_ = bf16[112,128]{1,0:T(8,128)(2,1)S(1)} collective-permute-done((bf16[112,128]{1,0:T(8,128)(2,1)S(1)}, bf16[112,128]{1,0:T(8,128)(2,1)S(1)}, u32[]{:S(2)}, u32[]{:S(2)}) %collective-permute-start.8) | collective-permute-done | bytes 28704 | tf_op jit(solution)/shard_map/ppermute | solution.py:350
  39.2 0.0 copy-done.3
  39.2 3.6 %ghost_last.1 = (f32[50,2,128]{2,1,0:T(2,128)}, f32[50,2,128]{2,1,0:T(2,128)}) custom-call(f32[208,128]{1,0:T(8,128)S(1)} %get-tuple-element.43.refs_0_, bf16[112,128]{1,0:T(8,128)(2,1)S(1)} %collective-permute-done.6.refs_1_, bf16[112,128]{1,0:T(8,128)(2,1)S(1)} %collective-permute-done.7.refs_2_, bf16[112,128]{1,0:T(8,128)(2,1)S(1)} %collective-permute-done.8.refs_3_, ...), custom_call_target="tpu_custom_call" | custom-call | flops 2000000 | bytes 100000 | tf_op jit(solution)/shard_map/ghost_last/pallas_call | solution.py:313
  42.9 0.0 all-to-all-done.arrived_ref
  42.9 0.6 %gather.1 = f32[1,192]{1,0:T(1,128)} custom-call(f32[16,1,256]{2,1,0:T(1,128)S(1)} %all-to-all-done.arrived_ref), custom_call_target="tpu_custom_call" | custom-call | flops 1000000 | bytes 100000 | tf_op jit(solution)/shard_map/gather/pallas_call | solution.py:313
Async XLA Ops:
  0.6 0.8 %copy-start = (f32[2,50,128]{2,0,1:T(2,128)S(1)}, f32[2,50,128]{2,0,1:T(2,128)}, u32[]{:S(2)}) copy-start(f32[2,50,128]{2,0,1:T(2,128)} %param.10) | copy-start | bytes 153604
  1.4 0.8 %copy-start.1 = (f32[2,50,128]{2,0,1:T(2,128)S(1)}, f32[2,50,128]{2,0,1:T(2,128)}, u32[]{:S(2)}) copy-start(f32[2,50,128]{2,0,1:T(2,128)} %param.11) | copy-start | bytes 153604
  2.3 13.6 %collective-permute-start = (bf16[112,128]{1,0:T(8,128)(2,1)S(1)}, bf16[112,128]{1,0:T(8,128)(2,1)S(1)}, u32[]{:S(2)}, u32[]{:S(2)}) collective-permute-start(bf16[112,128]{1,0:T(8,128)(2,1)S(1)} %get-tuple-element.29), channel_id=1, source_target_pairs={{0,1},{1,0},{2,3},{3,2},{4,5},{5,4},{6,7},{7,6},{8,9},{9,8},{10,11... | collective-permute-start | bytes 86024 | tf_op jit(solution)/shard_map/ppermute | solution.py:352
  2.9 13.0 %collective-permute-start.1 = (bf16[112,128]{1,0:T(8,128)(2,1)S(1)}, bf16[112,128]{1,0:T(8,128)(2,1)S(1)}, u32[]{:S(2)}, u32[]{:S(2)}) collective-permute-start(bf16[112,128]{1,0:T(8,128)(2,1)S(1)} %get-tuple-element.29), channel_id=1, source_target_pairs={{0,15},{1,2},{2,1},{3,4},{4,3},{5,6},{6,5},{7,8},{8,7},{9,10},{10,... | collective-permute-start | bytes 86024 | tf_op jit(solution)/shard_map/ppermute | solution.py:351
  8.5 7.4 %collective-permute-start.2 = (bf16[112,128]{1,0:T(8,128)(2,1)S(1)}, bf16[112,128]{1,0:T(8,128)(2,1)S(1)}, u32[]{:S(2)}, u32[]{:S(2)}) collective-permute-start(bf16[112,128]{1,0:T(8,128)(2,1)S(1)} %get-tuple-element.29), channel_id=1, source_target_pairs={{0,8},{1,9},{2,10},{3,11},{4,12},{5,13},{6,14},{7,15},{8,0},{9,1},... | collective-permute-start | bytes 86024 | tf_op jit(solution)/shard_map/ppermute | solution.py:350
  8.5 0.7 %copy-start.2 = (s32[128]{0:T(128)S(1)}, s32[128]{0:T(128)}, u32[]{:S(2)}) copy-start(s32[128]{0:T(128)} %param.15) | copy-start | bytes 1540
  9.2 0.7 %copy-start.5 = (f32[128]{0:T(128)S(1)}, f32[128]{0:T(128)}, u32[]{:S(2)}) copy-start(f32[128]{0:T(128)} %param.16) | copy-start | bytes 1540
  9.8 0.7 %copy-start.6 = (s32[50,6]{0,1:T(8,128)S(1)}, s32[50,6]{0,1:T(8,128)}, u32[]{:S(2)}) copy-start(s32[50,6]{0,1:T(8,128)} %param.14) | copy-start | bytes 3604
  10.5 0.7 %copy-start.7 = (f32[128]{0:T(128)S(1)}, f32[128]{0:T(128)}, u32[]{:S(2)}) copy-start(f32[128]{0:T(128)} %param.17) | copy-start | bytes 1540
  16.6 4.3 %collective-permute-start.3 = (bf16[112,128]{1,0:T(8,128)(2,1)S(1)}, bf16[112,128]{1,0:T(8,128)(2,1)S(1)}, u32[]{:S(2)}, u32[]{:S(2)}) collective-permute-start(bf16[112,128]{1,0:T(8,128)(2,1)S(1)} %get-tuple-element.39), channel_id=1, source_target_pairs={{0,1},{1,0},{2,3},{3,2},{4,5},{5,4},{6,7},{7,6},{8,9},{9,8},{10,11... | collective-permute-start | bytes 86024 | tf_op jit(solution)/shard_map/ppermute | solution.py:352
  16.7 6.2 %collective-permute-start.4 = (bf16[112,128]{1,0:T(8,128)(2,1)S(1)}, bf16[112,128]{1,0:T(8,128)(2,1)S(1)}, u32[]{:S(2)}, u32[]{:S(2)}) collective-permute-start(bf16[112,128]{1,0:T(8,128)(2,1)S(1)} %get-tuple-element.39), channel_id=1, source_target_pairs={{0,15},{1,2},{2,1},{3,4},{4,3},{5,6},{6,5},{7,8},{8,7},{9,10},{10,... | collective-permute-start | bytes 86024 | tf_op jit(solution)/shard_map/ppermute | solution.py:351
  18.0 5.1 %collective-permute-start.5 = (bf16[112,128]{1,0:T(8,128)(2,1)S(1)}, bf16[112,128]{1,0:T(8,128)(2,1)S(1)}, u32[]{:S(2)}, u32[]{:S(2)}) collective-permute-start(bf16[112,128]{1,0:T(8,128)(2,1)S(1)} %get-tuple-element.39), channel_id=1, source_target_pairs={{0,8},{1,9},{2,10},{3,11},{4,12},{5,13},{6,14},{7,15},{8,0},{9,1},... | collective-permute-start | bytes 86024 | tf_op jit(solution)/shard_map/ppermute | solution.py:350
  20.8 3.0 %copy-start.4 = (s32[16,12]{1,0:T(8,128)S(1)}, s32[16,12]{1,0:T(8,128)}, u32[]{:S(2)}) copy-start(s32[16,12]{1,0:T(8,128)} %refs_8_.1) | copy-start | bytes 2308
  23.8 15.4 %copy-start.3 = (s32[128]{0:T(128)S(1)}, s32[128]{0:T(128)}, u32[]{:S(2)}) copy-start(s32[128]{0:T(128)} %param.15) | copy-start | bytes 1540
  25.5 17.4 %all-to-all-start = ((f32[16,1,256]{2,1,0:T(1,128)}), f32[16,1,256]{2,1,0:T(1,128)S(1)}, u32[]{:S(2)}, u32[]{:S(2)}) async-start(f32[16,1,256]{2,1,0:T(1,128)} %get-tuple-element.48), calls=%async_computation | async-start | bytes 32768 | tf_op jit(solution)/shard_map/all_to_all | solution.py:405
  29.7 4.8 %collective-permute-start.6 = (bf16[112,128]{1,0:T(8,128)(2,1)S(1)}, bf16[112,128]{1,0:T(8,128)(2,1)S(1)}, u32[]{:S(2)}, u32[]{:S(2)}) collective-permute-start(bf16[112,128]{1,0:T(8,128)(2,1)S(1)} %get-tuple-element.44), channel_id=1, source_target_pairs={{0,1},{1,0},{2,3},{3,2},{4,5},{5,4},{6,7},{7,6},{8,9},{9,8},{10,11... | collective-permute-start | bytes 86024 | tf_op jit(solution)/shard_map/ppermute | solution.py:352
  30.1 6.1 %collective-permute-start.7 = (bf16[112,128]{1,0:T(8,128)(2,1)S(1)}, bf16[112,128]{1,0:T(8,128)(2,1)S(1)}, u32[]{:S(2)}, u32[]{:S(2)}) collective-permute-start(bf16[112,128]{1,0:T(8,128)(2,1)S(1)} %get-tuple-element.44), channel_id=1, source_target_pairs={{0,15},{1,2},{2,1},{3,4},{4,3},{5,6},{6,5},{7,8},{8,7},{9,10},{10,... | collective-permute-start | bytes 86024 | tf_op jit(solution)/shard_map/ppermute | solution.py:351
  34.5 4.8 %collective-permute-start.8 = (bf16[112,128]{1,0:T(8,128)(2,1)S(1)}, bf16[112,128]{1,0:T(8,128)(2,1)S(1)}, u32[]{:S(2)}, u32[]{:S(2)}) collective-permute-start(bf16[112,128]{1,0:T(8,128)(2,1)S(1)} %get-tuple-element.44), channel_id=1, source_target_pairs={{0,8},{1,9},{2,10},{3,11},{4,12},{5,13},{6,14},{7,15},{8,0},{9,1},... | collective-permute-start | bytes 86024 | tf_op jit(solution)/shard_map/ppermute | solution.py:350

commit v2 on v1

--- a/solution.py
+++ b/solution.py
@@ -7,6 +7,7 @@
 from jax.experimental.pallas import tpu as pltpu
 from jax.sharding import PartitionSpec as P
 
+
 EUPHOTIC = 6
 STEPS = 3
 
@@ -19,6 +20,7 @@
 F32 = jnp.float32
 BF16 = jnp.bfloat16
 MIB = 1 << 20
+PREPARE_FLOPS = 10**10
 
 CHANNELS = 4
 PAIR = 2 * CHANNELS
@@ -30,7 +32,6 @@
     def __init__(self, levels, columns, depth):
         self.levels = levels
         self.columns = columns
-        self.depth = depth
         self.pairs = levels // 2
         self.quads = (levels + 3) // 4
         self.rows = QUAD * self.quads
@@ -48,13 +49,14 @@
     return lax.broadcasted_iota(jnp.int32, (PAIR, columns), 0)
 
 
-def tiles_of(ref, level, columns):
-    return ref[level].reshape(3 * columns, columns)
-
-
-def pair_product(lhs, ref, pair, columns):
+def tiles_of(ref, level, first, columns):
+    return ref[level, first : first + 3].reshape(3 * columns, columns)
+
+
+def pair_product(lhs, ref, pair, columns, first=0):
     rhs = jnp.concatenate(
-        [tiles_of(ref, 2 * pair, columns), tiles_of(ref, 2 * pair + 1, columns)], axis=1
+        [tiles_of(ref, 2 * pair, first, columns), tiles_of(ref, 2 * pair + 1, first, columns)],
+        axis=1,
     )
     product = jnp.dot(lhs, rhs, preferred_element_type=F32)
     top = PAIR * (pair % 2)
@@ -93,55 +95,40 @@
     return jnp.where(level < wet - 1, reaching, 0.0)
 
 
-def prepare_kernel(size, state_ref, krylov_ref, low_ref, high_ref, send_ref, fields_ref):
+def prepare_kernel(size, small, *refs):
+    state_hbm, krylov_hbm = refs[:2]
+    small_hbm = refs[2 : 2 + small]
+    low_ref, high_ref, send_ref = refs[2 + small : 5 + small]
+    small_refs = refs[5 + small : 5 + 2 * small]
+    state_ref, krylov_ref, fields_ref, semaphore = refs[5 + 2 * small :]
+    pairs = [(state_hbm, state_ref), (krylov_hbm, krylov_ref), *zip(small_hbm, small_refs)]
+    copies = [
+        pltpu.make_async_copy(source, target, semaphore.at[place])
+        for place, (source, target) in enumerate(pairs)
+    ]
+    for copy in copies:
+        copy.start()
     fields_ref[...] = jnp.zeros_like(fields_ref)
+    copies[0].wait()
+    copies[1].wait()
     for channel in range(CHANNELS):
         source = state_ref if channel < 2 else krylov_ref
         fields_ref[pl.ds(channel, size.levels, stride=CHANNELS), :] = source[:, channel % 2, :]
     low_ref[...] = fields_ref[: size.low_rows, :]
     high_ref[...] = fields_ref[size.low_rows : size.low_rows + size.high_rows, :]
     send_ref[...] = fields_ref[: size.send_rows, :].astype(BF16)
-
-
-def chunks_of(size):
-    cuts = [size.quads * k // 3 for k in range(4)]
-    return [(4 * a, min(4 * b, size.levels)) for a, b in zip(cuts, cuts[1:])]
-
-
-def weight_copies(size, explicit_hbm, implicit_hbm, own_ref, ghost_ref, implicit_ref, semaphore):
-    copies = []
-    low = 2 * size.low_pairs
-
-    def add(source, target):
-        copies.append(pltpu.make_async_copy(source, target, semaphore.at[len(copies)]))
-
-    for start, stop in chunks_of(size):
-        part = pl.ds(start, stop - start)
-        add(explicit_hbm.at[part, pl.ds(0, 3)], own_ref.at[part])
-    part = pl.ds(low, size.levels - low)
-    add(implicit_hbm.at[part], implicit_ref.at[part])
-    part = pl.ds(0, 2 * size.ghost_pairs)
-    add(explicit_hbm.at[part, pl.ds(3, 3)], ghost_ref)
-    part = pl.ds(0, low)
-    add(implicit_hbm.at[part], implicit_ref.at[part])
-    return copies
+    for copy in copies[2:]:
+        copy.wait()
 
 
 def local_kernel(size, stage, slots, *refs):
     low_ref, high_ref, wet_ref, light_ref = refs[:4]
-    copies = None
     if stage == "first":
-        exponent_ref, columns_ref, explicit_hbm, implicit_hbm = refs[4:8]
+        exponent_ref, columns_ref, explicit_ref, implicit_ref = refs[4:8]
         partial_ref, next_high_ref, total_ref, remineral_ref, depth_ref = refs[8:13]
-        own_ref, ghost_ref, implicit_ref = refs[13:16]
-        fields_ref, middle_ref, rate_ref, semaphore = refs[16:]
-        copies = weight_copies(
-            size, explicit_hbm, implicit_hbm, own_ref, ghost_ref, implicit_ref, semaphore
-        )
-        for copy in copies:
-            copy.start()
+        fields_ref, middle_ref, rate_ref = refs[13:]
     else:
-        remineral_ref, total_in_ref, own_ref, implicit_ref = refs[4:8]
+        remineral_ref, total_in_ref, explicit_ref, implicit_ref = refs[4:8]
         if stage == "last":
             slots_ref, partial_ref, next_high_ref, payload_ref = refs[8:12]
         else:
@@ -205,20 +192,15 @@
             rate = rate + rate_ref[top : top + PAIR, :]
         return rate
 
-    arrivals = {start // 4: place for place, (start, _) in enumerate(chunks_of(size))}
     for quad in range(size.quads):
-        if copies and quad in arrivals:
-            copies[arrivals[quad]].wait()
         lhs = window(fields_ref, EDGE + QUAD * quad, (0, -CHANNELS, CHANNELS))
         for pair in range(2 * quad, min(2 * quad + 2, size.pairs)):
             top = PAIR * pair
-            value = pair_product(lhs, own_ref, pair, columns) + sources(pair)
+            value = pair_product(lhs, explicit_ref, pair, columns) + sources(pair)
             partial_ref[top : top + PAIR, :] = value
             middle_ref[EDGE + top : EDGE + top + PAIR, :] = value
     for start in range(live, size.rows, PAIR):
         partial_ref[start : start + PAIR, :] = zero_edge
-    if copies:
-        copies[-3].wait()
     for quad in range(size.low_pairs // 2, size.quads):
         lhs = window(middle_ref, EDGE + QUAD * quad, (-CHANNELS, 0, CHANNELS))
         for pair in range(max(2 * quad, size.low_pairs), min(2 * quad + 2, size.pairs)):
@@ -227,9 +209,6 @@
             next_high_ref[top : top + PAIR, :] = jnp.where(
                 wet_rows(pair, wet, columns), settled, 0.0
             )
-    if copies:
-        copies[-2].wait()
-        copies[-1].wait()
 
 
 def ghost_kernel(size, last, *refs):
@@ -247,8 +226,10 @@
         ]
         for copy in copies:
             copy.start()
+        first = 0
     else:
         ghost_ref, implicit_ref, low_ref, send_ref, middle_ref = refs[6:]
+        first = 3
     columns = size.columns
     wet = wet_ref[...]
     even = lax.axis_index("tile") % 2 == 0
@@ -271,7 +252,7 @@
         lhs = jnp.concatenate([before, after, across], axis=1).astype(BF16)
         for pair in range(2 * quad, min(2 * quad + 2, size.ghost_pairs)):
             top = PAIR * pair
-            value = pair_product(lhs, ghost_ref, pair, columns)
+            value = pair_product(lhs, ghost_ref, pair, columns, first)
             middle_ref[EDGE + top : EDGE + top + PAIR, :] = value + partial_ref[top : top + PAIR, :]
     if last:
         copies[1].wait()
@@ -304,7 +285,11 @@
     flux_ref[...] = flux[:, : flux_ref.shape[1]]
 
 
-def call(body, name, outputs, scratch, operands, flops=1000000, in_hbm=()):
+def in_vmem(value):
+    return pltpu.with_memory_space_constraint(value, pltpu.VMEM)
+
+
+def call(body, outputs, scratch, operands, flops=1000000, in_hbm=()):
     space = lambda place: pltpu.HBM if place in in_hbm else pltpu.VMEM
     operands = [
         pltpu.with_memory_space_constraint(value, pltpu.HBM) if place in in_hbm else value
@@ -312,7 +297,6 @@
     ]
     return pl.pallas_call(
         body,
-        name=name,
         out_shape=outputs,
         in_specs=[pl.BlockSpec(memory_space=space(k)) for k in range(len(operands))],
         out_specs=[pl.BlockSpec(memory_space=pltpu.VMEM)] * len(outputs),
@@ -340,7 +324,7 @@
     slots = column_slots.shape[1]
     width = -(-tile_count * slots // 128) * 128
     row_of = lambda value: value.reshape(1, columns)
-    wet, light, exponent = row_of(wet_levels), row_of(surface_light), row_of(martin_exponent)
+    explicit, implicit = in_vmem(explicit_tiles), in_vmem(implicit_tiles)
 
     same_chip = [(d, d ^ 1) for d in range(tile_count)]
     next_chip = [(d, (d + (1 if d % 2 else -1)) % tile_count) for d in range(tile_count)]
@@ -363,12 +347,27 @@
     local_scratch = [padded, padded, pltpu.VMEM((CHANNELS * PAIR, columns), F32)]
     depth_shape = pltpu.VMEM((explicit_columns.shape[1], columns), jnp.int32)
 
-    low, high, send = call(
-        functools.partial(prepare_kernel, size),
-        "prepare",
-        [shape(size.low_rows), shape(size.high_rows), shape(size.send_rows, BF16)],
-        [pltpu.VMEM((size.rows, columns), F32)],
-        [tracer_state.transpose(1, 0, 2), krylov_direction.transpose(1, 0, 2)],
+    small = [
+        row_of(wet_levels),
+        row_of(surface_light),
+        row_of(martin_exponent),
+        explicit_columns.T,
+        column_slots,
+    ]
+    tall = pltpu.VMEM((size.levels, CHANNELS // 2, columns), F32)
+    low, high, send, wet, light, exponent, column_rows, slot_rows = call(
+        functools.partial(prepare_kernel, size, len(small)),
+        [shape(size.low_rows), shape(size.high_rows), shape(size.send_rows, BF16)]
+        + [pltpu.VMEM(value.shape, value.dtype) for value in small],
+        [
+            tall,
+            tall,
+            pltpu.VMEM((size.rows, columns), F32),
+            pltpu.SemaphoreType.DMA((2 + len(small),)),
+        ],
+        [tracer_state.transpose(1, 0, 2), krylov_direction.transpose(1, 0, 2)] + small,
+        PREPARE_FLOPS,
+        tuple(range(2 + len(small))),
     )
     for time_index in range(STEPS):
         first, last = time_index == 0, time_index == STEPS - 1
@@ -376,49 +375,36 @@
         operands = [low, high, wet, light]
         outputs = [shape(size.rows), shape(size.high_rows)]
         if first:
-            partial, high, total, remineral, depth, own, ghost, implicit = call(
+            partial, high, total, remineral, depth = call(
                 functools.partial(local_kernel, size, "first", slots),
-                "local_first",
-                outputs
-                + [
-                    shape(1),
-                    shape(size.rows),
-                    depth_shape,
-                    tiles(size.levels),
-                    tiles(2 * size.ghost_pairs),
-                    tiles(size.levels),
-                ],
-                local_scratch + [pltpu.SemaphoreType.DMA((6,))],
-                operands + [exponent, explicit_columns.T, explicit_tiles, implicit_tiles],
-                8000000,
-                (6, 7),
+                outputs + [shape(1), shape(size.rows), depth_shape],
+                local_scratch,
+                operands + [exponent, column_rows, explicit, implicit],
+                4000000,
             )
         elif last:
             partial, high, payload = call(
                 functools.partial(local_kernel, size, "last", slots),
-                "local_last",
                 outputs + [jax.ShapeDtypeStruct((tile_count, 1, width), F32)],
                 local_scratch,
-                operands + [remineral, total, own, implicit, column_slots],
+                operands + [remineral, total, explicit, implicit, slot_rows],
                 4000000,
             )
             arrived = lax.all_to_all(payload, "tile", split_axis=0, concat_axis=0, tiled=True)
         else:
             partial, high, total = call(
                 functools.partial(local_kernel, size, "middle", slots),
-                "local",
                 outputs + [shape(1)],
                 local_scratch,
-                operands + [remineral, total, own, implicit],
+                operands + [remineral, total, explicit, implicit],
                 4000000,
             )
         operands = [partial, *ghosts, depth, wet]
         if last:
-            tall = jax.ShapeDtypeStruct((size.levels, CHANNELS // 2, columns), F32)
+            result = jax.ShapeDtypeStruct((size.levels, CHANNELS // 2, columns), F32)
             state_out, tangent_out = call(
                 functools.partial(ghost_kernel, size, True),
-                "ghost_last",
-                [tall, tall],
+                [result, result],
                 [
                     low_scratch,
                     pltpu.VMEM((size.rows, columns), F32),
@@ -433,17 +419,12 @@
         else:
             low, send = call(
                 functools.partial(ghost_kernel, size, False),
-                "ghost",
                 [shape(size.low_rows), shape(size.send_rows, BF16)],
                 [low_scratch],
-                operands + [ghost, implicit],
+                operands + [explicit, implicit],
             )
     (flux,) = call(
-        gather_kernel,
-        "gather",
-        [jax.ShapeDtypeStruct((1, tile_count * slots), F32)],
-        [],
-        [arrived],
+        gather_kernel, [jax.ShapeDtypeStruct((1, tile_count * slots), F32)], [], [arrived]
     )
     return state_out.transpose(1, 0, 2), tangent_out.transpose(1, 0, 2), flux.reshape(-1)
 

time: 43.8 us -> 39.4 us (0.90)
  waiting for transfers between devices: 7.03 us -> 12.1 us
  local copies, waits for them, and re-layouts: 4.3 us -> 0.01 us
  starting transfers between devices: 18.4 us -> 15.8 us
  Pallas kernels: 13 us -> 10.5 us
    unnamed x16 -> x4, local copies, waits for them, and re-layouts: 4.3 us -> 0.01 us
    ppermute x3, waiting for transfers between devices: 3.29 us -> 6.18 us  [exchange(): across = lax.ppermute(value, 'tile', opposite)]
    pallas_call x8, Pallas kernels: 13 us -> 10.5 us  [call(): pl.pallas_call(body, out_shape=outputs, in_specs=[pl.BlockSpec(memory_spa...]
    ppermute x3, waiting for transfers between devices: 3.72 us -> 5.93 us  [exchange(): other = lax.ppermute(value, 'tile', next_chip)]
    ppermute x3, starting transfers between devices: 1.75 us -> 0.01 us  [exchange(): across = lax.ppermute(value, 'tile', opposite)]
    all_to_all x1, starting transfers between devices: 4.24 us -> 3.49 us  [on_device(): lax.all_to_all(payload, 'tile', split_axis=0, concat_axis=0, tiled=True)]
  transfers between devices with their start and end apart: 10 -> 10, of which waited for: 4 -> 5; matrix products, arithmetic and copies ran while one was open for 0% -> 0% of each run, Pallas kernels for 22% -> 15%
where the time goes in v2:
time: 39.4 us; the launch traced here: 39.2 us
  starting transfers between devices  15.8 us (40%)
  waiting for transfers between devices  12.1 us (31%)
  Pallas kernels  10.5 us (27%)
  between operations  0.77 us (2%)
    ppermute x3, starting transfers between devices, exchange(): other = lax.ppermute(value, 'tile', next_chip)  11.3 us
    pallas_call x8, Pallas kernels, call(): pl.pallas_call(body, out_shape=outputs, in_specs=[pl.BlockSpec(memory_spa...  10.5 us
    ppermute x3, waiting for transfers between devices, exchange(): across = lax.ppermute(value, 'tile', opposite)  6.18 us
    ppermute x3, waiting for transfers between devices, exchange(): other = lax.ppermute(value, 'tile', next_chip)  5.93 us
    all_to_all x1, starting transfers between devices, on_device(): lax.all_to_all(payload, 'tile', split_axis=0, concat_axis=0, tiled=True)  3.49 us
    ppermute x3, starting transfers between devices, exchange(): pair = lax.ppermute(value, 'tile', same_chip)  1.02 us
  transfers between devices with their start and end apart: 10, of which 5 were waited for; matrix products, arithmetic and copies ran while one was open for 0% of the time, Pallas kernels for 15%

profile of v2, /device:TPU:0, one launch (start us, length us, event | category | flops | bytes accessed | tf_op | source)
XLA Modules:
  0.0 39.2 jit_solution(6561071987618470559)
XLA Ops:
  0.6 0.0 copy-start
  0.6 0.0 copy-start.1
  0.7 1.1 %shard_map.112 = (f32[104,128]{1,0:T(8,128)S(1)}, f32[96,128]{1,0:T(8,128)S(1)}, bf16[112,128]{1,0:T(8,128)(2,1)S(1)}, s32[1,128]{1,0:T(1,128)S(1)}, f32[1,128]{...) custom-call(f32[50,2,128]{2,1,0:T(2,128)} %bitcast.10, f32[50,2,128]{2,1,0:T(2,128)} %bitcast.11, ...), custom_call_target="tpu_custom_call" | custom-call | flops 10000000000 | bytes 100000 | tf_op jit(solution)/shard_map/pallas_call | solution.py:298
  1.8 0.6 %collective-permute-start = (bf16[112,128]{1,0:T(8,128)(2,1)S(1)}, bf16[112,128]{1,0:T(8,128)(2,1)S(1)}, u32[]{:S(2)}, u32[]{:S(2)}) collective-permute-start(bf16[112,128]{1,0:T(8,128)(2,1)S(1)} %get-tuple-element.35), channel_id=1, source_target_pairs={{0,1},{1,0},{2,3},{3,2},{4,5},{5,4},{6,7},{7,6},{8,9},{9,8},{10,11... | collective-permute-start | bytes 86024 | tf_op jit(solution)/shard_map/ppermute | solution.py:336
  2.3 5.7 %collective-permute-start.1 = (bf16[112,128]{1,0:T(8,128)(2,1)S(1)}, bf16[112,128]{1,0:T(8,128)(2,1)S(1)}, u32[]{:S(2)}, u32[]{:S(2)}) collective-permute-start(bf16[112,128]{1,0:T(8,128)(2,1)S(1)} %get-tuple-element.35), channel_id=1, source_target_pairs={{0,15},{1,2},{2,1},{3,4},{4,3},{5,6},{6,5},{7,8},{8,7},{9,10},{10,... | collective-permute-start | bytes 86024 | tf_op jit(solution)/shard_map/ppermute | solution.py:335
  8.0 0.0 collective-permute-start.2
  8.0 0.0 copy-done
  8.0 0.0 copy-done.1
  8.0 1.1 %shard_map.113 = (f32[208,128]{1,0:T(8,128)S(1)}, f32[96,128]{1,0:T(8,128)S(1)}, f32[1,128]{1,0:T(1,128)S(1)}, f32[208,128]{1,0:T(8,128)S(1)}, s32[6,128]{1,0:T(8,128)S(1)}) custom-call(f32[104,128]{1,0:T(8,128)S(1)} %get-tuple-element.28.refs_0_, f32[96,128]{1,0:T(8,128)S(1)} %get-tuple-element.29.refs_1_, s32[1,128]{1,0:T(1,128)S(1)} %get-tuple-element.30.refs_2_.refs_5_, ...), custom_call_target="tpu_custom_call" | custom-call | flops 4000000 | bytes 100000 | tf_op jit(solution)/shard_map/pallas_call | solution.py:298
  9.1 0.0 collective-permute-done.refs_1_
  9.1 0.5 %collective-permute-done.1.refs_2_ = bf16[112,128]{1,0:T(8,128)(2,1)S(1)} collective-permute-done((bf16[112,128]{1,0:T(8,128)(2,1)S(1)}, bf16[112,128]{1,0:T(8,128)(2,1)S(1)}, u32[]{:S(2)}, u32[]{:S(2)}) %collective-permute-start.1) | collective-permute-done | bytes 28704 | tf_op jit(solution)/shard_map/ppermute | solution.py:335
  9.7 3.1 %collective-permute-done.2.refs_3_ = bf16[112,128]{1,0:T(8,128)(2,1)S(1)} collective-permute-done((bf16[112,128]{1,0:T(8,128)(2,1)S(1)}, bf16[112,128]{1,0:T(8,128)(2,1)S(1)}, u32[]{:S(2)}, u32[]{:S(2)}) %collective-permute-start.2) | collective-permute-done | bytes 28704 | tf_op jit(solution)/shard_map/ppermute | solution.py:334
  12.8 0.7 %shard_map.114 = (f32[104,128]{1,0:T(8,128)S(1)}, bf16[112,128]{1,0:T(8,128)(2,1)S(1)}) custom-call(f32[208,128]{1,0:T(8,128)S(1)} %get-tuple-element.34.refs_0_, bf16[112,128]{1,0:T(8,128)(2,1)S(1)} %collective-permute-done.refs_1_, bf16[112,128]{1,0:T(8,128)(2,1)S(1)} %collective-permute-done.1.refs_2_, ...), custom_call_target="tpu_custom_call" | custom-call | flops 1000000 | bytes 100000 | tf_op jit(solution)/shard_map/pallas_call | solution.py:298
  13.5 0.1 collective-permute-start.3
  13.6 1.3 %collective-permute-start.4 = (bf16[112,128]{1,0:T(8,128)(2,1)S(1)}, bf16[112,128]{1,0:T(8,128)(2,1)S(1)}, u32[]{:S(2)}, u32[]{:S(2)}) collective-permute-start(bf16[112,128]{1,0:T(8,128)(2,1)S(1)} %get-tuple-element.42), channel_id=1, source_target_pairs={{0,15},{1,2},{2,1},{3,4},{4,3},{5,6},{6,5},{7,8},{8,7},{9,10},{10,... | collective-permute-start | bytes 86024 | tf_op jit(solution)/shard_map/ppermute | solution.py:335
  14.9 0.0 collective-permute-start.5
  14.9 1.1 %shard_map.115 = (f32[208,128]{1,0:T(8,128)S(1)}, f32[96,128]{1,0:T(8,128)S(1)}, f32[1,128]{1,0:T(1,128)S(1)}) custom-call(f32[104,128]{1,0:T(8,128)S(1)} %get-tuple-element.37.refs_0_, f32[96,128]{1,0:T(8,128)S(1)} %get-tuple-element.38.refs_1_, s32[1,128]{1,0:T(1,128)S(1)} %get-tuple-element.30.refs_2_.refs_5_, f32[1,128]{1,0:T(1,128)S(1)} %get-tuple-element.31.refs_3_, ...), custom_call_target="tpu_custom_call" | custom-call | flops 4000000 | bytes 100000 | tf_op jit(solution)/shard_map/pallas_call | solution.py:298
  15.9 0.0 collective-permute-done.3.refs_1_
  15.9 3.7 %collective-permute-done.4.refs_2_ = bf16[112,128]{1,0:T(8,128)(2,1)S(1)} collective-permute-done((bf16[112,128]{1,0:T(8,128)(2,1)S(1)}, bf16[112,128]{1,0:T(8,128)(2,1)S(1)}, u32[]{:S(2)}, u32[]{:S(2)}) %collective-permute-start.4) | collective-permute-done | bytes 28704 | tf_op jit(solution)/shard_map/ppermute | solution.py:335
  19.6 0.0 collective-permute-done.5.refs_3_
  19.6 0.7 %shard_map.116 = (f32[104,128]{1,0:T(8,128)S(1)}, bf16[112,128]{1,0:T(8,128)(2,1)S(1)}) custom-call(f32[208,128]{1,0:T(8,128)S(1)} %get-tuple-element.41.refs_0_, bf16[112,128]{1,0:T(8,128)(2,1)S(1)} %collective-permute-done.3.refs_1_, bf16[112,128]{1,0:T(8,128)(2,1)S(1)} %collective-permute-done.4.refs_2_, ...), custom_call_target="tpu_custom_call" | custom-call | flops 1000000 | bytes 100000 | tf_op jit(solution)/shard_map/pallas_call | solution.py:298
  20.3 1.7 %shard_map.117 = (f32[208,128]{1,0:T(8,128)S(1)}, f32[96,128]{1,0:T(8,128)S(1)}, f32[16,1,256]{2,1,0:T(1,128)}) custom-call(f32[104,128]{1,0:T(8,128)S(1)} %get-tuple-element.43.refs_0_, f32[96,128]{1,0:T(8,128)S(1)} %get-tuple-element.44.refs_1_, s32[1,128]{1,0:T(1,128)S(1)} %get-tuple-element.30.refs_2_.refs_5_, f32[1,128]{1,0:T(1,128)S(1)} %get-tuple-element.31.refs_3_, ...), custom_call_target="tpu_custom_call" | custom-call | flops 4000000 | bytes 100000 | tf_op jit(solution)/shard_map/pallas_call | solution.py:298
  22.0 3.5 %all-to-all-start = ((f32[16,1,256]{2,1,0:T(1,128)}), f32[16,1,256]{2,1,0:T(1,128)S(1)}, u32[]{:S(2)}, u32[]{:S(2)}) async-start(f32[16,1,256]{2,1,0:T(1,128)} %get-tuple-element.52), calls=%async_computation | async-start | bytes 32768 | tf_op jit(solution)/shard_map/all_to_all | solution.py:393
  25.5 0.4 collective-permute-start.6
  25.9 4.3 %collective-permute-start.7 = (bf16[112,128]{1,0:T(8,128)(2,1)S(1)}, bf16[112,128]{1,0:T(8,128)(2,1)S(1)}, u32[]{:S(2)}, u32[]{:S(2)}) collective-permute-start(bf16[112,128]{1,0:T(8,128)(2,1)S(1)} %get-tuple-element.48), channel_id=1, source_target_pairs={{0,15},{1,2},{2,1},{3,4},{4,3},{5,6},{6,5},{7,8},{8,7},{9,10},{10,... | collective-permute-start | bytes 86024 | tf_op jit(solution)/shard_map/ppermute | solution.py:335
  30.2 0.0 collective-permute-start.8
  30.2 0.0 collective-permute-done.6.refs_1_
  30.2 1.7 %collective-permute-done.7.refs_2_ = bf16[112,128]{1,0:T(8,128)(2,1)S(1)} collective-permute-done((bf16[112,128]{1,0:T(8,128)(2,1)S(1)}, bf16[112,128]{1,0:T(8,128)(2,1)S(1)}, u32[]{:S(2)}, u32[]{:S(2)}) %collective-permute-start.7) | collective-permute-done | bytes 28704 | tf_op jit(solution)/shard_map/ppermute | solution.py:335
  31.9 3.1 %collective-permute-done.8.refs_3_ = bf16[112,128]{1,0:T(8,128)(2,1)S(1)} collective-permute-done((bf16[112,128]{1,0:T(8,128)(2,1)S(1)}, bf16[112,128]{1,0:T(8,128)(2,1)S(1)}, u32[]{:S(2)}, u32[]{:S(2)}) %collective-permute-start.8) | collective-permute-done | bytes 28704 | tf_op jit(solution)/shard_map/ppermute | solution.py:334
  35.0 3.6 %shard_map.118 = (f32[50,2,128]{2,1,0:T(2,128)}, f32[50,2,128]{2,1,0:T(2,128)}) custom-call(f32[208,128]{1,0:T(8,128)S(1)} %get-tuple-element.47.refs_0_, bf16[112,128]{1,0:T(8,128)(2,1)S(1)} %collective-permute-done.6.refs_1_, bf16[112,128]{1,0:T(8,128)(2,1)S(1)} %collective-permute-done.7.refs_2_, bf16[112,128]{1,0:T(8,128)(2,1)S(1)} %collective-permute-done.8.refs_3_, ...), custom_call_target="tpu_custom_call" | custom-call | flops 2000000 | bytes 100000 | tf_op jit(solution)/shard_map/pallas_call | solution.py:298
  38.6 0.0 all-to-all-done.arrived_ref
  38.6 0.6 %shard_map.119 = f32[1,192]{1,0:T(1,128)} custom-call(f32[16,1,256]{2,1,0:T(1,128)S(1)} %all-to-all-done.arrived_ref), custom_call_target="tpu_custom_call" | custom-call | flops 1000000 | bytes 100000 | tf_op jit(solution)/shard_map/pallas_call | solution.py:298
Async XLA Ops:
  0.6 7.4 %copy-start = (bf16[50,6,128,128]{3,2,1,0:T(8,128)(2,1)S(1)}, bf16[50,6,128,128]{3,2,1,0:T(8,128)(2,1)}, u32[]{:S(2)}) copy-start(bf16[50,6,128,128]{3,2,1,0:T(8,128)(2,1)} %refs_6_.13) | copy-start | bytes 29491204
  0.6 7.4 %copy-start.1 = (bf16[50,3,128,128]{3,2,1,0:T(8,128)(2,1)S(1)}, bf16[50,3,128,128]{3,2,1,0:T(8,128)(2,1)}, u32[]{:S(2)}) copy-start(bf16[50,3,128,128]{3,2,1,0:T(8,128)(2,1)} %refs_7_.11) | copy-start | bytes 14745604
  1.8 7.3 %collective-permute-start = (bf16[112,128]{1,0:T(8,128)(2,1)S(1)}, bf16[112,128]{1,0:T(8,128)(2,1)S(1)}, u32[]{:S(2)}, u32[]{:S(2)}) collective-permute-start(bf16[112,128]{1,0:T(8,128)(2,1)S(1)} %get-tuple-element.35), channel_id=1, source_target_pairs={{0,1},{1,0},{2,3},{3,2},{4,5},{5,4},{6,7},{7,6},{8,9},{9,8},{10,11... | collective-permute-start | bytes 86024 | tf_op jit(solution)/shard_map/ppermute | solution.py:336
  2.3 7.3 %collective-permute-start.1 = (bf16[112,128]{1,0:T(8,128)(2,1)S(1)}, bf16[112,128]{1,0:T(8,128)(2,1)S(1)}, u32[]{:S(2)}, u32[]{:S(2)}) collective-permute-start(bf16[112,128]{1,0:T(8,128)(2,1)S(1)} %get-tuple-element.35), channel_id=1, source_target_pairs={{0,15},{1,2},{2,1},{3,4},{4,3},{5,6},{6,5},{7,8},{8,7},{9,10},{10,... | collective-permute-start | bytes 86024 | tf_op jit(solution)/shard_map/ppermute | solution.py:335
  8.0 4.8 %collective-permute-start.2 = (bf16[112,128]{1,0:T(8,128)(2,1)S(1)}, bf16[112,128]{1,0:T(8,128)(2,1)S(1)}, u32[]{:S(2)}, u32[]{:S(2)}) collective-permute-start(bf16[112,128]{1,0:T(8,128)(2,1)S(1)} %get-tuple-element.35), channel_id=1, source_target_pairs={{0,8},{1,9},{2,10},{3,11},{4,12},{5,13},{6,14},{7,15},{8,0},{9,1},... | collective-permute-start | bytes 86024 | tf_op jit(solution)/shard_map/ppermute | solution.py:334
  13.5 2.5 %collective-permute-start.3 = (bf16[112,128]{1,0:T(8,128)(2,1)S(1)}, bf16[112,128]{1,0:T(8,128)(2,1)S(1)}, u32[]{:S(2)}, u32[]{:S(2)}) collective-permute-start(bf16[112,128]{1,0:T(8,128)(2,1)S(1)} %get-tuple-element.42), channel_id=1, source_target_pairs={{0,1},{1,0},{2,3},{3,2},{4,5},{5,4},{6,7},{7,6},{8,9},{9,8},{10,11... | collective-permute-start | bytes 86024 | tf_op jit(solution)/shard_map/ppermute | solution.py:336
  13.6 6.1 %collective-permute-start.4 = (bf16[112,128]{1,0:T(8,128)(2,1)S(1)}, bf16[112,128]{1,0:T(8,128)(2,1)S(1)}, u32[]{:S(2)}, u32[]{:S(2)}) collective-permute-start(bf16[112,128]{1,0:T(8,128)(2,1)S(1)} %get-tuple-element.42), channel_id=1, source_target_pairs={{0,15},{1,2},{2,1},{3,4},{4,3},{5,6},{6,5},{7,8},{8,7},{9,10},{10,... | collective-permute-start | bytes 86024 | tf_op jit(solution)/shard_map/ppermute | solution.py:335
  14.9 4.8 %collective-permute-start.5 = (bf16[112,128]{1,0:T(8,128)(2,1)S(1)}, bf16[112,128]{1,0:T(8,128)(2,1)S(1)}, u32[]{:S(2)}, u32[]{:S(2)}) collective-permute-start(bf16[112,128]{1,0:T(8,128)(2,1)S(1)} %get-tuple-element.42), channel_id=1, source_target_pairs={{0,8},{1,9},{2,10},{3,11},{4,12},{5,13},{6,14},{7,15},{8,0},{9,1},... | collective-permute-start | bytes 86024 | tf_op jit(solution)/shard_map/ppermute | solution.py:334
  22.0 16.6 %all-to-all-start = ((f32[16,1,256]{2,1,0:T(1,128)}), f32[16,1,256]{2,1,0:T(1,128)S(1)}, u32[]{:S(2)}, u32[]{:S(2)}) async-start(f32[16,1,256]{2,1,0:T(1,128)} %get-tuple-element.52), calls=%async_computation | async-start | bytes 32768 | tf_op jit(solution)/shard_map/all_to_all | solution.py:393
  25.5 4.7 %collective-permute-start.6 = (bf16[112,128]{1,0:T(8,128)(2,1)S(1)}, bf16[112,128]{1,0:T(8,128)(2,1)S(1)}, u32[]{:S(2)}, u32[]{:S(2)}) collective-permute-start(bf16[112,128]{1,0:T(8,128)(2,1)S(1)} %get-tuple-element.48), channel_id=1, source_target_pairs={{0,1},{1,0},{2,3},{3,2},{4,5},{5,4},{6,7},{7,6},{8,9},{9,8},{10,11... | collective-permute-start | bytes 86024 | tf_op jit(solution)/shard_map/ppermute | solution.py:336
  25.9 6.0 %collective-permute-start.7 = (bf16[112,128]{1,0:T(8,128)(2,1)S(1)}, bf16[112,128]{1,0:T(8,128)(2,1)S(1)}, u32[]{:S(2)}, u32[]{:S(2)}) collective-permute-start(bf16[112,128]{1,0:T(8,128)(2,1)S(1)} %get-tuple-element.48), channel_id=1, source_target_pairs={{0,15},{1,2},{2,1},{3,4},{4,3},{5,6},{6,5},{7,8},{8,7},{9,10},{10,... | collective-permute-start | bytes 86024 | tf_op jit(solution)/shard_map/ppermute | solution.py:335
  30.2 4.8 %collective-permute-start.8 = (bf16[112,128]{1,0:T(8,128)(2,1)S(1)}, bf16[112,128]{1,0:T(8,128)(2,1)S(1)}, u32[]{:S(2)}, u32[]{:S(2)}) collective-permute-start(bf16[112,128]{1,0:T(8,128)(2,1)S(1)} %get-tuple-element.48), channel_id=1, source_target_pairs={{0,8},{1,9},{2,10},{3,11},{4,12},{5,13},{6,14},{7,15},{8,0},{9,1},... | collective-permute-start | bytes 86024 | tf_op jit(solution)/shard_map/ppermute | solution.py:334

commit v3 on v2

--- a/solution.py
+++ b/solution.py
@@ -121,18 +121,18 @@
         copy.wait()
 
 
-def local_kernel(size, stage, slots, *refs):
+def local_kernel(size, stage, *refs):
     low_ref, high_ref, wet_ref, light_ref = refs[:4]
     if stage == "first":
         exponent_ref, columns_ref, explicit_ref, implicit_ref = refs[4:8]
         partial_ref, next_high_ref, total_ref, remineral_ref, depth_ref = refs[8:13]
         fields_ref, middle_ref, rate_ref = refs[13:]
     else:
-        remineral_ref, total_in_ref, explicit_ref, implicit_ref = refs[4:8]
-        if stage == "last":
-            slots_ref, partial_ref, next_high_ref, payload_ref = refs[8:12]
+        remineral_ref, explicit_ref, implicit_ref = refs[4:7]
+        if stage == "middle":
+            total_in_ref, partial_ref, next_high_ref, total_ref = refs[7:11]
         else:
-            partial_ref, next_high_ref, total_ref = refs[8:11]
+            partial_ref, next_high_ref = refs[7:9]
         fields_ref, middle_ref, rate_ref = refs[-3:]
     columns = size.columns
     wet = wet_ref[...]
@@ -161,19 +161,10 @@
     uptake, slope = uptake_of(fields_ref, EDGE, wet, light, columns)
     export = (1.0 - dop_fraction) * jnp.sum(uptake, axis=0, keepdims=True)
     export_slope = (1.0 - dop_fraction) * jnp.sum(slope, axis=0, keepdims=True)
-    total = export if stage == "first" else total_in_ref[...] + export
-    if stage == "last":
-        targets, _, width = payload_ref.shape
-        column = lax.broadcasted_iota(jnp.int32, (targets, columns), 1)
-        lane = lax.broadcasted_iota(jnp.int32, (targets, width), 1) - slots * lax.axis_index("tile")
-        payload = jnp.zeros((targets, width), F32)
-        for slot in range(slots):
-            chosen = column == slots_ref[:, slot : slot + 1]
-            value = jnp.sum(jnp.where(chosen, total, 0.0), axis=1, keepdims=True)
-            payload = jnp.where(lane == slot, value, payload)
-        payload_ref[:, 0, :] = payload
-    else:
-        total_ref[...] = total
+    if stage == "first":
+        total_ref[...] = export
+    elif stage == "middle":
+        total_ref[...] = total_in_ref[...] + export
     for channel, rate in enumerate((uptake, uptake, slope, slope)):
         factor = time_step * (dop_fraction if channel % 2 else -1.0)
         rate_ref[pl.ds(channel, PAIR, stride=CHANNELS), :] = factor * rate
@@ -211,33 +202,62 @@
             )
 
 
-def ghost_kernel(size, last, *refs):
-    partial_ref, pair_ref, other_ref, across_ref, depth_ref, wet_ref = refs[:6]
-    if last:
-        explicit_hbm, implicit_hbm, high_ref = refs[6:9]
-        state_ref, tangent_ref, middle_ref, fields_ref, ghost_ref, implicit_ref, semaphore = refs[9:]
-        low = pl.ds(0, 2 * size.low_pairs)
-        part = pl.ds(0, 2 * size.ghost_pairs)
-        copies = [
-            pltpu.make_async_copy(
-                explicit_hbm.at[part, pl.ds(3, 3)], ghost_ref, semaphore.at[0]
-            ),
-            pltpu.make_async_copy(implicit_hbm.at[low], implicit_ref, semaphore.at[1]),
+def place_slots(total, slots_ref, slots, width):
+    targets = slots_ref.shape[0]
+    column = lax.broadcasted_iota(jnp.int32, (targets, total.shape[1]), 1)
+    lane = lax.broadcasted_iota(jnp.int32, (targets, width), 1) - slots * lax.axis_index("tile")
+    placed = jnp.zeros((targets, width), F32)
+    for slot in range(slots):
+        chosen = column == slots_ref[:, slot : slot + 1]
+        value = jnp.sum(jnp.where(chosen, total, 0.0), axis=1, keepdims=True)
+        placed = jnp.where(lane == slot, value, placed)
+    return placed
+
+
+def halves(rows):
+    half = rows.shape[0] // 2
+    upper = (lax.axis_index("tile") // half) % 2 == 1
+    first, second = rows[:half], rows[half:]
+    return jnp.where(upper, second, first), jnp.where(upper, first, second)
+
+
+def route_kernel(packed, *refs):
+    kept_ref, arrived_ref, keep_ref, send_ref = refs
+    rows = kept_ref[...]
+    if packed:
+        count, width = rows.shape
+        base = arrived_ref.shape[0] - 2 * count * (width // 128)
+        parts = [
+            arrived_ref[base + count * k : base + count * (k + 1), :].astype(F32)
+            for k in range(2 * (width // 128))
         ]
-        for copy in copies:
-            copy.start()
-        first = 0
+        high = jnp.concatenate(parts[: width // 128], axis=1)
+        low = jnp.concatenate(parts[width // 128 :], axis=1)
+        rows = rows + (high + low)
     else:
-        ghost_ref, implicit_ref, low_ref, send_ref, middle_ref = refs[6:]
-        first = 3
+        rows = rows + arrived_ref[...]
+    keep_ref[...], send_ref[...] = halves(rows)
+
+
+def flux_kernel(kept_ref, arrived_ref, flux_ref):
+    flux = kept_ref[...] + arrived_ref[...]
+    flux_ref[...] = flux[:, : flux_ref.shape[1]]
+
+
+def ghost_kernel(size, stage, slots, *refs):
+    partial_ref, pair_ref, other_ref, across_ref, depth_ref, wet_ref, explicit_ref, implicit_ref = refs[:8]
+    if stage == "last":
+        high_ref, state_ref, tangent_ref, middle_ref, fields_ref = refs[8:]
+    elif stage == "export":
+        light_ref, total_ref, slots_ref, low_ref, send_ref, across_out_ref, keep_ref, middle_ref = refs[8:]
+    else:
+        low_ref, send_ref, middle_ref = refs[8:]
     columns = size.columns
     wet = wet_ref[...]
     even = lax.axis_index("tile") % 2 == 0
     middle_ref[:EDGE, :] = jnp.zeros((EDGE, columns), F32)
     for top in range(PAIR * size.ghost_pairs, QUAD * size.low_quads + EDGE, PAIR):
         middle_ref[EDGE + top : EDGE + top + PAIR, :] = partial_ref[top : top + PAIR, :]
-    if last:
-        copies[0].wait()
     for quad in range(size.ghost_quads):
         span = slice(QUAD * quad, QUAD * quad + QUAD)
         own_chip = pair_ref[span, :].astype(F32)
@@ -252,17 +272,15 @@
         lhs = jnp.concatenate([before, after, across], axis=1).astype(BF16)
         for pair in range(2 * quad, min(2 * quad + 2, size.ghost_pairs)):
             top = PAIR * pair
-            value = pair_product(lhs, ghost_ref, pair, columns, first)
+            value = pair_product(lhs, explicit_ref, pair, columns, 3)
             middle_ref[EDGE + top : EDGE + top + PAIR, :] = value + partial_ref[top : top + PAIR, :]
-    if last:
-        copies[1].wait()
     values = []
     for quad in range(size.low_quads):
         lhs = window(middle_ref, EDGE + QUAD * quad, (-CHANNELS, 0, CHANNELS))
         for pair in range(2 * quad, min(2 * quad + 2, size.low_pairs)):
             settled = pair_product(lhs, implicit_ref, pair, columns)
             values.append(jnp.where(wet_rows(pair, wet, columns), settled, 0.0))
-    if last:
+    if stage == "last":
         for pair, value in enumerate(values):
             fields_ref[PAIR * pair : PAIR * pair + PAIR, :] = value
         fields_ref[size.low_rows : size.low_rows + size.high_rows, :] = high_ref[...]
@@ -277,12 +295,23 @@
         two = [
             values[pair] if pair < len(values) else blank for pair in (2 * quad, 2 * quad + 1)
         ]
-        send_ref[QUAD * quad : QUAD * quad + QUAD, :] = jnp.concatenate(two, axis=0).astype(BF16)
-
-
-def gather_kernel(arrived_ref, flux_ref):
-    flux = jnp.sum(arrived_ref[:, 0, :], axis=0, keepdims=True)
-    flux_ref[...] = flux[:, : flux_ref.shape[1]]
+        rows = jnp.concatenate(two, axis=0).astype(BF16)
+        send_ref[QUAD * quad : QUAD * quad + QUAD, :] = rows
+        if stage == "export":
+            across_out_ref[QUAD * quad : QUAD * quad + QUAD, :] = rows
+    if stage == "export":
+        uptake, _ = uptake_of(low_ref, 0, wet, light_ref[...], columns)
+        total = total_ref[...] + (1.0 - dop_fraction) * jnp.sum(uptake, axis=0, keepdims=True)
+        placed = place_slots(total, slots_ref, slots, keep_ref.shape[1])
+        keep_ref[...], leaving = halves(placed)
+        width = leaving.shape[1]
+        high = leaving.astype(BF16).astype(F32)
+        parts = [
+            part[:, start : start + 128]
+            for part in (high, leaving - high)
+            for start in range(0, width, 128)
+        ]
+        across_out_ref[size.send_rows :, :] = jnp.concatenate(parts, axis=0).astype(BF16)
 
 
 def in_vmem(value):
@@ -321,6 +350,7 @@
     size = Sizes(tracer_state.shape[1], tracer_state.shape[2], ghost_levels.shape[1])
     columns = size.columns
     tile_count = lax.axis_size("tile")
+    assert tile_count & (tile_count - 1) == 0
     slots = column_slots.shape[1]
     width = -(-tile_count * slots // 128) * 128
     row_of = lambda value: value.reshape(1, columns)
@@ -330,17 +360,14 @@
     next_chip = [(d, (d + (1 if d % 2 else -1)) % tile_count) for d in range(tile_count)]
     opposite = [(d, (d + tile_count // 2) % tile_count) for d in range(tile_count)]
 
-    def exchange(value):
-        across = lax.ppermute(value, "tile", opposite)
+    def exchange(value, across_value):
+        across = lax.ppermute(across_value, "tile", opposite)
         other = lax.ppermute(value, "tile", next_chip)
         pair = lax.ppermute(value, "tile", same_chip)
         return pair, other, across
 
     def shape(rows, dtype=F32):
         return pltpu.VMEM((rows, columns), dtype)
-
-    def tiles(levels):
-        return pltpu.VMEM((levels, 3, columns, columns), BF16)
 
     padded = pltpu.VMEM((size.padded, columns), F32)
     low_scratch = pltpu.VMEM((QUAD * size.low_quads + 2 * EDGE, columns), F32)
@@ -369,62 +396,79 @@
         PREPARE_FLOPS,
         tuple(range(2 + len(small))),
     )
+    across_send = send
     for time_index in range(STEPS):
         first, last = time_index == 0, time_index == STEPS - 1
-        ghosts = exchange(send)
+        ghosts = exchange(send, across_send)
         operands = [low, high, wet, light]
         outputs = [shape(size.rows), shape(size.high_rows)]
+        weights = [explicit, implicit]
         if first:
             partial, high, total, remineral, depth = call(
-                functools.partial(local_kernel, size, "first", slots),
+                functools.partial(local_kernel, size, "first"),
                 outputs + [shape(1), shape(size.rows), depth_shape],
                 local_scratch,
-                operands + [exponent, column_rows, explicit, implicit],
+                operands + [exponent, column_rows] + weights,
                 4000000,
             )
         elif last:
-            partial, high, payload = call(
-                functools.partial(local_kernel, size, "last", slots),
-                outputs + [jax.ShapeDtypeStruct((tile_count, 1, width), F32)],
+            partial, high = call(
+                functools.partial(local_kernel, size, "last"),
+                outputs,
                 local_scratch,
-                operands + [remineral, total, explicit, implicit, slot_rows],
+                operands + [remineral] + weights,
                 4000000,
             )
-            arrived = lax.all_to_all(payload, "tile", split_axis=0, concat_axis=0, tiled=True)
         else:
             partial, high, total = call(
-                functools.partial(local_kernel, size, "middle", slots),
+                functools.partial(local_kernel, size, "middle"),
                 outputs + [shape(1)],
                 local_scratch,
-                operands + [remineral, total, explicit, implicit],
+                operands + [remineral] + weights + [total],
                 4000000,
             )
-        operands = [partial, *ghosts, depth, wet]
+        operands = [partial, *ghosts, depth, wet] + weights
+        sends = [shape(size.low_rows), shape(size.send_rows, BF16)]
         if last:
             result = jax.ShapeDtypeStruct((size.levels, CHANNELS // 2, columns), F32)
             state_out, tangent_out = call(
-                functools.partial(ghost_kernel, size, True),
+                functools.partial(ghost_kernel, size, "last", slots),
                 [result, result],
-                [
-                    low_scratch,
-                    pltpu.VMEM((size.rows, columns), F32),
-                    tiles(2 * size.ghost_pairs),
-                    tiles(2 * size.low_pairs),
-                    pltpu.SemaphoreType.DMA((2,)),
-                ],
-                operands + [explicit_tiles, implicit_tiles, high],
+                [low_scratch, pltpu.VMEM((size.rows, columns), F32)],
+                operands + [high],
                 2000000,
-                (6, 7),
+            )
+        elif time_index == STEPS - 2:
+            half = tile_count // 2
+            packed_rows = size.send_rows + 2 * half * (width // 128)
+            low, send, across_send, kept = call(
+                functools.partial(ghost_kernel, size, "export", slots),
+                sends + [shape(packed_rows, BF16), pltpu.VMEM((half, width), F32)],
+                [low_scratch],
+                operands + [light, total, slot_rows],
             )
         else:
             low, send = call(
-                functools.partial(ghost_kernel, size, False),
-                [shape(size.low_rows), shape(size.send_rows, BF16)],
+                functools.partial(ghost_kernel, size, "middle", slots),
+                sends,
                 [low_scratch],
-                operands + [explicit, implicit],
-            )
+                operands,
+            )
+            across_send = send
+    arrived, half = ghosts[2], tile_count // 2
+    while half > 1:
+        half //= 2
+        piece = pltpu.VMEM((half, width), F32)
+        kept, leaving = call(
+            functools.partial(route_kernel, 2 * half == tile_count // 2),
+            [piece, piece],
+            [],
+            [kept, arrived],
+        )
+        partners = [(d, d ^ half) for d in range(tile_count)]
+        arrived = lax.ppermute(leaving, "tile", partners)
     (flux,) = call(
-        gather_kernel, [jax.ShapeDtypeStruct((1, tile_count * slots), F32)], [], [arrived]
+        flux_kernel, [jax.ShapeDtypeStruct((1, tile_count * slots), F32)], [], [kept, arrived]
     )
     return state_out.transpose(1, 0, 2), tangent_out.transpose(1, 0, 2), flux.reshape(-1)
 

time: 39.4 us -> 35.1 us (0.89)
  starting transfers between devices: 15.8 us -> 10 us
  waiting for transfers between devices: 12.1 us -> 16.4 us
  Pallas kernels: 10.5 us -> 7.77 us
    ppermute x3, starting transfers between devices: 11.3 us -> 4.38 us  [exchange(): other = lax.ppermute(value, 'tile', next_chip)]
    ppermute x3 -> x6, waiting for transfers between devices: 6.18 us -> 11.8 us  [the longest x3 7.17 us: on_device(): arrived = lax.ppermute(leaving, 'tile', partners)]
    ppermute x3 -> x6, starting transfers between devices: 0.01 us -> 5.47 us  [the longest x3 5.34 us: exchange(): across = lax.ppermute(across_value, 'tile', opposite)]
    all_to_all x1 -> x0, starting transfers between devices: 3.49 us -> none  [on_device(): lax.all_to_all(payload, 'tile', split_axis=0, concat_axis=0, tiled=True)]
    pallas_call x8 -> x11, Pallas kernels: 10.5 us -> 7.77 us  [call(): pl.pallas_call(body, out_shape=outputs, in_specs=[pl.BlockSpec(memory_spa...]
    ppermute x3, waiting for transfers between devices: 5.93 us -> 4.56 us  [exchange(): other = lax.ppermute(value, 'tile', next_chip)]
    ppermute x3, starting transfers between devices: 1.02 us -> 0.15 us  [exchange(): pair = lax.ppermute(value, 'tile', same_chip)]
  transfers between devices with their start and end apart: 10 -> 12, of which waited for: 5 -> 6; matrix products, arithmetic and copies ran while one was open for 0% -> 0% of each run, Pallas kernels for 15% -> 13%
where the time goes in v3:
time: 35.1 us; the launch traced here: 34.9 us
  waiting for transfers between devices  16.4 us (47%)
  starting transfers between devices  10 us (28%)
  Pallas kernels  7.77 us (22%)
  between operations  0.78 us (2%)
    pallas_call x11, Pallas kernels, call(): pl.pallas_call(body, out_shape=outputs, in_specs=[pl.BlockSpec(memory_spa...  7.77 us
    ppermute x3, waiting for transfers between devices, on_device(): arrived = lax.ppermute(leaving, 'tile', partners)  7.17 us
    ppermute x3, starting transfers between devices, exchange(): across = lax.ppermute(across_value, 'tile', opposite)  5.34 us
    ppermute x3, waiting for transfers between devices, exchange(): across = lax.ppermute(across_value, 'tile', opposite)  4.62 us
    ppermute x3, waiting for transfers between devices, exchange(): other = lax.ppermute(value, 'tile', next_chip)  4.56 us
    ppermute x3, starting transfers between devices, exchange(): other = lax.ppermute(value, 'tile', next_chip)  4.38 us
  transfers between devices with their start and end apart: 12, of which 6 were waited for; matrix products, arithmetic and copies ran while one was open for 0% of the time, Pallas kernels for 13%

profile of v3, /device:TPU:0, one launch (start us, length us, event | category | flops | bytes accessed | tf_op | source)
XLA Modules:
  0.0 34.9 jit_solution(15269422123990417720)
XLA Ops:
  0.6 0.0 copy-start
  0.6 0.0 copy-start.1
  0.7 1.1 %shard_map.112 = (f32[104,128]{1,0:T(8,128)S(1)}, f32[96,128]{1,0:T(8,128)S(1)}, bf16[112,128]{1,0:T(8,128)(2,1)S(1)}, s32[1,128]{1,0:T(1,128)S(1)}, f32[1,128]{...) custom-call(f32[50,2,128]{2,1,0:T(2,128)} %bitcast.9, f32[50,2,128]{2,1,0:T(2,128)} %bitcast.10, ...), custom_call_target="tpu_custom_call" | custom-call | flops 10000000000 | bytes 100000 | tf_op jit(solution)/shard_map/pallas_call | solution.py:327
  1.8 4.1 %collective-permute-start.2 = (bf16[112,128]{1,0:T(8,128)(2,1)S(1)}, bf16[112,128]{1,0:T(8,128)(2,1)S(1)}, u32[]{:S(2)}, u32[]{:S(2)}) collective-permute-start(bf16[112,128]{1,0:T(8,128)(2,1)S(1)} %get-tuple-element.42), channel_id=1, source_target_pairs={{0,8},{1,9},{2,10},{3,11},{4,12},{5,13},{6,14},{7,15},{8,0},{9,1},... | collective-permute-start | bytes 86024 | tf_op jit(solution)/shard_map/ppermute | solution.py:364
  5.9 1.5 %collective-permute-start.1 = (bf16[112,128]{1,0:T(8,128)(2,1)S(1)}, bf16[112,128]{1,0:T(8,128)(2,1)S(1)}, u32[]{:S(2)}, u32[]{:S(2)}) collective-permute-start(bf16[112,128]{1,0:T(8,128)(2,1)S(1)} %get-tuple-element.42), channel_id=1, source_target_pairs={{0,15},{1,2},{2,1},{3,4},{4,3},{5,6},{6,5},{7,8},{8,7},{9,10},{10,... | collective-permute-start | bytes 86024 | tf_op jit(solution)/shard_map/ppermute | solution.py:365
  7.4 0.1 collective-permute-start
  7.5 0.0 copy-done
  7.6 0.0 copy-done.1
  7.6 1.1 %shard_map.113 = (f32[208,128]{1,0:T(8,128)S(1)}, f32[96,128]{1,0:T(8,128)S(1)}, f32[1,128]{1,0:T(1,128)S(1)}, f32[208,128]{1,0:T(8,128)S(1)}, s32[6,128]{1,0:T(8,128)S(1)}) custom-call(f32[104,128]{1,0:T(8,128)S(1)} %get-tuple-element.35.refs_0_, f32[96,128]{1,0:T(8,128)S(1)} %get-tuple-element.36.refs_1_, s32[1,128]{1,0:T(1,128)S(1)} %get-tuple-element.37.refs_2_.refs_5_, ...), custom_call_target="tpu_custom_call" | custom-call | flops 4000000 | bytes 100000 | tf_op jit(solution)/shard_map/pallas_call | solution.py:327
  8.6 0.0 collective-permute-done.2.refs_3_
  8.6 3.3 %collective-permute-done.1.refs_2_ = bf16[112,128]{1,0:T(8,128)(2,1)S(1)} collective-permute-done((bf16[112,128]{1,0:T(8,128)(2,1)S(1)}, bf16[112,128]{1,0:T(8,128)(2,1)S(1)}, u32[]{:S(2)}, u32[]{:S(2)}) %collective-permute-start.1) | collective-permute-done | bytes 28704 | tf_op jit(solution)/shard_map/ppermute | solution.py:365
  11.9 0.0 collective-permute-done.refs_1_
  11.9 0.7 %shard_map.114 = (f32[104,128]{1,0:T(8,128)S(1)}, bf16[112,128]{1,0:T(8,128)(2,1)S(1)}) custom-call(f32[208,128]{1,0:T(8,128)S(1)} %get-tuple-element.41.refs_0_, bf16[112,128]{1,0:T(8,128)(2,1)S(1)} %collective-permute-done.refs_1_, bf16[112,128]{1,0:T(8,128)(2,1)S(1)} %collective-permute-done.1.refs_2_, ...), custom_call_target="tpu_custom_call" | custom-call | flops 1000000 | bytes 100000 | tf_op jit(solution)/shard_map/pallas_call | solution.py:327
  12.6 0.1 collective-permute-start.5
  12.7 2.0 %collective-permute-start.4 = (bf16[112,128]{1,0:T(8,128)(2,1)S(1)}, bf16[112,128]{1,0:T(8,128)(2,1)S(1)}, u32[]{:S(2)}, u32[]{:S(2)}) collective-permute-start(bf16[112,128]{1,0:T(8,128)(2,1)S(1)} %get-tuple-element.49), channel_id=1, source_target_pairs={{0,15},{1,2},{2,1},{3,4},{4,3},{5,6},{6,5},{7,8},{8,7},{9,10},{10,... | collective-permute-start | bytes 86024 | tf_op jit(solution)/shard_map/ppermute | solution.py:365
  14.7 0.0 collective-permute-start.3
  14.7 1.1 %shard_map.115 = (f32[208,128]{1,0:T(8,128)S(1)}, f32[96,128]{1,0:T(8,128)S(1)}, f32[1,128]{1,0:T(1,128)S(1)}) custom-call(f32[104,128]{1,0:T(8,128)S(1)} %get-tuple-element.44.refs_0_, f32[96,128]{1,0:T(8,128)S(1)} %get-tuple-element.45.refs_1_, s32[1,128]{1,0:T(1,128)S(1)} %get-tuple-element.37.refs_2_.refs_5_, ...), custom_call_target="tpu_custom_call" | custom-call | flops 4000000 | bytes 100000 | tf_op jit(solution)/shard_map/pallas_call | solution.py:327
  15.7 1.7 %collective-permute-done.5.refs_3_ = bf16[112,128]{1,0:T(8,128)(2,1)S(1)} collective-permute-done((bf16[112,128]{1,0:T(8,128)(2,1)S(1)}, bf16[112,128]{1,0:T(8,128)(2,1)S(1)}, u32[]{:S(2)}, u32[]{:S(2)}) %collective-permute-start.5) | collective-permute-done | bytes 28704 | tf_op jit(solution)/shard_map/ppermute | solution.py:364
  17.5 1.3 %collective-permute-done.4.refs_2_ = bf16[112,128]{1,0:T(8,128)(2,1)S(1)} collective-permute-done((bf16[112,128]{1,0:T(8,128)(2,1)S(1)}, bf16[112,128]{1,0:T(8,128)(2,1)S(1)}, u32[]{:S(2)}, u32[]{:S(2)}) %collective-permute-start.4) | collective-permute-done | bytes 28704 | tf_op jit(solution)/shard_map/ppermute | solution.py:365
  18.8 0.0 collective-permute-done.3.refs_1_
  18.8 0.7 %shard_map.116 = (f32[104,128]{1,0:T(8,128)S(1)}, bf16[112,128]{1,0:T(8,128)(2,1)S(1)}, bf16[144,128]{1,0:T(8,128)(2,1)S(1)}, f32[8,256]{1,0:T(8,128)S(1)}) custom-call(f32[208,128]{1,0:T(8,128)S(1)} %get-tuple-element.48.refs_0_, bf16[112,128]{1,0:T(8,128)(2,1)S(1)} %collective-permute-done.3.refs_1_, bf16[112,128]{1,0:T(8,128)(2,1)S(1)} %collective-permute-done.4.refs_2_, ...), custom_call_target="tpu_custom_call" | custom-call | flops 1000000 | bytes 100000 | tf_op jit(solution)/shard_map/pallas_call | solution.py:327
  19.5 1.1 %collective-permute-start.8 = (bf16[144,128]{1,0:T(8,128)(2,1)S(1)}, bf16[144,128]{1,0:T(8,128)(2,1)S(1)}, u32[]{:S(2)}, u32[]{:S(2)}) collective-permute-start(bf16[144,128]{1,0:T(8,128)(2,1)S(1)} %get-tuple-element.56), channel_id=1, source_target_pairs={{0,8},{1,9},{2,10},{3,11},{4,12},{5,13},{6,14},{7,15},{8,0},{9,1},... | collective-permute-start | bytes 110600 | tf_op jit(solution)/shard_map/ppermute | solution.py:364
  20.6 0.9 %collective-permute-start.7 = (bf16[112,128]{1,0:T(8,128)(2,1)S(1)}, bf16[112,128]{1,0:T(8,128)(2,1)S(1)}, u32[]{:S(2)}, u32[]{:S(2)}) collective-permute-start(bf16[112,128]{1,0:T(8,128)(2,1)S(1)} %get-tuple-element.55), channel_id=1, source_target_pairs={{0,15},{1,2},{2,1},{3,4},{4,3},{5,6},{6,5},{7,8},{8,7},{9,10},{10,... | collective-permute-start | bytes 86024 | tf_op jit(solution)/shard_map/ppermute | solution.py:365
  21.6 0.0 collective-permute-start.6
  21.6 2.9 %collective-permute-done.8.refs_3_.refs_1_ = bf16[144,128]{1,0:T(8,128)(2,1)S(1)} collective-permute-done((bf16[144,128]{1,0:T(8,128)(2,1)S(1)}, bf16[144,128]{1,0:T(8,128)(2,1)S(1)}, u32[]{:S(2)}, u32[]{:S(2)}) %collective-permute-start.8) | collective-permute-done | bytes 36896 | tf_op jit(solution)/shard_map/ppermute | solution.py:364
  24.4 0.0 collective-permute-start.9
  24.4 3.6 %collective-permute-done.9.refs_1_ = f32[4,256]{1,0:T(4,128)S(1)} collective-permute-done((f32[4,256]{1,0:T(4,128)S(1)}, f32[4,256]{1,0:T(4,128)S(1)}, u32[]{:S(2)}, u32[]{:S(2)}) %collective-permute-start.9) | collective-permute-done | bytes 4128 | tf_op jit(solution)/shard_map/ppermute | solution.py:469
  28.1 0.1 collective-permute-start.10
  28.1 3.6 %collective-permute-done.10.refs_1_ = f32[2,256]{1,0:T(2,128)S(1)} collective-permute-done((f32[2,256]{1,0:T(2,128)S(1)}, f32[2,256]{1,0:T(2,128)S(1)}, u32[]{:S(2)}, u32[]{:S(2)}) %collective-permute-start.10) | collective-permute-done | bytes 2080 | tf_op jit(solution)/shard_map/ppermute | solution.py:469
  31.7 0.1 collective-permute-start.11
  31.8 1.1 %shard_map.117 = (f32[208,128]{1,0:T(8,128)S(1)}, f32[96,128]{1,0:T(8,128)S(1)}) custom-call(f32[104,128]{1,0:T(8,128)S(1)} %get-tuple-element.52.refs_0_, f32[96,128]{1,0:T(8,128)S(1)} %get-tuple-element.53.refs_1_, s32[1,128]{1,0:T(1,128)S(1)} %get-tuple-element.37.refs_2_.refs_5_, f32[1,128]{1,0:T(1,128)S(1)} %get-tuple-element.38.refs_3_.refs_8_, ...), custom_call_target="tpu_custom_call" | custom-call | flops 4000000 | bytes 100000 | tf_op jit(solution)/shard_map/pallas_call | solution.py:327
  32.8 0.0 collective-permute-done.7.refs_2_
  32.9 0.0 collective-permute-done.6.refs_1_
  32.9 1.5 %shard_map.118 = (f32[50,2,128]{2,1,0:T(2,128)}, f32[50,2,128]{2,1,0:T(2,128)}) custom-call(f32[208,128]{1,0:T(8,128)S(1)} %get-tuple-element.54.refs_0_, bf16[112,128]{1,0:T(8,128)(2,1)S(1)} %collective-permute-done.6.refs_1_, bf16[112,128]{1,0:T(8,128)(2,1)S(1)} %collective-permute-done.7.refs_2_, ...), custom_call_target="tpu_custom_call" | custom-call | flops 2000000 | bytes 100000 | tf_op jit(solution)/shard_map/pallas_call | solution.py:327
  34.4 0.0 collective-permute-done.11.arrived_ref
  34.4 0.6 %shard_map.122 = f32[1,192]{1,0:T(1,128)} custom-call(f32[1,256]{1,0:T(1,128)S(1)} %get-tuple-element.65.kept_ref, f32[1,256]{1,0:T(1,128)S(1)} %collective-permute-done.11.arrived_ref), custom_call_target="tpu_custom_call" | custom-call | flops 1000000 | bytes 100000 | tf_op jit(solution)/shard_map/pallas_call | solution.py:327
  (3 shorter events, 0.0 us)
Async XLA Ops:
  0.6 6.9 %copy-start = (bf16[50,6,128,128]{3,2,1,0:T(8,128)(2,1)S(1)}, bf16[50,6,128,128]{3,2,1,0:T(8,128)(2,1)}, u32[]{:S(2)}) copy-start(bf16[50,6,128,128]{3,2,1,0:T(8,128)(2,1)} %refs_6_.13) | copy-start | bytes 29491204
  0.6 6.9 %copy-start.1 = (bf16[50,3,128,128]{3,2,1,0:T(8,128)(2,1)S(1)}, bf16[50,3,128,128]{3,2,1,0:T(8,128)(2,1)}, u32[]{:S(2)}) copy-start(bf16[50,3,128,128]{3,2,1,0:T(8,128)(2,1)} %refs_7_.7) | copy-start | bytes 14745604
  1.8 6.8 %collective-permute-start.2 = (bf16[112,128]{1,0:T(8,128)(2,1)S(1)}, bf16[112,128]{1,0:T(8,128)(2,1)S(1)}, u32[]{:S(2)}, u32[]{:S(2)}) collective-permute-start(bf16[112,128]{1,0:T(8,128)(2,1)S(1)} %get-tuple-element.42), channel_id=1, source_target_pairs={{0,8},{1,9},{2,10},{3,11},{4,12},{5,13},{6,14},{7,15},{8,0},{9,1},... | collective-permute-start | bytes 86024 | tf_op jit(solution)/shard_map/ppermute | solution.py:364
  5.9 6.0 %collective-permute-start.1 = (bf16[112,128]{1,0:T(8,128)(2,1)S(1)}, bf16[112,128]{1,0:T(8,128)(2,1)S(1)}, u32[]{:S(2)}, u32[]{:S(2)}) collective-permute-start(bf16[112,128]{1,0:T(8,128)(2,1)S(1)} %get-tuple-element.42), channel_id=1, source_target_pairs={{0,15},{1,2},{2,1},{3,4},{4,3},{5,6},{6,5},{7,8},{8,7},{9,10},{10,... | collective-permute-start | bytes 86024 | tf_op jit(solution)/shard_map/ppermute | solution.py:365
  7.4 4.5 %collective-permute-start = (bf16[112,128]{1,0:T(8,128)(2,1)S(1)}, bf16[112,128]{1,0:T(8,128)(2,1)S(1)}, u32[]{:S(2)}, u32[]{:S(2)}) collective-permute-start(bf16[112,128]{1,0:T(8,128)(2,1)S(1)} %get-tuple-element.42), channel_id=1, source_target_pairs={{0,1},{1,0},{2,3},{3,2},{4,5},{5,4},{6,7},{7,6},{8,9},{9,8},{10,11... | collective-permute-start | bytes 86024 | tf_op jit(solution)/shard_map/ppermute | solution.py:366
  12.6 4.9 %collective-permute-start.5 = (bf16[112,128]{1,0:T(8,128)(2,1)S(1)}, bf16[112,128]{1,0:T(8,128)(2,1)S(1)}, u32[]{:S(2)}, u32[]{:S(2)}) collective-permute-start(bf16[112,128]{1,0:T(8,128)(2,1)S(1)} %get-tuple-element.49), channel_id=1, source_target_pairs={{0,8},{1,9},{2,10},{3,11},{4,12},{5,13},{6,14},{7,15},{8,0},{9,1},... | collective-permute-start | bytes 86024 | tf_op jit(solution)/shard_map/ppermute | solution.py:364
  12.7 6.1 %collective-permute-start.4 = (bf16[112,128]{1,0:T(8,128)(2,1)S(1)}, bf16[112,128]{1,0:T(8,128)(2,1)S(1)}, u32[]{:S(2)}, u32[]{:S(2)}) collective-permute-start(bf16[112,128]{1,0:T(8,128)(2,1)S(1)} %get-tuple-element.49), channel_id=1, source_target_pairs={{0,15},{1,2},{2,1},{3,4},{4,3},{5,6},{6,5},{7,8},{8,7},{9,10},{10,... | collective-permute-start | bytes 86024 | tf_op jit(solution)/shard_map/ppermute | solution.py:365
  14.7 4.1 %collective-permute-start.3 = (bf16[112,128]{1,0:T(8,128)(2,1)S(1)}, bf16[112,128]{1,0:T(8,128)(2,1)S(1)}, u32[]{:S(2)}, u32[]{:S(2)}) collective-permute-start(bf16[112,128]{1,0:T(8,128)(2,1)S(1)} %get-tuple-element.49), channel_id=1, source_target_pairs={{0,1},{1,0},{2,3},{3,2},{4,5},{5,4},{6,7},{7,6},{8,9},{9,8},{10,11... | collective-permute-start | bytes 86024 | tf_op jit(solution)/shard_map/ppermute | solution.py:366
  19.5 4.9 %collective-permute-start.8 = (bf16[144,128]{1,0:T(8,128)(2,1)S(1)}, bf16[144,128]{1,0:T(8,128)(2,1)S(1)}, u32[]{:S(2)}, u32[]{:S(2)}) collective-permute-start(bf16[144,128]{1,0:T(8,128)(2,1)S(1)} %get-tuple-element.56), channel_id=1, source_target_pairs={{0,8},{1,9},{2,10},{3,11},{4,12},{5,13},{6,14},{7,15},{8,0},{9,1},... | collective-permute-start | bytes 110600 | tf_op jit(solution)/shard_map/ppermute | solution.py:364
  20.6 12.2 %collective-permute-start.7 = (bf16[112,128]{1,0:T(8,128)(2,1)S(1)}, bf16[112,128]{1,0:T(8,128)(2,1)S(1)}, u32[]{:S(2)}, u32[]{:S(2)}) collective-permute-start(bf16[112,128]{1,0:T(8,128)(2,1)S(1)} %get-tuple-element.55), channel_id=1, source_target_pairs={{0,15},{1,2},{2,1},{3,4},{4,3},{5,6},{6,5},{7,8},{8,7},{9,10},{10,... | collective-permute-start | bytes 86024 | tf_op jit(solution)/shard_map/ppermute | solution.py:365
  21.6 11.3 %collective-permute-start.6 = (bf16[112,128]{1,0:T(8,128)(2,1)S(1)}, bf16[112,128]{1,0:T(8,128)(2,1)S(1)}, u32[]{:S(2)}, u32[]{:S(2)}) collective-permute-start(bf16[112,128]{1,0:T(8,128)(2,1)S(1)} %get-tuple-element.55), channel_id=1, source_target_pairs={{0,1},{1,0},{2,3},{3,2},{4,5},{5,4},{6,7},{7,6},{8,9},{9,8},{10,11... | collective-permute-start | bytes 86024 | tf_op jit(solution)/shard_map/ppermute | solution.py:366
  24.4 3.6 %collective-permute-start.9 = (f32[4,256]{1,0:T(4,128)S(1)}, f32[4,256]{1,0:T(4,128)S(1)}, u32[]{:S(2)}, u32[]{:S(2)}) collective-permute-start(f32[4,256]{1,0:T(4,128)S(1)} %get-tuple-element.62), channel_id=1, source_target_pairs={{0,4},{1,5},{2,6},{3,7},{4,0},{5,1},{6,2},{7,3},{8,12},{9,13},{10,... | collective-permute-start | bytes 12296 | tf_op jit(solution)/shard_map/ppermute | solution.py:469
  28.1 3.6 %collective-permute-start.10 = (f32[2,256]{1,0:T(2,128)S(1)}, f32[2,256]{1,0:T(2,128)S(1)}, u32[]{:S(2)}, u32[]{:S(2)}) collective-permute-start(f32[2,256]{1,0:T(2,128)S(1)} %get-tuple-element.64), channel_id=1, source_target_pairs={{0,2},{1,3},{2,0},{3,1},{4,6},{5,7},{6,4},{7,5},{8,10},{9,11},{10,... | collective-permute-start | bytes 6152 | tf_op jit(solution)/shard_map/ppermute | solution.py:469
  31.7 2.6 %collective-permute-start.11 = (f32[1,256]{1,0:T(1,128)S(1)}, f32[1,256]{1,0:T(1,128)S(1)}, u32[]{:S(2)}, u32[]{:S(2)}) collective-permute-start(f32[1,256]{1,0:T(1,128)S(1)} %get-tuple-element.66), channel_id=1, source_target_pairs={{0,1},{1,0},{2,3},{3,2},{4,5},{5,4},{6,7},{7,6},{8,9},{9,8},{10,11... | collective-permute-start | bytes 3080 | tf_op jit(solution)/shard_map/ppermute | solution.py:469

commit v4 on v3

--- a/solution.py
+++ b/solution.py
@@ -222,7 +222,7 @@
 
 
 def route_kernel(packed, *refs):
-    kept_ref, arrived_ref, keep_ref, send_ref = refs
+    kept_ref, arrived_ref, keep_ref, *send_refs = refs
     rows = kept_ref[...]
     if packed:
         count, width = rows.shape
@@ -236,11 +236,19 @@
         rows = rows + (high + low)
     else:
         rows = rows + arrived_ref[...]
-    keep_ref[...], send_ref[...] = halves(rows)
-
-
-def flux_kernel(kept_ref, arrived_ref, flux_ref):
-    flux = kept_ref[...] + arrived_ref[...]
+    mine, other = halves(rows)
+    if len(send_refs) == 1:
+        keep_ref[...], send_refs[0][...] = mine, other
+    else:
+        keep_ref[...], send_refs[0][...] = halves(mine)
+        send_refs[1][...], send_refs[2][...] = halves(other)
+
+
+def flux_kernel(*refs):
+    *part_refs, flux_ref = refs
+    flux = part_refs[0][...]
+    for ref in part_refs[1:]:
+        flux = flux + ref[...]
     flux_ref[...] = flux[:, : flux_ref.shape[1]]
 
 
@@ -457,18 +465,21 @@
             across_send = send
     arrived, half = ghosts[2], tile_count // 2
     while half > 1:
-        half //= 2
+        packed = 2 * half == tile_count
+        step = 4 if half == 4 else 2
+        half //= step
         piece = pltpu.VMEM((half, width), F32)
-        kept, leaving = call(
-            functools.partial(route_kernel, 2 * half == tile_count // 2),
-            [piece, piece],
-            [],
-            [kept, arrived],
+        kept, *leaving = call(
+            functools.partial(route_kernel, packed), [piece] * step, [], [kept, arrived]
         )
-        partners = [(d, d ^ half) for d in range(tile_count)]
-        arrived = lax.ppermute(leaving, "tile", partners)
+        pieces = []
+        for place, value in enumerate(leaving, 1):
+            away = place * half
+            partners = [(d, d ^ away) for d in range(tile_count)]
+            pieces.append(lax.ppermute(value, "tile", partners))
+        arrived = pieces[0]
     (flux,) = call(
-        flux_kernel, [jax.ShapeDtypeStruct((1, tile_count * slots), F32)], [], [kept, arrived]
+        flux_kernel, [jax.ShapeDtypeStruct((1, tile_count * slots), F32)], [], [kept, *pieces]
     )
     return state_out.transpose(1, 0, 2), tangent_out.transpose(1, 0, 2), flux.reshape(-1)
 

time: 35.1 us -> 33.3 us (0.949)
  waiting for transfers between devices: 16.4 us -> 12.8 us
  starting transfers between devices: 10 us -> 11.8 us
    ppermute x3 -> x4, waiting for transfers between devices: 7.17 us -> 3.61 us  [on_device(): pieces.append(lax.ppermute(value, 'tile', partners))]
    ppermute x3 -> x4, starting transfers between devices: 0.13 us -> 1.91 us  [on_device(): pieces.append(lax.ppermute(value, 'tile', partners))]
    pallas_call x11 -> x10, Pallas kernels: 7.77 us -> 7.77 us  [call(): pl.pallas_call(body, out_shape=outputs, in_specs=[pl.BlockSpec(memory_spa...]
  transfers between devices with their start and end apart: 12 -> 13, of which waited for: 6 -> 5; matrix products, arithmetic and copies ran while one was open for 0% -> 0% of each run, Pallas kernels for 13% -> 14%
where the time goes in v4:
time: 33.3 us; the launch traced here: 33.1 us
  waiting for transfers between devices  12.8 us (38%)
  starting transfers between devices  11.8 us (35%)
  Pallas kernels  7.77 us (23%)
  between operations  0.78 us (2%)
    pallas_call x10, Pallas kernels, call(): pl.pallas_call(body, out_shape=outputs, in_specs=[pl.BlockSpec(memory_spa...  7.77 us
    ppermute x3, starting transfers between devices, exchange(): across = lax.ppermute(across_value, 'tile', opposite)  5.34 us
    ppermute x3, waiting for transfers between devices, exchange(): across = lax.ppermute(across_value, 'tile', opposite)  4.62 us
    ppermute x3, waiting for transfers between devices, exchange(): other = lax.ppermute(value, 'tile', next_chip)  4.56 us
    ppermute x3, starting transfers between devices, exchange(): other = lax.ppermute(value, 'tile', next_chip)  4.38 us
    ppermute x4, waiting for transfers between devices, on_device(): pieces.append(lax.ppermute(value, 'tile', partners))  3.61 us
    ppermute x4, starting transfers between devices, on_device(): pieces.append(lax.ppermute(value, 'tile', partners))  1.91 us
  transfers between devices with their start and end apart: 13, of which 5 were waited for; matrix products, arithmetic and copies ran while one was open for 0% of the time, Pallas kernels for 14%

profile of v4, /device:TPU:0, one launch (start us, length us, event | category | flops | bytes accessed | tf_op | source)
XLA Modules:
  0.0 33.1 jit_solution(8906581596742268953)
XLA Ops:
  0.6 0.0 copy-start
  0.6 0.0 copy-start.1
  0.7 1.1 %shard_map.112 = (f32[104,128]{1,0:T(8,128)S(1)}, f32[96,128]{1,0:T(8,128)S(1)}, bf16[112,128]{1,0:T(8,128)(2,1)S(1)}, s32[1,128]{1,0:T(1,128)S(1)}, f32[1,128]{...) custom-call(f32[50,2,128]{2,1,0:T(2,128)} %bitcast.10, f32[50,2,128]{2,1,0:T(2,128)} %bitcast.11, ...), custom_call_target="tpu_custom_call" | custom-call | flops 10000000000 | bytes 100000 | tf_op jit(solution)/shard_map/pallas_call | solution.py:335
  1.8 4.1 %collective-permute-start.2 = (bf16[112,128]{1,0:T(8,128)(2,1)S(1)}, bf16[112,128]{1,0:T(8,128)(2,1)S(1)}, u32[]{:S(2)}, u32[]{:S(2)}) collective-permute-start(bf16[112,128]{1,0:T(8,128)(2,1)S(1)} %get-tuple-element.42), channel_id=1, source_target_pairs={{0,8},{1,9},{2,10},{3,11},{4,12},{5,13},{6,14},{7,15},{8,0},{9,1},... | collective-permute-start | bytes 86024 | tf_op jit(solution)/shard_map/ppermute | solution.py:372
  5.9 1.5 %collective-permute-start.1 = (bf16[112,128]{1,0:T(8,128)(2,1)S(1)}, bf16[112,128]{1,0:T(8,128)(2,1)S(1)}, u32[]{:S(2)}, u32[]{:S(2)}) collective-permute-start(bf16[112,128]{1,0:T(8,128)(2,1)S(1)} %get-tuple-element.42), channel_id=1, source_target_pairs={{0,15},{1,2},{2,1},{3,4},{4,3},{5,6},{6,5},{7,8},{8,7},{9,10},{10,... | collective-permute-start | bytes 86024 | tf_op jit(solution)/shard_map/ppermute | solution.py:373
  7.4 0.1 collective-permute-start
  7.5 0.0 copy-done
  7.6 0.0 copy-done.1
  7.6 1.1 %shard_map.113 = (f32[208,128]{1,0:T(8,128)S(1)}, f32[96,128]{1,0:T(8,128)S(1)}, f32[1,128]{1,0:T(1,128)S(1)}, f32[208,128]{1,0:T(8,128)S(1)}, s32[6,128]{1,0:T(8,128)S(1)}) custom-call(f32[104,128]{1,0:T(8,128)S(1)} %get-tuple-element.35.refs_0_, f32[96,128]{1,0:T(8,128)S(1)} %get-tuple-element.36.refs_1_, s32[1,128]{1,0:T(1,128)S(1)} %get-tuple-element.37.refs_2_.refs_5_, ...), custom_call_target="tpu_custom_call" | custom-call | flops 4000000 | bytes 100000 | tf_op jit(solution)/shard_map/pallas_call | solution.py:335
  8.6 0.0 collective-permute-done.2.refs_3_
  8.6 3.3 %collective-permute-done.1.refs_2_ = bf16[112,128]{1,0:T(8,128)(2,1)S(1)} collective-permute-done((bf16[112,128]{1,0:T(8,128)(2,1)S(1)}, bf16[112,128]{1,0:T(8,128)(2,1)S(1)}, u32[]{:S(2)}, u32[]{:S(2)}) %collective-permute-start.1) | collective-permute-done | bytes 28704 | tf_op jit(solution)/shard_map/ppermute | solution.py:373
  11.9 0.0 collective-permute-done.refs_1_
  11.9 0.7 %shard_map.114 = (f32[104,128]{1,0:T(8,128)S(1)}, bf16[112,128]{1,0:T(8,128)(2,1)S(1)}) custom-call(f32[208,128]{1,0:T(8,128)S(1)} %get-tuple-element.41.refs_0_, bf16[112,128]{1,0:T(8,128)(2,1)S(1)} %collective-permute-done.refs_1_, bf16[112,128]{1,0:T(8,128)(2,1)S(1)} %collective-permute-done.1.refs_2_, ...), custom_call_target="tpu_custom_call" | custom-call | flops 1000000 | bytes 100000 | tf_op jit(solution)/shard_map/pallas_call | solution.py:335
  12.6 0.1 collective-permute-start.5
  12.7 2.0 %collective-permute-start.4 = (bf16[112,128]{1,0:T(8,128)(2,1)S(1)}, bf16[112,128]{1,0:T(8,128)(2,1)S(1)}, u32[]{:S(2)}, u32[]{:S(2)}) collective-permute-start(bf16[112,128]{1,0:T(8,128)(2,1)S(1)} %get-tuple-element.49), channel_id=1, source_target_pairs={{0,15},{1,2},{2,1},{3,4},{4,3},{5,6},{6,5},{7,8},{8,7},{9,10},{10,... | collective-permute-start | bytes 86024 | tf_op jit(solution)/shard_map/ppermute | solution.py:373
  14.7 0.0 collective-permute-start.3
  14.7 1.1 %shard_map.115 = (f32[208,128]{1,0:T(8,128)S(1)}, f32[96,128]{1,0:T(8,128)S(1)}, f32[1,128]{1,0:T(1,128)S(1)}) custom-call(f32[104,128]{1,0:T(8,128)S(1)} %get-tuple-element.44.refs_0_, f32[96,128]{1,0:T(8,128)S(1)} %get-tuple-element.45.refs_1_, s32[1,128]{1,0:T(1,128)S(1)} %get-tuple-element.37.refs_2_.refs_5_, ...), custom_call_target="tpu_custom_call" | custom-call | flops 4000000 | bytes 100000 | tf_op jit(solution)/shard_map/pallas_call | solution.py:335
  15.7 1.7 %collective-permute-done.5.refs_3_ = bf16[112,128]{1,0:T(8,128)(2,1)S(1)} collective-permute-done((bf16[112,128]{1,0:T(8,128)(2,1)S(1)}, bf16[112,128]{1,0:T(8,128)(2,1)S(1)}, u32[]{:S(2)}, u32[]{:S(2)}) %collective-permute-start.5) | collective-permute-done | bytes 28704 | tf_op jit(solution)/shard_map/ppermute | solution.py:372
  17.5 1.3 %collective-permute-done.4.refs_2_ = bf16[112,128]{1,0:T(8,128)(2,1)S(1)} collective-permute-done((bf16[112,128]{1,0:T(8,128)(2,1)S(1)}, bf16[112,128]{1,0:T(8,128)(2,1)S(1)}, u32[]{:S(2)}, u32[]{:S(2)}) %collective-permute-start.4) | collective-permute-done | bytes 28704 | tf_op jit(solution)/shard_map/ppermute | solution.py:373
  18.8 0.0 collective-permute-done.3.refs_1_
  18.8 0.7 %shard_map.116 = (f32[104,128]{1,0:T(8,128)S(1)}, bf16[112,128]{1,0:T(8,128)(2,1)S(1)}, bf16[144,128]{1,0:T(8,128)(2,1)S(1)}, f32[8,256]{1,0:T(8,128)S(1)}) custom-call(f32[208,128]{1,0:T(8,128)S(1)} %get-tuple-element.48.refs_0_, bf16[112,128]{1,0:T(8,128)(2,1)S(1)} %collective-permute-done.3.refs_1_, bf16[112,128]{1,0:T(8,128)(2,1)S(1)} %collective-permute-done.4.refs_2_, ...), custom_call_target="tpu_custom_call" | custom-call | flops 1000000 | bytes 100000 | tf_op jit(solution)/shard_map/pallas_call | solution.py:335
  19.5 1.1 %collective-permute-start.8 = (bf16[144,128]{1,0:T(8,128)(2,1)S(1)}, bf16[144,128]{1,0:T(8,128)(2,1)S(1)}, u32[]{:S(2)}, u32[]{:S(2)}) collective-permute-start(bf16[144,128]{1,0:T(8,128)(2,1)S(1)} %get-tuple-element.56), channel_id=1, source_target_pairs={{0,8},{1,9},{2,10},{3,11},{4,12},{5,13},{6,14},{7,15},{8,0},{9,1},... | collective-permute-start | bytes 110600 | tf_op jit(solution)/shard_map/ppermute | solution.py:372
  20.6 0.9 %collective-permute-start.7 = (bf16[112,128]{1,0:T(8,128)(2,1)S(1)}, bf16[112,128]{1,0:T(8,128)(2,1)S(1)}, u32[]{:S(2)}, u32[]{:S(2)}) collective-permute-start(bf16[112,128]{1,0:T(8,128)(2,1)S(1)} %get-tuple-element.55), channel_id=1, source_target_pairs={{0,15},{1,2},{2,1},{3,4},{4,3},{5,6},{6,5},{7,8},{8,7},{9,10},{10,... | collective-permute-start | bytes 86024 | tf_op jit(solution)/shard_map/ppermute | solution.py:373
  21.6 0.0 collective-permute-start.6
  21.6 2.9 %collective-permute-done.8.refs_3_.refs_1_ = bf16[144,128]{1,0:T(8,128)(2,1)S(1)} collective-permute-done((bf16[144,128]{1,0:T(8,128)(2,1)S(1)}, bf16[144,128]{1,0:T(8,128)(2,1)S(1)}, u32[]{:S(2)}, u32[]{:S(2)}) %collective-permute-start.8) | collective-permute-done | bytes 36896 | tf_op jit(solution)/shard_map/ppermute | solution.py:372
  24.4 0.0 collective-permute-start.9
  24.4 3.6 %collective-permute-done.9.refs_1_ = f32[4,256]{1,0:T(4,128)S(1)} collective-permute-done((f32[4,256]{1,0:T(4,128)S(1)}, f32[4,256]{1,0:T(4,128)S(1)}, u32[]{:S(2)}, u32[]{:S(2)}) %collective-permute-start.9) | collective-permute-done | bytes 4128 | tf_op jit(solution)/shard_map/ppermute | solution.py:479
  28.1 0.1 collective-permute-start.10
  28.1 0.1 collective-permute-start.11
  28.2 1.8 %collective-permute-start.12 = (f32[1,256]{1,0:T(1,128)S(1)}, f32[1,256]{1,0:T(1,128)S(1)}, u32[]{:S(2)}, u32[]{:S(2)}) collective-permute-start(f32[1,256]{1,0:T(1,128)S(1)} %get-tuple-element.66), channel_id=1, source_target_pairs={{0,3},{1,2},{2,1},{3,0},{4,7},{5,6},{6,5},{7,4},{8,11},{9,10},{10,... | collective-permute-start | bytes 3080 | tf_op jit(solution)/shard_map/ppermute | solution.py:479
  30.0 1.1 %shard_map.117 = (f32[208,128]{1,0:T(8,128)S(1)}, f32[96,128]{1,0:T(8,128)S(1)}) custom-call(f32[104,128]{1,0:T(8,128)S(1)} %get-tuple-element.52.refs_0_, f32[96,128]{1,0:T(8,128)S(1)} %get-tuple-element.53.refs_1_, s32[1,128]{1,0:T(1,128)S(1)} %get-tuple-element.37.refs_2_.refs_5_, f32[1,128]{1,0:T(1,128)S(1)} %get-tuple-element.38.refs_3_.refs_8_, ...), custom_call_target="tpu_custom_call" | custom-call | flops 4000000 | bytes 100000 | tf_op jit(solution)/shard_map/pallas_call | solution.py:335
  31.0 0.0 collective-permute-done.7.refs_2_
  31.1 0.0 collective-permute-done.6.refs_1_
  31.1 1.5 %shard_map.118 = (f32[50,2,128]{2,1,0:T(2,128)}, f32[50,2,128]{2,1,0:T(2,128)}) custom-call(f32[208,128]{1,0:T(8,128)S(1)} %get-tuple-element.54.refs_0_, bf16[112,128]{1,0:T(8,128)(2,1)S(1)} %collective-permute-done.6.refs_1_, bf16[112,128]{1,0:T(8,128)(2,1)S(1)} %collective-permute-done.7.refs_2_, ...), custom_call_target="tpu_custom_call" | custom-call | flops 2000000 | bytes 100000 | tf_op jit(solution)/shard_map/pallas_call | solution.py:335
  32.6 0.0 collective-permute-done.10.refs_1_
  32.6 0.0 collective-permute-done.11.refs_2_
  32.6 0.0 collective-permute-done.12.refs_3_
  32.6 0.6 %shard_map.121 = f32[1,192]{1,0:T(1,128)} custom-call(f32[1,256]{1,0:T(1,128)S(1)} %get-tuple-element.63.refs_0_, f32[1,256]{1,0:T(1,128)S(1)} %collective-permute-done.10.refs_1_, f32[1,256]{1,0:T(1,128)S(1)} %collective-permute-done.11.refs_2_, f32[1,256]{1,0:T(1,128)S(1)} %collective-permute-done.12.refs_3_), custom_call_target="tpu_custom_call" | custom-call | flops 1000000 | bytes 100000 | tf_op jit(solution)/shard_map/pallas_call | solution.py:335
  (2 shorter events, 0.0 us)
Async XLA Ops:
  0.6 6.9 %copy-start = (bf16[50,6,128,128]{3,2,1,0:T(8,128)(2,1)S(1)}, bf16[50,6,128,128]{3,2,1,0:T(8,128)(2,1)}, u32[]{:S(2)}) copy-start(bf16[50,6,128,128]{3,2,1,0:T(8,128)(2,1)} %refs_6_.13) | copy-start | bytes 29491204
  0.6 6.9 %copy-start.1 = (bf16[50,3,128,128]{3,2,1,0:T(8,128)(2,1)S(1)}, bf16[50,3,128,128]{3,2,1,0:T(8,128)(2,1)}, u32[]{:S(2)}) copy-start(bf16[50,3,128,128]{3,2,1,0:T(8,128)(2,1)} %refs_7_.7) | copy-start | bytes 14745604
  1.8 6.8 %collective-permute-start.2 = (bf16[112,128]{1,0:T(8,128)(2,1)S(1)}, bf16[112,128]{1,0:T(8,128)(2,1)S(1)}, u32[]{:S(2)}, u32[]{:S(2)}) collective-permute-start(bf16[112,128]{1,0:T(8,128)(2,1)S(1)} %get-tuple-element.42), channel_id=1, source_target_pairs={{0,8},{1,9},{2,10},{3,11},{4,12},{5,13},{6,14},{7,15},{8,0},{9,1},... | collective-permute-start | bytes 86024 | tf_op jit(solution)/shard_map/ppermute | solution.py:372
  5.9 6.0 %collective-permute-start.1 = (bf16[112,128]{1,0:T(8,128)(2,1)S(1)}, bf16[112,128]{1,0:T(8,128)(2,1)S(1)}, u32[]{:S(2)}, u32[]{:S(2)}) collective-permute-start(bf16[112,128]{1,0:T(8,128)(2,1)S(1)} %get-tuple-element.42), channel_id=1, source_target_pairs={{0,15},{1,2},{2,1},{3,4},{4,3},{5,6},{6,5},{7,8},{8,7},{9,10},{10,... | collective-permute-start | bytes 86024 | tf_op jit(solution)/shard_map/ppermute | solution.py:373
  7.4 4.5 %collective-permute-start = (bf16[112,128]{1,0:T(8,128)(2,1)S(1)}, bf16[112,128]{1,0:T(8,128)(2,1)S(1)}, u32[]{:S(2)}, u32[]{:S(2)}) collective-permute-start(bf16[112,128]{1,0:T(8,128)(2,1)S(1)} %get-tuple-element.42), channel_id=1, source_target_pairs={{0,1},{1,0},{2,3},{3,2},{4,5},{5,4},{6,7},{7,6},{8,9},{9,8},{10,11... | collective-permute-start | bytes 86024 | tf_op jit(solution)/shard_map/ppermute | solution.py:374
  12.6 4.9 %collective-permute-start.5 = (bf16[112,128]{1,0:T(8,128)(2,1)S(1)}, bf16[112,128]{1,0:T(8,128)(2,1)S(1)}, u32[]{:S(2)}, u32[]{:S(2)}) collective-permute-start(bf16[112,128]{1,0:T(8,128)(2,1)S(1)} %get-tuple-element.49), channel_id=1, source_target_pairs={{0,8},{1,9},{2,10},{3,11},{4,12},{5,13},{6,14},{7,15},{8,0},{9,1},... | collective-permute-start | bytes 86024 | tf_op jit(solution)/shard_map/ppermute | solution.py:372
  12.7 6.1 %collective-permute-start.4 = (bf16[112,128]{1,0:T(8,128)(2,1)S(1)}, bf16[112,128]{1,0:T(8,128)(2,1)S(1)}, u32[]{:S(2)}, u32[]{:S(2)}) collective-permute-start(bf16[112,128]{1,0:T(8,128)(2,1)S(1)} %get-tuple-element.49), channel_id=1, source_target_pairs={{0,15},{1,2},{2,1},{3,4},{4,3},{5,6},{6,5},{7,8},{8,7},{9,10},{10,... | collective-permute-start | bytes 86024 | tf_op jit(solution)/shard_map/ppermute | solution.py:373
  14.7 4.1 %collective-permute-start.3 = (bf16[112,128]{1,0:T(8,128)(2,1)S(1)}, bf16[112,128]{1,0:T(8,128)(2,1)S(1)}, u32[]{:S(2)}, u32[]{:S(2)}) collective-permute-start(bf16[112,128]{1,0:T(8,128)(2,1)S(1)} %get-tuple-element.49), channel_id=1, source_target_pairs={{0,1},{1,0},{2,3},{3,2},{4,5},{5,4},{6,7},{7,6},{8,9},{9,8},{10,11... | collective-permute-start | bytes 86024 | tf_op jit(solution)/shard_map/ppermute | solution.py:374
  19.5 4.9 %collective-permute-start.8 = (bf16[144,128]{1,0:T(8,128)(2,1)S(1)}, bf16[144,128]{1,0:T(8,128)(2,1)S(1)}, u32[]{:S(2)}, u32[]{:S(2)}) collective-permute-start(bf16[144,128]{1,0:T(8,128)(2,1)S(1)} %get-tuple-element.56), channel_id=1, source_target_pairs={{0,8},{1,9},{2,10},{3,11},{4,12},{5,13},{6,14},{7,15},{8,0},{9,1},... | collective-permute-start | bytes 110600 | tf_op jit(solution)/shard_map/ppermute | solution.py:372
  20.6 10.4 %collective-permute-start.7 = (bf16[112,128]{1,0:T(8,128)(2,1)S(1)}, bf16[112,128]{1,0:T(8,128)(2,1)S(1)}, u32[]{:S(2)}, u32[]{:S(2)}) collective-permute-start(bf16[112,128]{1,0:T(8,128)(2,1)S(1)} %get-tuple-element.55), channel_id=1, source_target_pairs={{0,15},{1,2},{2,1},{3,4},{4,3},{5,6},{6,5},{7,8},{8,7},{9,10},{10,... | collective-permute-start | bytes 86024 | tf_op jit(solution)/shard_map/ppermute | solution.py:373
  21.6 9.5 %collective-permute-start.6 = (bf16[112,128]{1,0:T(8,128)(2,1)S(1)}, bf16[112,128]{1,0:T(8,128)(2,1)S(1)}, u32[]{:S(2)}, u32[]{:S(2)}) collective-permute-start(bf16[112,128]{1,0:T(8,128)(2,1)S(1)} %get-tuple-element.55), channel_id=1, source_target_pairs={{0,1},{1,0},{2,3},{3,2},{4,5},{5,4},{6,7},{7,6},{8,9},{9,8},{10,11... | collective-permute-start | bytes 86024 | tf_op jit(solution)/shard_map/ppermute | solution.py:374
  24.4 3.6 %collective-permute-start.9 = (f32[4,256]{1,0:T(4,128)S(1)}, f32[4,256]{1,0:T(4,128)S(1)}, u32[]{:S(2)}, u32[]{:S(2)}) collective-permute-start(f32[4,256]{1,0:T(4,128)S(1)} %get-tuple-element.62), channel_id=1, source_target_pairs={{0,4},{1,5},{2,6},{3,7},{4,0},{5,1},{6,2},{7,3},{8,12},{9,13},{10,... | collective-permute-start | bytes 12296 | tf_op jit(solution)/shard_map/ppermute | solution.py:479
  28.1 4.5 %collective-permute-start.10 = (f32[1,256]{1,0:T(1,128)S(1)}, f32[1,256]{1,0:T(1,128)S(1)}, u32[]{:S(2)}, u32[]{:S(2)}) collective-permute-start(f32[1,256]{1,0:T(1,128)S(1)} %get-tuple-element.64), channel_id=1, source_target_pairs={{0,1},{1,0},{2,3},{3,2},{4,5},{5,4},{6,7},{7,6},{8,9},{9,8},{10,11... | collective-permute-start | bytes 3080 | tf_op jit(solution)/shard_map/ppermute | solution.py:479
  28.1 4.4 %collective-permute-start.11 = (f32[1,256]{1,0:T(1,128)S(1)}, f32[1,256]{1,0:T(1,128)S(1)}, u32[]{:S(2)}, u32[]{:S(2)}) collective-permute-start(f32[1,256]{1,0:T(1,128)S(1)} %get-tuple-element.65), channel_id=1, source_target_pairs={{0,2},{1,3},{2,0},{3,1},{4,6},{5,7},{6,4},{7,5},{8,10},{9,11},{10,... | collective-permute-start | bytes 3080 | tf_op jit(solution)/shard_map/ppermute | solution.py:479
  28.2 4.3 %collective-permute-start.12 = (f32[1,256]{1,0:T(1,128)S(1)}, f32[1,256]{1,0:T(1,128)S(1)}, u32[]{:S(2)}, u32[]{:S(2)}) collective-permute-start(f32[1,256]{1,0:T(1,128)S(1)} %get-tuple-element.66), channel_id=1, source_target_pairs={{0,3},{1,2},{2,1},{3,0},{4,7},{5,6},{6,5},{7,4},{8,11},{9,10},{10,... | collective-permute-start | bytes 3080 | tf_op jit(solution)/shard_map/ppermute | solution.py:479

commit v5 on v4

--- a/solution.py
+++ b/solution.py
@@ -221,27 +221,43 @@
     return jnp.where(upper, second, first), jnp.where(upper, first, second)
 
 
-def route_kernel(packed, *refs):
-    kept_ref, arrived_ref, keep_ref, *send_refs = refs
+def quarters(rows):
+    mine, other = halves(rows)
+    return (*halves(mine), *halves(other))
+
+
+def pack(rows):
+    high = rows.astype(BF16).astype(F32)
+    return jnp.concatenate(
+        [
+            part[:, start : start + 128]
+            for part in (high, rows - high)
+            for start in range(0, rows.shape[1], 128)
+        ],
+        axis=0,
+    )
+
+
+def unpack(packed, count, width):
+    blocks = width // 128
+    parts = [packed[count * k : count * (k + 1)] for k in range(2 * blocks)]
+    high = jnp.concatenate(parts[:blocks], axis=1)
+    return high + jnp.concatenate(parts[blocks:], axis=1)
+
+
+def route_kernel(arrivals, first, *refs):
+    kept_ref, *arrived_refs = refs[: 1 + arrivals]
+    out_refs = refs[1 + arrivals :]
     rows = kept_ref[...]
-    if packed:
-        count, width = rows.shape
-        base = arrived_ref.shape[0] - 2 * count * (width // 128)
-        parts = [
-            arrived_ref[base + count * k : base + count * (k + 1), :].astype(F32)
-            for k in range(2 * (width // 128))
-        ]
-        high = jnp.concatenate(parts[: width // 128], axis=1)
-        low = jnp.concatenate(parts[width // 128 :], axis=1)
-        rows = rows + (high + low)
-    else:
-        rows = rows + arrived_ref[...]
-    mine, other = halves(rows)
-    if len(send_refs) == 1:
-        keep_ref[...], send_refs[0][...] = mine, other
-    else:
-        keep_ref[...], send_refs[0][...] = halves(mine)
-        send_refs[1][...], send_refs[2][...] = halves(other)
+    count, width = rows.shape
+    if first:
+        packed = arrived_refs.pop()
+        start = packed.shape[0] - 2 * count * (width // 128)
+        rows = rows + unpack(packed[start:, :].astype(F32), count, width)
+    for ref in arrived_refs:
+        rows = rows + ref[...]
+    for ref, part in zip(out_refs, quarters(rows) if len(out_refs) == 4 else halves(rows)):
+        ref[...] = part
 
 
 def flux_kernel(*refs):
@@ -257,7 +273,8 @@
     if stage == "last":
         high_ref, state_ref, tangent_ref, middle_ref, fields_ref = refs[8:]
     elif stage == "export":
-        light_ref, total_ref, slots_ref, low_ref, send_ref, across_out_ref, keep_ref, middle_ref = refs[8:]
+        light_ref, total_ref, slots_ref, low_ref, send_ref, across_out_ref = refs[8:14]
+        keep_ref, near_ref, far_ref, middle_ref = refs[14:]
     else:
         low_ref, send_ref, middle_ref = refs[8:]
     columns = size.columns
@@ -311,15 +328,8 @@
         uptake, _ = uptake_of(low_ref, 0, wet, light_ref[...], columns)
         total = total_ref[...] + (1.0 - dop_fraction) * jnp.sum(uptake, axis=0, keepdims=True)
         placed = place_slots(total, slots_ref, slots, keep_ref.shape[1])
-        keep_ref[...], leaving = halves(placed)
-        width = leaving.shape[1]
-        high = leaving.astype(BF16).astype(F32)
-        parts = [
-            part[:, start : start + 128]
-            for part in (high, leaving - high)
-            for start in range(0, width, 128)
-        ]
-        across_out_ref[size.send_rows :, :] = jnp.concatenate(parts, axis=0).astype(BF16)
+        keep_ref[...], near_ref[...], leaving, far_ref[...] = quarters(placed)
+        across_out_ref[size.send_rows :, :] = pack(leaving).astype(BF16)
 
 
 def in_vmem(value):
@@ -373,6 +383,10 @@
         other = lax.ppermute(value, "tile", next_chip)
         pair = lax.ppermute(value, "tile", same_chip)
         return pair, other, across
+
+    def hop(value, away):
+        partners = [(d, d ^ away) for d in range(tile_count)]
+        return lax.ppermute(value, "tile", partners)
 
     def shape(rows, dtype=F32):
         return pltpu.VMEM((rows, columns), dtype)
@@ -447,14 +461,15 @@
                 2000000,
             )
         elif time_index == STEPS - 2:
-            half = tile_count // 2
-            packed_rows = size.send_rows + 2 * half * (width // 128)
-            low, send, across_send, kept = call(
+            quarter = tile_count // 4
+            packed_rows = size.send_rows + 2 * quarter * (width // 128)
+            low, send, across_send, kept, near, far = call(
                 functools.partial(ghost_kernel, size, "export", slots),
-                sends + [shape(packed_rows, BF16), pltpu.VMEM((half, width), F32)],
+                sends + [shape(packed_rows, BF16)] + [pltpu.VMEM((quarter, width), F32)] * 3,
                 [low_scratch],
                 operands + [light, total, slot_rows],
             )
+            hops = [hop(near, quarter), hop(far, 3 * quarter)]
         else:
             low, send = call(
                 functools.partial(ghost_kernel, size, "middle", slots),
@@ -463,23 +478,19 @@
                 operands,
             )
             across_send = send
-    arrived, half = ghosts[2], tile_count // 2
-    while half > 1:
-        packed = 2 * half == tile_count
-        step = 4 if half == 4 else 2
-        half //= step
-        piece = pltpu.VMEM((half, width), F32)
+    arrived, rest = [*hops, ghosts[2]], tile_count // 4
+    while rest > 1:
+        step = 4 if rest >= 4 else 2
+        rest //= step
         kept, *leaving = call(
-            functools.partial(route_kernel, packed), [piece] * step, [], [kept, arrived]
+            functools.partial(route_kernel, len(arrived), 4 * step * rest == tile_count),
+            [pltpu.VMEM((rest, width), F32)] * step,
+            [],
+            [kept, *arrived],
         )
-        pieces = []
-        for place, value in enumerate(leaving, 1):
-            away = place * half
-            partners = [(d, d ^ away) for d in range(tile_count)]
-            pieces.append(lax.ppermute(value, "tile", partners))
-        arrived = pieces[0]
+        arrived = [hop(value, place * rest) for place, value in enumerate(leaving, 1)]
     (flux,) = call(
-        flux_kernel, [jax.ShapeDtypeStruct((1, tile_count * slots), F32)], [], [kept, *pieces]
+        flux_kernel, [jax.ShapeDtypeStruct((1, tile_count * slots), F32)], [], [kept, *arrived]
     )
     return state_out.transpose(1, 0, 2), tangent_out.transpose(1, 0, 2), flux.reshape(-1)
 

time: 33.3 us -> 33.9 us (1.018)
  starting transfers between devices: 11.8 us -> 16.3 us
  waiting for transfers between devices: 12.8 us -> 8.99 us
    ppermute x4 -> x5, starting transfers between devices: 1.91 us -> 6.39 us  [hop(): return lax.ppermute(value, 'tile', partners)]
    ppermute x3, waiting for transfers between devices: 4.62 us -> 1.74 us  [exchange(): across = lax.ppermute(across_value, 'tile', opposite)]
    ppermute x4 -> x5, waiting for transfers between devices: 3.61 us -> 2.67 us  [hop(): return lax.ppermute(value, 'tile', partners)]
    pallas_call x10 -> x9, Pallas kernels: 7.77 us -> 7.77 us  [call(): pl.pallas_call(body, out_shape=outputs, in_specs=[pl.BlockSpec(memory_spa...]
  transfers between devices with their start and end apart: 13 -> 14, of which waited for: 5 -> 6; matrix products, arithmetic and copies ran while one was open for 0% -> 0% of each run, Pallas kernels for 14% -> 14%
where the time goes in v5:
time: 33.9 us; the launch traced here: 33.8 us
  starting transfers between devices  16.3 us (48%)
  waiting for transfers between devices  8.99 us (27%)
  Pallas kernels  7.77 us (23%)
  between operations  0.77 us (2%)
    pallas_call x9, Pallas kernels, call(): pl.pallas_call(body, out_shape=outputs, in_specs=[pl.BlockSpec(memory_spa...  7.77 us
    ppermute x5, starting transfers between devices, hop(): return lax.ppermute(value, 'tile', partners)  6.39 us
    ppermute x3, starting transfers between devices, exchange(): across = lax.ppermute(across_value, 'tile', opposite)  5.34 us
    ppermute x3, waiting for transfers between devices, exchange(): other = lax.ppermute(value, 'tile', next_chip)  4.56 us
    ppermute x3, starting transfers between devices, exchange(): other = lax.ppermute(value, 'tile', next_chip)  4.38 us
    ppermute x5, waiting for transfers between devices, hop(): return lax.ppermute(value, 'tile', partners)  2.67 us
    ppermute x3, waiting for transfers between devices, exchange(): across = lax.ppermute(across_value, 'tile', opposite)  1.74 us
  transfers between devices with their start and end apart: 14, of which 6 were waited for; matrix products, arithmetic and copies ran while one was open for 0% of the time, Pallas kernels for 14%

profile of v5, /device:TPU:0, one launch (start us, length us, event | category | flops | bytes accessed | tf_op | source)
XLA Modules:
  0.0 33.8 jit_solution(6778564997517647508)
XLA Ops:
  0.6 0.0 copy-start
  0.6 0.0 copy-start.1
  0.7 1.1 %shard_map.112 = (f32[104,128]{1,0:T(8,128)S(1)}, f32[96,128]{1,0:T(8,128)S(1)}, bf16[112,128]{1,0:T(8,128)(2,1)S(1)}, s32[1,128]{1,0:T(1,128)S(1)}, f32[1,128]{...) custom-call(f32[50,2,128]{2,1,0:T(2,128)} %bitcast.10, f32[50,2,128]{2,1,0:T(2,128)} %bitcast.11, ...), custom_call_target="tpu_custom_call" | custom-call | flops 10000000000 | bytes 100000 | tf_op jit(solution)/shard_map/pallas_call | solution.py:345
  1.8 4.1 %collective-permute-start.2 = (bf16[112,128]{1,0:T(8,128)(2,1)S(1)}, bf16[112,128]{1,0:T(8,128)(2,1)S(1)}, u32[]{:S(2)}, u32[]{:S(2)}) collective-permute-start(bf16[112,128]{1,0:T(8,128)(2,1)S(1)} %get-tuple-element.42), channel_id=1, source_target_pairs={{0,8},{1,9},{2,10},{3,11},{4,12},{5,13},{6,14},{7,15},{8,0},{9,1},... | collective-permute-start | bytes 86024 | tf_op jit(solution)/shard_map/ppermute | solution.py:382
  5.9 1.5 %collective-permute-start.1 = (bf16[112,128]{1,0:T(8,128)(2,1)S(1)}, bf16[112,128]{1,0:T(8,128)(2,1)S(1)}, u32[]{:S(2)}, u32[]{:S(2)}) collective-permute-start(bf16[112,128]{1,0:T(8,128)(2,1)S(1)} %get-tuple-element.42), channel_id=1, source_target_pairs={{0,15},{1,2},{2,1},{3,4},{4,3},{5,6},{6,5},{7,8},{8,7},{9,10},{10,... | collective-permute-start | bytes 86024 | tf_op jit(solution)/shard_map/ppermute | solution.py:383
  7.4 0.1 collective-permute-start
  7.5 0.0 copy-done
  7.6 0.0 copy-done.1
  7.6 1.1 %shard_map.113 = (f32[208,128]{1,0:T(8,128)S(1)}, f32[96,128]{1,0:T(8,128)S(1)}, f32[1,128]{1,0:T(1,128)S(1)}, f32[208,128]{1,0:T(8,128)S(1)}, s32[6,128]{1,0:T(8,128)S(1)}) custom-call(f32[104,128]{1,0:T(8,128)S(1)} %get-tuple-element.35.refs_0_, f32[96,128]{1,0:T(8,128)S(1)} %get-tuple-element.36.refs_1_, s32[1,128]{1,0:T(1,128)S(1)} %get-tuple-element.37.refs_2_.refs_5_, ...), custom_call_target="tpu_custom_call" | custom-call | flops 4000000 | bytes 100000 | tf_op jit(solution)/shard_map/pallas_call | solution.py:345
  8.6 0.0 collective-permute-done.2.refs_3_
  8.6 3.3 %collective-permute-done.1.refs_2_ = bf16[112,128]{1,0:T(8,128)(2,1)S(1)} collective-permute-done((bf16[112,128]{1,0:T(8,128)(2,1)S(1)}, bf16[112,128]{1,0:T(8,128)(2,1)S(1)}, u32[]{:S(2)}, u32[]{:S(2)}) %collective-permute-start.1) | collective-permute-done | bytes 28704 | tf_op jit(solution)/shard_map/ppermute | solution.py:383
  11.9 0.0 collective-permute-done.refs_1_
  11.9 0.7 %shard_map.114 = (f32[104,128]{1,0:T(8,128)S(1)}, bf16[112,128]{1,0:T(8,128)(2,1)S(1)}) custom-call(f32[208,128]{1,0:T(8,128)S(1)} %get-tuple-element.41.refs_0_, bf16[112,128]{1,0:T(8,128)(2,1)S(1)} %collective-permute-done.refs_1_, bf16[112,128]{1,0:T(8,128)(2,1)S(1)} %collective-permute-done.1.refs_2_, ...), custom_call_target="tpu_custom_call" | custom-call | flops 1000000 | bytes 100000 | tf_op jit(solution)/shard_map/pallas_call | solution.py:345
  12.6 0.1 collective-permute-start.5
  12.7 2.0 %collective-permute-start.4 = (bf16[112,128]{1,0:T(8,128)(2,1)S(1)}, bf16[112,128]{1,0:T(8,128)(2,1)S(1)}, u32[]{:S(2)}, u32[]{:S(2)}) collective-permute-start(bf16[112,128]{1,0:T(8,128)(2,1)S(1)} %get-tuple-element.49), channel_id=1, source_target_pairs={{0,15},{1,2},{2,1},{3,4},{4,3},{5,6},{6,5},{7,8},{8,7},{9,10},{10,... | collective-permute-start | bytes 86024 | tf_op jit(solution)/shard_map/ppermute | solution.py:383
  14.7 0.0 collective-permute-start.3
  14.7 1.1 %shard_map.115 = (f32[208,128]{1,0:T(8,128)S(1)}, f32[96,128]{1,0:T(8,128)S(1)}, f32[1,128]{1,0:T(1,128)S(1)}) custom-call(f32[104,128]{1,0:T(8,128)S(1)} %get-tuple-element.44.refs_0_, f32[96,128]{1,0:T(8,128)S(1)} %get-tuple-element.45.refs_1_, s32[1,128]{1,0:T(1,128)S(1)} %get-tuple-element.37.refs_2_.refs_5_, ...), custom_call_target="tpu_custom_call" | custom-call | flops 4000000 | bytes 100000 | tf_op jit(solution)/shard_map/pallas_call | solution.py:345
  15.7 1.7 %collective-permute-done.5.refs_3_ = bf16[112,128]{1,0:T(8,128)(2,1)S(1)} collective-permute-done((bf16[112,128]{1,0:T(8,128)(2,1)S(1)}, bf16[112,128]{1,0:T(8,128)(2,1)S(1)}, u32[]{:S(2)}, u32[]{:S(2)}) %collective-permute-start.5) | collective-permute-done | bytes 28704 | tf_op jit(solution)/shard_map/ppermute | solution.py:382
  17.5 1.3 %collective-permute-done.4.refs_2_ = bf16[112,128]{1,0:T(8,128)(2,1)S(1)} collective-permute-done((bf16[112,128]{1,0:T(8,128)(2,1)S(1)}, bf16[112,128]{1,0:T(8,128)(2,1)S(1)}, u32[]{:S(2)}, u32[]{:S(2)}) %collective-permute-start.4) | collective-permute-done | bytes 28704 | tf_op jit(solution)/shard_map/ppermute | solution.py:383
  18.8 0.0 collective-permute-done.3.refs_1_
  18.8 0.7 %shard_map.116 = (f32[104,128]{1,0:T(8,128)S(1)}, bf16[112,128]{1,0:T(8,128)(2,1)S(1)}, bf16[128,128]{1,0:T(8,128)(2,1)S(1)}, f32[4,256]{1,0:T(4,128)S(1)}, f32[4,256]{1,0:T(4,128)S(1)}, /*index=5*/f32[4,256]{1,0:T(4,128)S(1)}) custom-call(f32[208,128]{1,0:T(8,128)S(1)} %get-tuple-element.48.refs_0_, bf16[112,128]{1,0:T(8,128)(2,1)S(1)} %collective-permute-done.3.refs_1_, ...), custom_call_target="tpu_custom_call" | custom-call | flops 1000000 | bytes 100000 | tf_op jit(solution)/shard_map/pallas_call | solution.py:345
  19.5 1.1 %collective-permute-start.8 = (bf16[128,128]{1,0:T(8,128)(2,1)S(1)}, bf16[128,128]{1,0:T(8,128)(2,1)S(1)}, u32[]{:S(2)}, u32[]{:S(2)}) collective-permute-start(bf16[128,128]{1,0:T(8,128)(2,1)S(1)} %get-tuple-element.56), channel_id=1, source_target_pairs={{0,8},{1,9},{2,10},{3,11},{4,12},{5,13},{6,14},{7,15},{8,0},{9,1},... | collective-permute-start | bytes 98312 | tf_op jit(solution)/shard_map/ppermute | solution.py:382
  20.6 0.9 %collective-permute-start.7 = (bf16[112,128]{1,0:T(8,128)(2,1)S(1)}, bf16[112,128]{1,0:T(8,128)(2,1)S(1)}, u32[]{:S(2)}, u32[]{:S(2)}) collective-permute-start(bf16[112,128]{1,0:T(8,128)(2,1)S(1)} %get-tuple-element.55), channel_id=1, source_target_pairs={{0,15},{1,2},{2,1},{3,4},{4,3},{5,6},{6,5},{7,8},{8,7},{9,10},{10,... | collective-permute-start | bytes 86024 | tf_op jit(solution)/shard_map/ppermute | solution.py:383
  21.6 0.0 collective-permute-start.6
  21.6 0.0 collective-permute-start.9
  21.6 3.1 %collective-permute-start.10 = (f32[4,256]{1,0:T(4,128)S(1)}, f32[4,256]{1,0:T(4,128)S(1)}, u32[]{:S(2)}, u32[]{:S(2)}) collective-permute-start(f32[4,256]{1,0:T(4,128)S(1)} %get-tuple-element.62), channel_id=1, source_target_pairs={{0,12},{1,13},{2,14},{3,15},{4,8},{5,9},{6,10},{7,11},{8,4},{9,5},... | collective-permute-start | bytes 12296 | tf_op jit(solution)/shard_map/ppermute | solution.py:389
  24.7 0.5 %collective-permute-done.9.refs_1_ = f32[4,256]{1,0:T(4,128)S(1)} collective-permute-done((f32[4,256]{1,0:T(4,128)S(1)}, f32[4,256]{1,0:T(4,128)S(1)}, u32[]{:S(2)}, u32[]{:S(2)}) %collective-permute-start.9) | collective-permute-done | bytes 4128 | tf_op jit(solution)/shard_map/ppermute | solution.py:389
  25.2 1.8 %collective-permute-done.10.refs_2_ = f32[4,256]{1,0:T(4,128)S(1)} collective-permute-done((f32[4,256]{1,0:T(4,128)S(1)}, f32[4,256]{1,0:T(4,128)S(1)}, u32[]{:S(2)}, u32[]{:S(2)}) %collective-permute-start.10) | collective-permute-done | bytes 4128 | tf_op jit(solution)/shard_map/ppermute | solution.py:389
  27.0 0.0 collective-permute-done.8.refs_3_
  27.0 0.1 collective-permute-start.11
  27.1 3.1 %collective-permute-start.12 = (f32[1,256]{1,0:T(1,128)S(1)}, f32[1,256]{1,0:T(1,128)S(1)}, u32[]{:S(2)}, u32[]{:S(2)}) collective-permute-start(f32[1,256]{1,0:T(1,128)S(1)} %get-tuple-element.65), channel_id=1, source_target_pairs={{0,2},{1,3},{2,0},{3,1},{4,6},{5,7},{6,4},{7,5},{8,10},{9,11},{10,... | collective-permute-start | bytes 3080 | tf_op jit(solution)/shard_map/ppermute | solution.py:389
  30.2 0.0 collective-permute-start.13
  30.3 1.1 %shard_map.117 = (f32[208,128]{1,0:T(8,128)S(1)}, f32[96,128]{1,0:T(8,128)S(1)}) custom-call(f32[104,128]{1,0:T(8,128)S(1)} %get-tuple-element.52.refs_0_, f32[96,128]{1,0:T(8,128)S(1)} %get-tuple-element.53.refs_1_, s32[1,128]{1,0:T(1,128)S(1)} %get-tuple-element.37.refs_2_.refs_5_, f32[1,128]{1,0:T(1,128)S(1)} %get-tuple-element.38.refs_3_.refs_8_, ...), custom_call_target="tpu_custom_call" | custom-call | flops 4000000 | bytes 100000 | tf_op jit(solution)/shard_map/pallas_call | solution.py:345
  31.3 0.0 collective-permute-done.7.refs_2_
  31.4 0.0 collective-permute-done.6.refs_1_
  31.4 1.5 %shard_map.118 = (f32[50,2,128]{2,1,0:T(2,128)}, f32[50,2,128]{2,1,0:T(2,128)}) custom-call(f32[208,128]{1,0:T(8,128)S(1)} %get-tuple-element.54.refs_0_, bf16[112,128]{1,0:T(8,128)(2,1)S(1)} %collective-permute-done.6.refs_1_, bf16[112,128]{1,0:T(8,128)(2,1)S(1)} %collective-permute-done.7.refs_2_, bf16[128,128]{1,0:T(8,128)(2,1)S(1)} %collective-permute-done.8.refs_3_, ...), custom_call_target="tpu_custom_call" | custom-call | flops 2000000 | bytes 100000 | tf_op jit(solution)/shard_map/pallas_call | solution.py:345
  32.8 0.0 collective-permute-done.11.refs_1_
  32.8 0.0 collective-permute-done.12.refs_2_
  32.8 0.4 %collective-permute-done.13.refs_3_ = f32[1,256]{1,0:T(1,128)S(1)} collective-permute-done((f32[1,256]{1,0:T(1,128)S(1)}, f32[1,256]{1,0:T(1,128)S(1)}, u32[]{:S(2)}, u32[]{:S(2)}) %collective-permute-start.13) | collective-permute-done | bytes 1056 | tf_op jit(solution)/shard_map/ppermute | solution.py:389
  33.2 0.6 %shard_map.120 = f32[1,192]{1,0:T(1,128)} custom-call(f32[1,256]{1,0:T(1,128)S(1)} %get-tuple-element.63.refs_0_, f32[1,256]{1,0:T(1,128)S(1)} %collective-permute-done.11.refs_1_, f32[1,256]{1,0:T(1,128)S(1)} %collective-permute-done.12.refs_2_, f32[1,256]{1,0:T(1,128)S(1)} %collective-permute-done.13.refs_3_), custom_call_target="tpu_custom_call" | custom-call | flops 1000000 | bytes 100000 | tf_op jit(solution)/shard_map/pallas_call | solution.py:345
  (1 shorter events, 0.0 us)
Async XLA Ops:
  0.6 6.9 %copy-start = (bf16[50,6,128,128]{3,2,1,0:T(8,128)(2,1)S(1)}, bf16[50,6,128,128]{3,2,1,0:T(8,128)(2,1)}, u32[]{:S(2)}) copy-start(bf16[50,6,128,128]{3,2,1,0:T(8,128)(2,1)} %refs_6_.13) | copy-start | bytes 29491204
  0.6 6.9 %copy-start.1 = (bf16[50,3,128,128]{3,2,1,0:T(8,128)(2,1)S(1)}, bf16[50,3,128,128]{3,2,1,0:T(8,128)(2,1)}, u32[]{:S(2)}) copy-start(bf16[50,3,128,128]{3,2,1,0:T(8,128)(2,1)} %refs_7_.7) | copy-start | bytes 14745604
  1.8 6.8 %collective-permute-start.2 = (bf16[112,128]{1,0:T(8,128)(2,1)S(1)}, bf16[112,128]{1,0:T(8,128)(2,1)S(1)}, u32[]{:S(2)}, u32[]{:S(2)}) collective-permute-start(bf16[112,128]{1,0:T(8,128)(2,1)S(1)} %get-tuple-element.42), channel_id=1, source_target_pairs={{0,8},{1,9},{2,10},{3,11},{4,12},{5,13},{6,14},{7,15},{8,0},{9,1},... | collective-permute-start | bytes 86024 | tf_op jit(solution)/shard_map/ppermute | solution.py:382
  5.9 6.0 %collective-permute-start.1 = (bf16[112,128]{1,0:T(8,128)(2,1)S(1)}, bf16[112,128]{1,0:T(8,128)(2,1)S(1)}, u32[]{:S(2)}, u32[]{:S(2)}) collective-permute-start(bf16[112,128]{1,0:T(8,128)(2,1)S(1)} %get-tuple-element.42), channel_id=1, source_target_pairs={{0,15},{1,2},{2,1},{3,4},{4,3},{5,6},{6,5},{7,8},{8,7},{9,10},{10,... | collective-permute-start | bytes 86024 | tf_op jit(solution)/shard_map/ppermute | solution.py:383
  7.4 4.5 %collective-permute-start = (bf16[112,128]{1,0:T(8,128)(2,1)S(1)}, bf16[112,128]{1,0:T(8,128)(2,1)S(1)}, u32[]{:S(2)}, u32[]{:S(2)}) collective-permute-start(bf16[112,128]{1,0:T(8,128)(2,1)S(1)} %get-tuple-element.42), channel_id=1, source_target_pairs={{0,1},{1,0},{2,3},{3,2},{4,5},{5,4},{6,7},{7,6},{8,9},{9,8},{10,11... | collective-permute-start | bytes 86024 | tf_op jit(solution)/shard_map/ppermute | solution.py:384
  12.6 4.9 %collective-permute-start.5 = (bf16[112,128]{1,0:T(8,128)(2,1)S(1)}, bf16[112,128]{1,0:T(8,128)(2,1)S(1)}, u32[]{:S(2)}, u32[]{:S(2)}) collective-permute-start(bf16[112,128]{1,0:T(8,128)(2,1)S(1)} %get-tuple-element.49), channel_id=1, source_target_pairs={{0,8},{1,9},{2,10},{3,11},{4,12},{5,13},{6,14},{7,15},{8,0},{9,1},... | collective-permute-start | bytes 86024 | tf_op jit(solution)/shard_map/ppermute | solution.py:382
  12.7 6.1 %collective-permute-start.4 = (bf16[112,128]{1,0:T(8,128)(2,1)S(1)}, bf16[112,128]{1,0:T(8,128)(2,1)S(1)}, u32[]{:S(2)}, u32[]{:S(2)}) collective-permute-start(bf16[112,128]{1,0:T(8,128)(2,1)S(1)} %get-tuple-element.49), channel_id=1, source_target_pairs={{0,15},{1,2},{2,1},{3,4},{4,3},{5,6},{6,5},{7,8},{8,7},{9,10},{10,... | collective-permute-start | bytes 86024 | tf_op jit(solution)/shard_map/ppermute | solution.py:383
  14.7 4.1 %collective-permute-start.3 = (bf16[112,128]{1,0:T(8,128)(2,1)S(1)}, bf16[112,128]{1,0:T(8,128)(2,1)S(1)}, u32[]{:S(2)}, u32[]{:S(2)}) collective-permute-start(bf16[112,128]{1,0:T(8,128)(2,1)S(1)} %get-tuple-element.49), channel_id=1, source_target_pairs={{0,1},{1,0},{2,3},{3,2},{4,5},{5,4},{6,7},{7,6},{8,9},{9,8},{10,11... | collective-permute-start | bytes 86024 | tf_op jit(solution)/shard_map/ppermute | solution.py:384
  19.5 7.5 %collective-permute-start.8 = (bf16[128,128]{1,0:T(8,128)(2,1)S(1)}, bf16[128,128]{1,0:T(8,128)(2,1)S(1)}, u32[]{:S(2)}, u32[]{:S(2)}) collective-permute-start(bf16[128,128]{1,0:T(8,128)(2,1)S(1)} %get-tuple-element.56), channel_id=1, source_target_pairs={{0,8},{1,9},{2,10},{3,11},{4,12},{5,13},{6,14},{7,15},{8,0},{9,1},... | collective-permute-start | bytes 98312 | tf_op jit(solution)/shard_map/ppermute | solution.py:382
  20.6 10.7 %collective-permute-start.7 = (bf16[112,128]{1,0:T(8,128)(2,1)S(1)}, bf16[112,128]{1,0:T(8,128)(2,1)S(1)}, u32[]{:S(2)}, u32[]{:S(2)}) collective-permute-start(bf16[112,128]{1,0:T(8,128)(2,1)S(1)} %get-tuple-element.55), channel_id=1, source_target_pairs={{0,15},{1,2},{2,1},{3,4},{4,3},{5,6},{6,5},{7,8},{8,7},{9,10},{10,... | collective-permute-start | bytes 86024 | tf_op jit(solution)/shard_map/ppermute | solution.py:383
  21.6 9.8 %collective-permute-start.6 = (bf16[112,128]{1,0:T(8,128)(2,1)S(1)}, bf16[112,128]{1,0:T(8,128)(2,1)S(1)}, u32[]{:S(2)}, u32[]{:S(2)}) collective-permute-start(bf16[112,128]{1,0:T(8,128)(2,1)S(1)} %get-tuple-element.55), channel_id=1, source_target_pairs={{0,1},{1,0},{2,3},{3,2},{4,5},{5,4},{6,7},{7,6},{8,9},{9,8},{10,11... | collective-permute-start | bytes 86024 | tf_op jit(solution)/shard_map/ppermute | solution.py:384
  21.6 3.6 %collective-permute-start.9 = (f32[4,256]{1,0:T(4,128)S(1)}, f32[4,256]{1,0:T(4,128)S(1)}, u32[]{:S(2)}, u32[]{:S(2)}) collective-permute-start(f32[4,256]{1,0:T(4,128)S(1)} %get-tuple-element.61), channel_id=1, source_target_pairs={{0,4},{1,5},{2,6},{3,7},{4,0},{5,1},{6,2},{7,3},{8,12},{9,13},{10,... | collective-permute-start | bytes 12296 | tf_op jit(solution)/shard_map/ppermute | solution.py:389
  21.6 5.4 %collective-permute-start.10 = (f32[4,256]{1,0:T(4,128)S(1)}, f32[4,256]{1,0:T(4,128)S(1)}, u32[]{:S(2)}, u32[]{:S(2)}) collective-permute-start(f32[4,256]{1,0:T(4,128)S(1)} %get-tuple-element.62), channel_id=1, source_target_pairs={{0,12},{1,13},{2,14},{3,15},{4,8},{5,9},{6,10},{7,11},{8,4},{9,5},... | collective-permute-start | bytes 12296 | tf_op jit(solution)/shard_map/ppermute | solution.py:389
  27.0 5.8 %collective-permute-start.11 = (f32[1,256]{1,0:T(1,128)S(1)}, f32[1,256]{1,0:T(1,128)S(1)}, u32[]{:S(2)}, u32[]{:S(2)}) collective-permute-start(f32[1,256]{1,0:T(1,128)S(1)} %get-tuple-element.64), channel_id=1, source_target_pairs={{0,1},{1,0},{2,3},{3,2},{4,5},{5,4},{6,7},{7,6},{8,9},{9,8},{10,11... | collective-permute-start | bytes 3080 | tf_op jit(solution)/shard_map/ppermute | solution.py:389
  27.1 5.8 %collective-permute-start.12 = (f32[1,256]{1,0:T(1,128)S(1)}, f32[1,256]{1,0:T(1,128)S(1)}, u32[]{:S(2)}, u32[]{:S(2)}) collective-permute-start(f32[1,256]{1,0:T(1,128)S(1)} %get-tuple-element.65), channel_id=1, source_target_pairs={{0,2},{1,3},{2,0},{3,1},{4,6},{5,7},{6,4},{7,5},{8,10},{9,11},{10,... | collective-permute-start | bytes 3080 | tf_op jit(solution)/shard_map/ppermute | solution.py:389
  30.2 3.0 %collective-permute-start.13 = (f32[1,256]{1,0:T(1,128)S(1)}, f32[1,256]{1,0:T(1,128)S(1)}, u32[]{:S(2)}, u32[]{:S(2)}) collective-permute-start(f32[1,256]{1,0:T(1,128)S(1)} %get-tuple-element.66), channel_id=1, source_target_pairs={{0,3},{1,2},{2,1},{3,0},{4,7},{5,6},{6,5},{7,4},{8,11},{9,10},{10,... | collective-permute-start | bytes 3080 | tf_op jit(solution)/shard_map/ppermute | solution.py:389

commit v6 on v5

--- a/solution.py
+++ b/solution.py
@@ -49,6 +49,14 @@
     return lax.broadcasted_iota(jnp.int32, (PAIR, columns), 0)
 
 
+def own_halves(lhs, rhs, pair, columns):
+    product = jnp.dot(lhs, rhs, preferred_element_type=F32)
+    top = PAIR * (pair % 2)
+    upper = product[top : top + PAIR, :columns]
+    lower = product[top : top + PAIR, columns:]
+    return jnp.where(sublane(columns) < CHANNELS, upper, lower)
+
+
 def tiles_of(ref, level, first, columns):
     return ref[level, first : first + 3].reshape(3 * columns, columns)
 
@@ -58,11 +66,15 @@
         [tiles_of(ref, 2 * pair, first, columns), tiles_of(ref, 2 * pair + 1, first, columns)],
         axis=1,
     )
-    product = jnp.dot(lhs, rhs, preferred_element_type=F32)
-    top = PAIR * (pair % 2)
-    upper = product[top : top + PAIR, :columns]
-    lower = product[top : top + PAIR, columns:]
-    return jnp.where(sublane(columns) < CHANNELS, upper, lower)
+    return own_halves(lhs, rhs, pair, columns)
+
+
+def chosen_product(lhs, ref, pair, tiles, columns):
+    blocks = [
+        jnp.concatenate([ref[level, tile] for tile in tiles], axis=0)
+        for level in (2 * pair, 2 * pair + 1)
+    ]
+    return own_halves(lhs, jnp.concatenate(blocks, axis=1), pair, columns)
 
 
 def window(ref, start, offsets):
@@ -260,16 +272,55 @@
         ref[...] = part
 
 
-def flux_kernel(*refs):
-    *part_refs, flux_ref = refs
+def finish_kernel(state_ref, tangent_ref, *refs):
+    *part_refs, state_hbm, tangent_hbm, flux_hbm, flux_ref, semaphore = refs
+    copies = [
+        pltpu.make_async_copy(state_ref, state_hbm, semaphore.at[0]),
+        pltpu.make_async_copy(tangent_ref, tangent_hbm, semaphore.at[1]),
+    ]
+    for copy in copies:
+        copy.start()
     flux = part_refs[0][...]
     for ref in part_refs[1:]:
         flux = flux + ref[...]
     flux_ref[...] = flux[:, : flux_ref.shape[1]]
+    copies.append(pltpu.make_async_copy(flux_ref, flux_hbm, semaphore.at[2]))
+    copies[2].start()
+    for copy in copies:
+        copy.wait()
+
+
+def ghost_level(quad, columns):
+    return lax.broadcasted_iota(jnp.int32, (QUAD, columns), 0) // CHANNELS + CHANNELS * quad
+
+
+def side_tile():
+    return 3 + (lax.axis_index("tile") + 1) % 2
+
+
+def early_kernel(size, partial_ref, pair_ref, across_ref, depth_ref, explicit_ref, out_ref):
+    columns = size.columns
+    side = side_tile()
+    side_depth, across_depth = depth_ref[pl.ds(side, 1), :], depth_ref[5:6, :]
+    for quad in range(size.ghost_quads):
+        span = slice(QUAD * quad, QUAD * quad + QUAD)
+        level = ghost_level(quad, columns)
+        own_chip = jnp.where(level < side_depth, pair_ref[span, :].astype(F32), 0.0)
+        across = jnp.where(level < across_depth, across_ref[span, :].astype(F32), 0.0)
+        lhs = jnp.concatenate([own_chip, across], axis=1).astype(BF16)
+        for pair in range(2 * quad, min(2 * quad + 2, size.ghost_pairs)):
+            top = PAIR * pair
+            value = chosen_product(lhs, explicit_ref, pair, (side, 5), columns)
+            out_ref[top : top + PAIR, :] = value + partial_ref[top : top + PAIR, :]
 
 
 def ghost_kernel(size, stage, slots, *refs):
-    partial_ref, pair_ref, other_ref, across_ref, depth_ref, wet_ref, explicit_ref, implicit_ref = refs[:8]
+    if stage == "last":
+        partial_ref, pair_ref, other_ref, across_ref = refs[:4]
+    else:
+        partial_ref, early_ref, other_ref = refs[:3]
+        refs = refs[:1] + refs
+    depth_ref, wet_ref, explicit_ref, implicit_ref = refs[4:8]
     if stage == "last":
         high_ref, state_ref, tangent_ref, middle_ref, fields_ref = refs[8:]
     elif stage == "export":
@@ -283,22 +334,31 @@
     middle_ref[:EDGE, :] = jnp.zeros((EDGE, columns), F32)
     for top in range(PAIR * size.ghost_pairs, QUAD * size.low_quads + EDGE, PAIR):
         middle_ref[EDGE + top : EDGE + top + PAIR, :] = partial_ref[top : top + PAIR, :]
+    next_tile = 7 - side_tile()
     for quad in range(size.ghost_quads):
         span = slice(QUAD * quad, QUAD * quad + QUAD)
-        own_chip = pair_ref[span, :].astype(F32)
+        level = ghost_level(quad, columns)
         next_chip = other_ref[span, :].astype(F32)
-        across = across_ref[span, :].astype(F32)
-        level = lax.broadcasted_iota(jnp.int32, (QUAD, columns), 0) // CHANNELS + CHANNELS * quad
-        before = jnp.where(even, next_chip, own_chip)
-        after = jnp.where(even, own_chip, next_chip)
-        before = jnp.where(level < depth_ref[3:4, :], before, 0.0)
-        after = jnp.where(level < depth_ref[4:5, :], after, 0.0)
-        across = jnp.where(level < depth_ref[5:6, :], across, 0.0)
-        lhs = jnp.concatenate([before, after, across], axis=1).astype(BF16)
+        if stage == "last":
+            own_chip = pair_ref[span, :].astype(F32)
+            before = jnp.where(even, next_chip, own_chip)
+            after = jnp.where(even, own_chip, next_chip)
+            before = jnp.where(level < depth_ref[3:4, :], before, 0.0)
+            after = jnp.where(level < depth_ref[4:5, :], after, 0.0)
+            across = jnp.where(level < depth_ref[5:6, :], across_ref[span, :].astype(F32), 0.0)
+            lhs = jnp.concatenate([before, after, across], axis=1).astype(BF16)
+        else:
+            next_depth = depth_ref[pl.ds(next_tile, 1), :]
+            lhs = jnp.where(level < next_depth, next_chip, 0.0).astype(BF16)
         for pair in range(2 * quad, min(2 * quad + 2, size.ghost_pairs)):
             top = PAIR * pair
-            value = pair_product(lhs, explicit_ref, pair, columns, 3)
-            middle_ref[EDGE + top : EDGE + top + PAIR, :] = value + partial_ref[top : top + PAIR, :]
+            if stage == "last":
+                value = pair_product(lhs, explicit_ref, pair, columns, 3)
+                value = value + partial_ref[top : top + PAIR, :]
+            else:
+                value = chosen_product(lhs, explicit_ref, pair, (next_tile,), columns)
+                value = value + early_ref[top : top + PAIR, :]
+            middle_ref[EDGE + top : EDGE + top + PAIR, :] = value
     values = []
     for quad in range(size.low_quads):
         lhs = window(middle_ref, EDGE + QUAD * quad, (-CHANNELS, 0, CHANNELS))
@@ -336,7 +396,7 @@
     return pltpu.with_memory_space_constraint(value, pltpu.VMEM)
 
 
-def call(body, outputs, scratch, operands, flops=1000000, in_hbm=()):
+def call(body, outputs, scratch, operands, flops=1000000, in_hbm=(), out_space=pltpu.VMEM):
     space = lambda place: pltpu.HBM if place in in_hbm else pltpu.VMEM
     operands = [
         pltpu.with_memory_space_constraint(value, pltpu.HBM) if place in in_hbm else value
@@ -346,7 +406,7 @@
         body,
         out_shape=outputs,
         in_specs=[pl.BlockSpec(memory_space=space(k)) for k in range(len(operands))],
-        out_specs=[pl.BlockSpec(memory_space=pltpu.VMEM)] * len(outputs),
+        out_specs=[pl.BlockSpec(memory_space=out_space)] * len(outputs),
         scratch_shapes=scratch,
         compiler_params=pltpu.CompilerParams(vmem_limit_bytes=8 * MIB),
         cost_estimate=pl.CostEstimate(flops=flops, bytes_accessed=100000, transcendentals=0),
@@ -449,13 +509,22 @@
                 operands + [remineral] + weights + [total],
                 4000000,
             )
-        operands = [partial, *ghosts, depth, wet] + weights
+        pair_ghost, other_ghost, across_ghost = ghosts
+        if last:
+            operands = [partial, *ghosts, depth, wet] + weights
+        else:
+            (early,) = call(
+                functools.partial(early_kernel, size),
+                [shape(PAIR * size.ghost_pairs)],
+                [],
+                [partial, pair_ghost, across_ghost, depth, explicit],
+            )
+            operands = [partial, early, other_ghost, depth, wet] + weights
         sends = [shape(size.low_rows), shape(size.send_rows, BF16)]
         if last:
-            result = jax.ShapeDtypeStruct((size.levels, CHANNELS // 2, columns), F32)
             state_out, tangent_out = call(
                 functools.partial(ghost_kernel, size, "last", slots),
-                [result, result],
+                [tall, tall],
                 [low_scratch, pltpu.VMEM((size.rows, columns), F32)],
                 operands + [high],
                 2000000,
@@ -489,8 +558,13 @@
             [kept, *arrived],
         )
         arrived = [hop(value, place * rest) for place, value in enumerate(leaving, 1)]
-    (flux,) = call(
-        flux_kernel, [jax.ShapeDtypeStruct((1, tile_count * slots), F32)], [], [kept, *arrived]
+    result = pltpu.HBM((size.levels, CHANNELS // 2, columns), F32)
+    state_out, tangent_out, flux = call(
+        finish_kernel,
+        [result, result, pltpu.HBM((1, tile_count * slots), F32)],
+        [pltpu.VMEM((1, tile_count * slots), F32), pltpu.SemaphoreType.DMA((3,))],
+        [state_out, tangent_out, kept, *arrived],
+        out_space=pltpu.HBM,
     )
     return state_out.transpose(1, 0, 2), tangent_out.transpose(1, 0, 2), flux.reshape(-1)
 

time: 33.9 us -> 33.8 us (level)
  waiting for transfers between devices: 8.99 us -> 7.24 us
  starting transfers between devices: 16.3 us -> 18 us
    ppermute x3, starting transfers between devices: 4.38 us -> 7.01 us  [exchange(): other = lax.ppermute(value, 'tile', next_chip)]
    ppermute x3, waiting for transfers between devices: 4.56 us -> 3.07 us  [exchange(): other = lax.ppermute(value, 'tile', next_chip)]
    ppermute x3, waiting for transfers between devices: 1.74 us -> 0.86 us  [exchange(): across = lax.ppermute(across_value, 'tile', opposite)]
    ppermute x5, starting transfers between devices: 6.39 us -> 5.51 us  [hop(): return lax.ppermute(value, 'tile', partners)]
    ppermute x5, waiting for transfers between devices: 2.67 us -> 3.29 us  [hop(): return lax.ppermute(value, 'tile', partners)]
    pallas_call x9 -> x11, Pallas kernels: 7.77 us -> 7.64 us  [call(): pl.pallas_call(body, out_shape=outputs, in_specs=[pl.BlockSpec(memory_spa...]
where the time goes in v6:
time: 33.8 us; the launch traced here: 33.6 us
  starting transfers between devices  18 us (53%)
  Pallas kernels  7.64 us (23%)
  waiting for transfers between devices  7.24 us (21%)
  between operations  0.78 us (2%)
    pallas_call x11, Pallas kernels, call(): pl.pallas_call(body, out_shape=outputs, in_specs=[pl.BlockSpec(memory_spa...  7.64 us
    ppermute x3, starting transfers between devices, exchange(): other = lax.ppermute(value, 'tile', next_chip)  7.01 us
    ppermute x5, starting transfers between devices, hop(): return lax.ppermute(value, 'tile', partners)  5.51 us
    ppermute x3, starting transfers between devices, exchange(): across = lax.ppermute(across_value, 'tile', opposite)  5.43 us
    ppermute x5, waiting for transfers between devices, hop(): return lax.ppermute(value, 'tile', partners)  3.29 us
    ppermute x3, waiting for transfers between devices, exchange(): other = lax.ppermute(value, 'tile', next_chip)  3.07 us
    ppermute x3, waiting for transfers between devices, exchange(): across = lax.ppermute(across_value, 'tile', opposite)  0.86 us
  transfers between devices with their start and end apart: 14, of which 6 were waited for; matrix products, arithmetic and copies ran while one was open for 0% of the time, Pallas kernels for 14%

profile of v6, /device:TPU:0, one launch (start us, length us, event | category | flops | bytes accessed | tf_op | source)
XLA Modules:
  0.0 33.6 jit_solution(16309324152488254545)
XLA Ops:
  0.6 0.0 copy-start
  0.6 0.0 copy-start.1
  0.7 1.1 %shard_map.112 = (f32[104,128]{1,0:T(8,128)S(1)}, f32[96,128]{1,0:T(8,128)S(1)}, bf16[112,128]{1,0:T(8,128)(2,1)S(1)}, s32[1,128]{1,0:T(1,128)S(1)}, f32[1,128]{...) custom-call(f32[50,2,128]{2,1,0:T(2,128)} %bitcast.9, f32[50,2,128]{2,1,0:T(2,128)} %bitcast.10, ...), custom_call_target="tpu_custom_call" | custom-call | flops 10000000000 | bytes 100000 | tf_op jit(solution)/shard_map/pallas_call | solution.py:405
  1.8 4.1 %collective-permute-start.1 = (bf16[112,128]{1,0:T(8,128)(2,1)S(1)}, bf16[112,128]{1,0:T(8,128)(2,1)S(1)}, u32[]{:S(2)}, u32[]{:S(2)}) collective-permute-start(bf16[112,128]{1,0:T(8,128)(2,1)S(1)} %get-tuple-element.45), channel_id=1, source_target_pairs={{0,8},{1,9},{2,10},{3,11},{4,12},{5,13},{6,14},{7,15},{8,0},{9,1},... | collective-permute-start | bytes 86024 | tf_op jit(solution)/shard_map/ppermute | solution.py:442
  5.9 0.0 collective-permute-start
  5.9 2.4 %collective-permute-start.2 = (bf16[112,128]{1,0:T(8,128)(2,1)S(1)}, bf16[112,128]{1,0:T(8,128)(2,1)S(1)}, u32[]{:S(2)}, u32[]{:S(2)}) collective-permute-start(bf16[112,128]{1,0:T(8,128)(2,1)S(1)} %get-tuple-element.45), channel_id=1, source_target_pairs={{0,15},{1,2},{2,1},{3,4},{4,3},{5,6},{6,5},{7,8},{8,7},{9,10},{10,... | collective-permute-start | bytes 86024 | tf_op jit(solution)/shard_map/ppermute | solution.py:443
  8.3 0.0 copy-done
  8.3 0.0 copy-done.1
  8.3 1.1 %shard_map.113 = (f32[208,128]{1,0:T(8,128)S(1)}, f32[96,128]{1,0:T(8,128)S(1)}, f32[1,128]{1,0:T(1,128)S(1)}, f32[208,128]{1,0:T(8,128)S(1)}, s32[6,128]{1,0:T(8,128)S(1)}) custom-call(f32[104,128]{1,0:T(8,128)S(1)} %get-tuple-element.38.refs_0_, f32[96,128]{1,0:T(8,128)S(1)} %get-tuple-element.39.refs_1_, ...), custom_call_target="tpu_custom_call" | custom-call | flops 4000000 | bytes 100000 | tf_op jit(solution)/shard_map/pallas_call | solution.py:405
  9.4 0.0 collective-permute-done.1.across_ref
  9.4 0.0 collective-permute-done.pair_ref
  9.5 0.4 %shard_map.114.refs_1_ = f32[104,128]{1,0:T(8,128)S(1)} custom-call(f32[208,128]{1,0:T(8,128)S(1)} %get-tuple-element.44.partial_ref.refs_0_, bf16[112,128]{1,0:T(8,128)(2,1)S(1)} %collective-permute-done.pair_ref, bf16[112,128]{1,0:T(8,128)(2,1)S(1)} %collective-permute-done.1.across_ref, s32[6,128]{1,0:T(8,128)S(1)} %get-tuple-element.46.depth_ref.refs_3_.refs_4_, ...), custom_call_target="tpu_custom_call" | custom-call | flops 1000000 | bytes 100000 | tf_op jit(solution)/shard_map/pallas_call | solution.py:405
  9.8 2.1 %collective-permute-done.2.refs_2_ = bf16[112,128]{1,0:T(8,128)(2,1)S(1)} collective-permute-done((bf16[112,128]{1,0:T(8,128)(2,1)S(1)}, bf16[112,128]{1,0:T(8,128)(2,1)S(1)}, u32[]{:S(2)}, u32[]{:S(2)}) %collective-permute-start.2) | collective-permute-done | bytes 28704 | tf_op jit(solution)/shard_map/ppermute | solution.py:443
  11.9 0.6 %shard_map.115 = (f32[104,128]{1,0:T(8,128)S(1)}, bf16[112,128]{1,0:T(8,128)(2,1)S(1)}) custom-call(f32[208,128]{1,0:T(8,128)S(1)} %get-tuple-element.44.partial_ref.refs_0_, f32[104,128]{1,0:T(8,128)S(1)} %shard_map.114.refs_1_, bf16[112,128]{1,0:T(8,128)(2,1)S(1)} %collective-permute-done.2.refs_2_, ...), custom_call_target="tpu_custom_call" | custom-call | flops 1000000 | bytes 100000 | tf_op jit(solution)/shard_map/pallas_call | solution.py:405
  12.5 0.2 collective-permute-start.4
  12.7 0.0 collective-permute-start.3
  12.7 2.8 %collective-permute-start.5 = (bf16[112,128]{1,0:T(8,128)(2,1)S(1)}, bf16[112,128]{1,0:T(8,128)(2,1)S(1)}, u32[]{:S(2)}, u32[]{:S(2)}) collective-permute-start(bf16[112,128]{1,0:T(8,128)(2,1)S(1)} %get-tuple-element.52), channel_id=1, source_target_pairs={{0,15},{1,2},{2,1},{3,4},{4,3},{5,6},{6,5},{7,8},{8,7},{9,10},{10,... | collective-permute-start | bytes 86024 | tf_op jit(solution)/shard_map/ppermute | solution.py:443
  15.5 1.0 %shard_map.116 = (f32[208,128]{1,0:T(8,128)S(1)}, f32[96,128]{1,0:T(8,128)S(1)}, f32[1,128]{1,0:T(1,128)S(1)}) custom-call(f32[104,128]{1,0:T(8,128)S(1)} %get-tuple-element.47.refs_0_, f32[96,128]{1,0:T(8,128)S(1)} %get-tuple-element.48.refs_1_, s32[1,128]{1,0:T(1,128)S(1)} %get-tuple-element.40.refs_2_.refs_4_.refs_5_, ...), custom_call_target="tpu_custom_call" | custom-call | flops 4000000 | bytes 100000 | tf_op jit(solution)/shard_map/pallas_call | solution.py:405
  16.5 0.9 %collective-permute-done.4.across_ref = bf16[112,128]{1,0:T(8,128)(2,1)S(1)} collective-permute-done((bf16[112,128]{1,0:T(8,128)(2,1)S(1)}, bf16[112,128]{1,0:T(8,128)(2,1)S(1)}, u32[]{:S(2)}, u32[]{:S(2)}) %collective-permute-start.4) | collective-permute-done | bytes 28704 | tf_op jit(solution)/shard_map/ppermute | solution.py:442
  17.4 0.0 collective-permute-done.3.pair_ref
  17.4 0.3 %shard_map.117.refs_1_ = f32[104,128]{1,0:T(8,128)S(1)} custom-call(f32[208,128]{1,0:T(8,128)S(1)} %get-tuple-element.51.partial_ref.refs_0_, bf16[112,128]{1,0:T(8,128)(2,1)S(1)} %collective-permute-done.3.pair_ref, bf16[112,128]{1,0:T(8,128)(2,1)S(1)} %collective-permute-done.4.across_ref, s32[6,128]{1,0:T(8,128)S(1)} %get-tuple-element.46.depth_ref.refs_3_.refs_4_, ...), custom_call_target="tpu_custom_call" | custom-call | flops 1000000 | bytes 100000 | tf_op jit(solution)/shard_map/pallas_call | solution.py:405
  17.7 1.0 %collective-permute-done.5.refs_2_ = bf16[112,128]{1,0:T(8,128)(2,1)S(1)} collective-permute-done((bf16[112,128]{1,0:T(8,128)(2,1)S(1)}, bf16[112,128]{1,0:T(8,128)(2,1)S(1)}, u32[]{:S(2)}, u32[]{:S(2)}) %collective-permute-start.5) | collective-permute-done | bytes 28704 | tf_op jit(solution)/shard_map/ppermute | solution.py:443
  18.7 0.6 %shard_map.118 = (f32[104,128]{1,0:T(8,128)S(1)}, bf16[112,128]{1,0:T(8,128)(2,1)S(1)}, bf16[128,128]{1,0:T(8,128)(2,1)S(1)}, f32[4,256]{1,0:T(4,128)S(1)}, f32[4,256]{1,0:T(4,128)S(1)}, /*index=5*/f32[4,256]{1,0:T(4,128)S(1)}) custom-call(f32[208,128]{1,0:T(8,128)S(1)} %get-tuple-element.51.partial_ref.refs_0_, f32[104,128]{1,0:T(8,128)S(1)} %shard_map.117.refs_1_, ...), custom_call_target="tpu_custom_call" | custom-call | flops 1000000 | bytes 100000 | tf_op jit(solution)/shard_map/pallas_call | solution.py:405
  19.3 1.1 %collective-permute-start.8 = (bf16[128,128]{1,0:T(8,128)(2,1)S(1)}, bf16[128,128]{1,0:T(8,128)(2,1)S(1)}, u32[]{:S(2)}, u32[]{:S(2)}) collective-permute-start(bf16[128,128]{1,0:T(8,128)(2,1)S(1)} %get-tuple-element.59), channel_id=1, source_target_pairs={{0,8},{1,9},{2,10},{3,11},{4,12},{5,13},{6,14},{7,15},{8,0},{9,1},... | collective-permute-start | bytes 98312 | tf_op jit(solution)/shard_map/ppermute | solution.py:442
  20.4 1.8 %collective-permute-start.7 = (bf16[112,128]{1,0:T(8,128)(2,1)S(1)}, bf16[112,128]{1,0:T(8,128)(2,1)S(1)}, u32[]{:S(2)}, u32[]{:S(2)}) collective-permute-start(bf16[112,128]{1,0:T(8,128)(2,1)S(1)} %get-tuple-element.58), channel_id=1, source_target_pairs={{0,15},{1,2},{2,1},{3,4},{4,3},{5,6},{6,5},{7,8},{8,7},{9,10},{10,... | collective-permute-start | bytes 86024 | tf_op jit(solution)/shard_map/ppermute | solution.py:443
  22.2 0.0 collective-permute-start.6
  22.2 0.0 collective-permute-start.9
  22.2 3.1 %collective-permute-start.10 = (f32[4,256]{1,0:T(4,128)S(1)}, f32[4,256]{1,0:T(4,128)S(1)}, u32[]{:S(2)}, u32[]{:S(2)}) collective-permute-start(f32[4,256]{1,0:T(4,128)S(1)} %get-tuple-element.65), channel_id=1, source_target_pairs={{0,12},{1,13},{2,14},{3,15},{4,8},{5,9},{6,10},{7,11},{8,4},{9,5},... | collective-permute-start | bytes 12296 | tf_op jit(solution)/shard_map/ppermute | solution.py:449
  25.3 0.5 %collective-permute-done.9.refs_1_ = f32[4,256]{1,0:T(4,128)S(1)} collective-permute-done((f32[4,256]{1,0:T(4,128)S(1)}, f32[4,256]{1,0:T(4,128)S(1)}, u32[]{:S(2)}, u32[]{:S(2)}) %collective-permute-start.9) | collective-permute-done | bytes 4128 | tf_op jit(solution)/shard_map/ppermute | solution.py:449
  25.8 1.8 %collective-permute-done.10.refs_2_ = f32[4,256]{1,0:T(4,128)S(1)} collective-permute-done((f32[4,256]{1,0:T(4,128)S(1)}, f32[4,256]{1,0:T(4,128)S(1)}, u32[]{:S(2)}, u32[]{:S(2)}) %collective-permute-start.10) | collective-permute-done | bytes 4128 | tf_op jit(solution)/shard_map/ppermute | solution.py:449
  27.6 0.0 collective-permute-done.8.refs_3_
  27.6 0.1 collective-permute-start.11
  27.7 2.3 %collective-permute-start.12 = (f32[1,256]{1,0:T(1,128)S(1)}, f32[1,256]{1,0:T(1,128)S(1)}, u32[]{:S(2)}, u32[]{:S(2)}) collective-permute-start(f32[1,256]{1,0:T(1,128)S(1)} %get-tuple-element.68), channel_id=1, source_target_pairs={{0,2},{1,3},{2,0},{3,1},{4,6},{5,7},{6,4},{7,5},{8,10},{9,11},{10,... | collective-permute-start | bytes 3080 | tf_op jit(solution)/shard_map/ppermute | solution.py:449
  30.0 0.0 collective-permute-start.13
  30.0 1.1 %shard_map.119 = (f32[208,128]{1,0:T(8,128)S(1)}, f32[96,128]{1,0:T(8,128)S(1)}) custom-call(f32[104,128]{1,0:T(8,128)S(1)} %get-tuple-element.55.refs_0_, f32[96,128]{1,0:T(8,128)S(1)} %get-tuple-element.56.refs_1_, s32[1,128]{1,0:T(1,128)S(1)} %get-tuple-element.40.refs_2_.refs_4_.refs_5_, f32[1,128]{1,0:T(1,128)S(1)} %get-tuple-element.41.refs_3_.refs_7_, ...), custom_call_target="tpu_custom_call" | custom-call | flops 4000000 | bytes 100000 | tf_op jit(solution)/shard_map/pallas_call | solution.py:405
  31.1 0.0 collective-permute-done.7.refs_2_
  31.1 0.0 collective-permute-done.6.refs_1_
  31.1 0.8 %shard_map.120 = (f32[50,2,128]{2,1,0:T(2,128)S(1)}, f32[50,2,128]{2,1,0:T(2,128)S(1)}) custom-call(f32[208,128]{1,0:T(8,128)S(1)} %get-tuple-element.57.refs_0_, bf16[112,128]{1,0:T(8,128)(2,1)S(1)} %collective-permute-done.6.refs_1_, bf16[112,128]{1,0:T(8,128)(2,1)S(1)} %collective-permute-done.7.refs_2_, ...), custom_call_target="tpu_custom_call" | custom-call | flops 2000000 | bytes 100000 | tf_op jit(solution)/shard_map/pallas_call | solution.py:405
  32.0 0.0 collective-permute-done.11.refs_1_
  32.0 0.0 collective-permute-done.12.refs_2_
  32.0 1.0 %collective-permute-done.13.refs_3_ = f32[1,256]{1,0:T(1,128)S(1)} collective-permute-done((f32[1,256]{1,0:T(1,128)S(1)}, f32[1,256]{1,0:T(1,128)S(1)}, u32[]{:S(2)}, u32[]{:S(2)}) %collective-permute-start.13) | collective-permute-done | bytes 1056 | tf_op jit(solution)/shard_map/ppermute | solution.py:449
  33.0 0.7 %shard_map.122 = (f32[50,2,128]{2,1,0:T(2,128)}, f32[50,2,128]{2,1,0:T(2,128)}, f32[1,192]{1,0:T(1,128)}) custom-call(f32[50,2,128]{2,1,0:T(2,128)S(1)} %get-tuple-element.61.state_ref, f32[50,2,128]{2,1,0:T(2,128)S(1)} %get-tuple-element.62.tangent_ref, f32[1,256]{1,0:T(1,128)S(1)} %get-tuple-element.66.refs_0_, ...), custom_call_target="tpu_custom_call" | custom-call | flops 1000000 | bytes 100000 | tf_op jit(solution)/shard_map/pallas_call | solution.py:405
  (1 shorter events, 0.0 us)
Async XLA Ops:
  0.6 7.7 %copy-start = (bf16[50,6,128,128]{3,2,1,0:T(8,128)(2,1)S(1)}, bf16[50,6,128,128]{3,2,1,0:T(8,128)(2,1)}, u32[]{:S(2)}) copy-start(bf16[50,6,128,128]{3,2,1,0:T(8,128)(2,1)} %refs_6_.13) | copy-start | bytes 29491204
  0.6 7.7 %copy-start.1 = (bf16[50,3,128,128]{3,2,1,0:T(8,128)(2,1)S(1)}, bf16[50,3,128,128]{3,2,1,0:T(8,128)(2,1)}, u32[]{:S(2)}) copy-start(bf16[50,3,128,128]{3,2,1,0:T(8,128)(2,1)} %refs_7_.3) | copy-start | bytes 14745604
  1.8 7.6 %collective-permute-start.1 = (bf16[112,128]{1,0:T(8,128)(2,1)S(1)}, bf16[112,128]{1,0:T(8,128)(2,1)S(1)}, u32[]{:S(2)}, u32[]{:S(2)}) collective-permute-start(bf16[112,128]{1,0:T(8,128)(2,1)S(1)} %get-tuple-element.45), channel_id=1, source_target_pairs={{0,8},{1,9},{2,10},{3,11},{4,12},{5,13},{6,14},{7,15},{8,0},{9,1},... | collective-permute-start | bytes 86024 | tf_op jit(solution)/shard_map/ppermute | solution.py:442
  5.9 3.5 %collective-permute-start = (bf16[112,128]{1,0:T(8,128)(2,1)S(1)}, bf16[112,128]{1,0:T(8,128)(2,1)S(1)}, u32[]{:S(2)}, u32[]{:S(2)}) collective-permute-start(bf16[112,128]{1,0:T(8,128)(2,1)S(1)} %get-tuple-element.45), channel_id=1, source_target_pairs={{0,1},{1,0},{2,3},{3,2},{4,5},{5,4},{6,7},{7,6},{8,9},{9,8},{10,11... | collective-permute-start | bytes 86024 | tf_op jit(solution)/shard_map/ppermute | solution.py:444
  5.9 6.0 %collective-permute-start.2 = (bf16[112,128]{1,0:T(8,128)(2,1)S(1)}, bf16[112,128]{1,0:T(8,128)(2,1)S(1)}, u32[]{:S(2)}, u32[]{:S(2)}) collective-permute-start(bf16[112,128]{1,0:T(8,128)(2,1)S(1)} %get-tuple-element.45), channel_id=1, source_target_pairs={{0,15},{1,2},{2,1},{3,4},{4,3},{5,6},{6,5},{7,8},{8,7},{9,10},{10,... | collective-permute-start | bytes 86024 | tf_op jit(solution)/shard_map/ppermute | solution.py:443
  12.5 4.9 %collective-permute-start.4 = (bf16[112,128]{1,0:T(8,128)(2,1)S(1)}, bf16[112,128]{1,0:T(8,128)(2,1)S(1)}, u32[]{:S(2)}, u32[]{:S(2)}) collective-permute-start(bf16[112,128]{1,0:T(8,128)(2,1)S(1)} %get-tuple-element.52), channel_id=1, source_target_pairs={{0,8},{1,9},{2,10},{3,11},{4,12},{5,13},{6,14},{7,15},{8,0},{9,1},... | collective-permute-start | bytes 86024 | tf_op jit(solution)/shard_map/ppermute | solution.py:442
  12.7 4.7 %collective-permute-start.3 = (bf16[112,128]{1,0:T(8,128)(2,1)S(1)}, bf16[112,128]{1,0:T(8,128)(2,1)S(1)}, u32[]{:S(2)}, u32[]{:S(2)}) collective-permute-start(bf16[112,128]{1,0:T(8,128)(2,1)S(1)} %get-tuple-element.52), channel_id=1, source_target_pairs={{0,1},{1,0},{2,3},{3,2},{4,5},{5,4},{6,7},{7,6},{8,9},{9,8},{10,11... | collective-permute-start | bytes 86024 | tf_op jit(solution)/shard_map/ppermute | solution.py:444
  12.7 6.0 %collective-permute-start.5 = (bf16[112,128]{1,0:T(8,128)(2,1)S(1)}, bf16[112,128]{1,0:T(8,128)(2,1)S(1)}, u32[]{:S(2)}, u32[]{:S(2)}) collective-permute-start(bf16[112,128]{1,0:T(8,128)(2,1)S(1)} %get-tuple-element.52), channel_id=1, source_target_pairs={{0,15},{1,2},{2,1},{3,4},{4,3},{5,6},{6,5},{7,8},{8,7},{9,10},{10,... | collective-permute-start | bytes 86024 | tf_op jit(solution)/shard_map/ppermute | solution.py:443
  19.3 8.3 %collective-permute-start.8 = (bf16[128,128]{1,0:T(8,128)(2,1)S(1)}, bf16[128,128]{1,0:T(8,128)(2,1)S(1)}, u32[]{:S(2)}, u32[]{:S(2)}) collective-permute-start(bf16[128,128]{1,0:T(8,128)(2,1)S(1)} %get-tuple-element.59), channel_id=1, source_target_pairs={{0,8},{1,9},{2,10},{3,11},{4,12},{5,13},{6,14},{7,15},{8,0},{9,1},... | collective-permute-start | bytes 98312 | tf_op jit(solution)/shard_map/ppermute | solution.py:442
  20.4 10.7 %collective-permute-start.7 = (bf16[112,128]{1,0:T(8,128)(2,1)S(1)}, bf16[112,128]{1,0:T(8,128)(2,1)S(1)}, u32[]{:S(2)}, u32[]{:S(2)}) collective-permute-start(bf16[112,128]{1,0:T(8,128)(2,1)S(1)} %get-tuple-element.58), channel_id=1, source_target_pairs={{0,15},{1,2},{2,1},{3,4},{4,3},{5,6},{6,5},{7,8},{8,7},{9,10},{10,... | collective-permute-start | bytes 86024 | tf_op jit(solution)/shard_map/ppermute | solution.py:443
  22.2 8.9 %collective-permute-start.6 = (bf16[112,128]{1,0:T(8,128)(2,1)S(1)}, bf16[112,128]{1,0:T(8,128)(2,1)S(1)}, u32[]{:S(2)}, u32[]{:S(2)}) collective-permute-start(bf16[112,128]{1,0:T(8,128)(2,1)S(1)} %get-tuple-element.58), channel_id=1, source_target_pairs={{0,1},{1,0},{2,3},{3,2},{4,5},{5,4},{6,7},{7,6},{8,9},{9,8},{10,11... | collective-permute-start | bytes 86024 | tf_op jit(solution)/shard_map/ppermute | solution.py:444
  22.2 3.6 %collective-permute-start.9 = (f32[4,256]{1,0:T(4,128)S(1)}, f32[4,256]{1,0:T(4,128)S(1)}, u32[]{:S(2)}, u32[]{:S(2)}) collective-permute-start(f32[4,256]{1,0:T(4,128)S(1)} %get-tuple-element.64), channel_id=1, source_target_pairs={{0,4},{1,5},{2,6},{3,7},{4,0},{5,1},{6,2},{7,3},{8,12},{9,13},{10,... | collective-permute-start | bytes 12296 | tf_op jit(solution)/shard_map/ppermute | solution.py:449
  22.2 5.4 %collective-permute-start.10 = (f32[4,256]{1,0:T(4,128)S(1)}, f32[4,256]{1,0:T(4,128)S(1)}, u32[]{:S(2)}, u32[]{:S(2)}) collective-permute-start(f32[4,256]{1,0:T(4,128)S(1)} %get-tuple-element.65), channel_id=1, source_target_pairs={{0,12},{1,13},{2,14},{3,15},{4,8},{5,9},{6,10},{7,11},{8,4},{9,5},... | collective-permute-start | bytes 12296 | tf_op jit(solution)/shard_map/ppermute | solution.py:449
  27.6 4.3 %collective-permute-start.11 = (f32[1,256]{1,0:T(1,128)S(1)}, f32[1,256]{1,0:T(1,128)S(1)}, u32[]{:S(2)}, u32[]{:S(2)}) collective-permute-start(f32[1,256]{1,0:T(1,128)S(1)} %get-tuple-element.67), channel_id=1, source_target_pairs={{0,1},{1,0},{2,3},{3,2},{4,5},{5,4},{6,7},{7,6},{8,9},{9,8},{10,11... | collective-permute-start | bytes 3080 | tf_op jit(solution)/shard_map/ppermute | solution.py:449
  27.7 4.3 %collective-permute-start.12 = (f32[1,256]{1,0:T(1,128)S(1)}, f32[1,256]{1,0:T(1,128)S(1)}, u32[]{:S(2)}, u32[]{:S(2)}) collective-permute-start(f32[1,256]{1,0:T(1,128)S(1)} %get-tuple-element.68), channel_id=1, source_target_pairs={{0,2},{1,3},{2,0},{3,1},{4,6},{5,7},{6,4},{7,5},{8,10},{9,11},{10,... | collective-permute-start | bytes 3080 | tf_op jit(solution)/shard_map/ppermute | solution.py:449
  30.0 3.0 %collective-permute-start.13 = (f32[1,256]{1,0:T(1,128)S(1)}, f32[1,256]{1,0:T(1,128)S(1)}, u32[]{:S(2)}, u32[]{:S(2)}) collective-permute-start(f32[1,256]{1,0:T(1,128)S(1)} %get-tuple-element.69), channel_id=1, source_target_pairs={{0,3},{1,2},{2,1},{3,0},{4,7},{5,6},{6,5},{7,4},{8,11},{9,10},{10,... | collective-permute-start | bytes 3080 | tf_op jit(solution)/shard_map/ppermute | solution.py:449
